TPU v7x, 32 devices: a whole 2x2x4 slice. The times are simulated.
32 devices in a mesh: dp: 4 (over y, x), seq: 8 (over z, core).
Axes of the slice: x: 2, y: 2, z: 4, core: 2. Of those that a mesh axis runs over, the one named last changes fastest.
Arguments:
- queries: bfloat16 [4, 1024, 2048], P('dp', 'seq'), may hold values from -6 to 6
- key_vectors: bfloat16 [4, 1024, 2048], P('dp', 'seq'), may hold values from -6 to 6
- values: bfloat16 [4, 1024, 2048], P('dp', 'seq'), may hold values from -6 to 6
- out_grad: bfloat16 [4, 1024, 2048], P('dp', 'seq'), may hold values from -6 to 6
- inputs: bfloat16 [4, 1024, 2048], P('dp', 'seq'), may hold values from -6 to 6
Outputs:
- query_grad: bfloat16 [4, 1024, 2048], P('dp', 'seq')
- key_grad: bfloat16 [4, 1024, 2048], P('dp', 'seq')
- value_grad: bfloat16 [4, 1024, 2048], P('dp', 'seq')
- weight_grad: float32 [2048, 2048], P('dp', 'seq')
All inputs are finite; a program needn't handle non-finite values.
Results may differ from a plain program's by a relative error of at most 0.025.
Values may be sent and summed in bfloat16 or wider, within the bound.
No kernel may reach another device: no remote copies, remote signals or barrier semaphores. Data moves between devices by JAX's collectives and lax.ppermute only.
A program may use at most 128 MiB of HBM per device.

v0:
```python
import jax
import jax.numpy as jnp
from jax import lax
from jax.sharding import PartitionSpec as P

HD = 128


def partner(value, axis, apart):
    return lax.ppermute(value, axis, [(i, i ^ 1 << apart) for i in range(lax.axis_size(axis))])


def body(queries, key_vectors, values, out_grad, inputs):
    seq_count = lax.axis_size("seq")
    groups = seq_count // 2
    parity = lax.axis_index("seq") % 2
    is_even = parity == 0
    tok_rows = queries.shape[1]
    half_rows = tok_rows // 2
    width = queries.shape[2]
    group_width = 2 * width // seq_count
    heads_here = group_width // HD
    model_width = inputs.shape[2]
    own_rows = seq_count * half_rows
    length = 2 * own_rows
    doc_rows = own_rows // 4
    block_rows = min(doc_rows, max(256, length // 16))
    block_count = own_rows // block_rows
    scale = HD ** (-0.5)

    def to_heads(array):
        return (
            array[0]
            .reshape(half_rows, 2, groups, group_width)
            .transpose(0, 2, 1, 3)
            .reshape(half_rows, seq_count, group_width)
        )

    moved = (
        lax.all_to_all(to_heads(queries), "seq", split_axis=1, concat_axis=0, tiled=True),
        lax.all_to_all(to_heads(key_vectors), "seq", split_axis=1, concat_axis=0, tiled=True),
        lax.all_to_all(to_heads(values), "seq", split_axis=1, concat_axis=0, tiled=True),
        lax.all_to_all(to_heads(out_grad), "seq", split_axis=1, concat_axis=0, tiled=True),
    )
    q_rows = moved[0].reshape(own_rows, group_width)
    k_rows = moved[1].reshape(own_rows, group_width)
    v_rows = moved[2].reshape(own_rows, group_width)
    g_rows = moved[3].reshape(own_rows, group_width)
    k_other, v_other = partner((k_rows, v_rows), "seq", 0)

    def in_order(mine, theirs):
        even_rows = jnp.where(is_even, mine, theirs)
        odd_rows = jnp.where(is_even, theirs, mine)
        return jnp.stack([even_rows, odd_rows], axis=1).reshape(2 * mine.shape[0], mine.shape[1])

    key_all = in_order(k_rows, k_other).reshape(length, heads_here, HD)
    value_all = in_order(v_rows, v_other).reshape(length, heads_here, HD)
    query_heads = q_rows.reshape(own_rows, heads_here, HD)
    grad_heads = g_rows.reshape(own_rows, heads_here, HD)
    key_total = jnp.zeros((length, heads_here, HD), jnp.float32)
    value_total = jnp.zeros((length, heads_here, HD), jnp.float32)
    query_parts = []
    for block in range(block_count):
        start = block * block_rows
        stop = start + block_rows
        low = 2 * (start // doc_rows * doc_rows)
        high = 2 * stop
        query_block = query_heads[start:stop]
        grad_block = grad_heads[start:stop]
        key_block = key_all[low:high]
        value_block = value_all[low:high]
        scores = (
            jnp.einsum("qhd,khd->hqk", query_block, key_block, preferred_element_type=jnp.float32)
            * scale
        )
        query_pos = 2 * (start + jnp.arange(block_rows, dtype=jnp.int32)) + parity
        key_pos = low + jnp.arange(high - low, dtype=jnp.int32)
        visible = key_pos[None, :] <= query_pos[:, None]
        scores = jnp.where(visible[None], scores, -jnp.inf)
        top = jnp.max(scores, axis=2, keepdims=True)
        weights = jnp.exp(scores - top)
        probs = weights / jnp.sum(weights, axis=2, keepdims=True)
        probs_low = probs.astype(jnp.bfloat16)
        dprob = jnp.einsum(
            "qhd,khd->hqk", grad_block, value_block, preferred_element_type=jnp.float32
        )
        delta = jnp.sum(probs * dprob, axis=2, keepdims=True)
        dscore = (probs * (dprob - delta) * scale).astype(jnp.bfloat16)
        query_parts.append(
            jnp.einsum(
                "hqk,khd->qhd", dscore, key_block, preferred_element_type=jnp.float32
            ).astype(jnp.bfloat16)
        )
        key_total = key_total.at[low:high].add(
            jnp.einsum("hqk,qhd->khd", dscore, query_block, preferred_element_type=jnp.float32)
        )
        value_total = value_total.at[low:high].add(
            jnp.einsum("hqk,qhd->khd", probs_low, grad_block, preferred_element_type=jnp.float32)
        )
    query_grad = jnp.concatenate(query_parts, axis=0).reshape(own_rows, group_width)

    def by_parity(total):
        paired = total.reshape(own_rows, 2, group_width)
        mine = jnp.where(is_even, paired[:, 0], paired[:, 1])
        theirs = jnp.where(is_even, paired[:, 1], paired[:, 0])
        return (mine.astype(jnp.bfloat16), theirs.astype(jnp.bfloat16))

    key_mine, key_theirs = by_parity(key_total)
    value_mine, value_theirs = by_parity(value_total)
    key_back, value_back = partner((key_theirs, value_theirs), "seq", 0)
    key_grad = (key_mine.astype(jnp.float32) + key_back.astype(jnp.float32)).astype(jnp.bfloat16)
    value_grad = (value_mine.astype(jnp.float32) + value_back.astype(jnp.float32)).astype(
        jnp.bfloat16
    )
    spread = jnp.broadcast_to(
        inputs[0].reshape(half_rows, 1, 2, model_width), (half_rows, groups, 2, model_width)
    ).reshape(half_rows, seq_count, model_width)
    input_rows = lax.all_to_all(spread, "seq", split_axis=1, concat_axis=0, tiled=True).reshape(
        own_rows, model_width
    )
    term = jnp.einsum("td,tc->dc", input_rows, value_grad, preferred_element_type=jnp.float32)
    halves = term.reshape(term.shape[0], 2, term.shape[1] // 2)
    mine = jnp.where(is_even, halves[:, 0], halves[:, 1])
    theirs = jnp.where(is_even, halves[:, 1], halves[:, 0])
    mine, theirs = (mine, theirs)
    received = partner(theirs.astype(jnp.bfloat16), "seq", 0).astype(theirs.dtype)
    weight_grad = lax.psum_scatter(
        (mine + received).astype(jnp.bfloat16), "dp", scatter_dimension=0, tiled=True
    ).astype(jnp.float32)

    def to_tokens(array):
        return array.reshape(seq_count, half_rows, 1, group_width)

    def from_heads(array):
        return (
            array.reshape(half_rows, groups, 2, group_width)
            .transpose(0, 2, 1, 3)
            .reshape(1, tok_rows, width)
        )

    returned = (
        lax.all_to_all(to_tokens(query_grad), "seq", split_axis=0, concat_axis=2, tiled=True),
        lax.all_to_all(to_tokens(key_grad), "seq", split_axis=0, concat_axis=2, tiled=True),
        lax.all_to_all(to_tokens(value_grad), "seq", split_axis=0, concat_axis=2, tiled=True),
    )
    return (from_heads(returned[0]), from_heads(returned[1]), from_heads(returned[2]), weight_grad)


def solution(mesh):
    return jax.shard_map(
        body,
        mesh=mesh,
        in_specs=(
            P("dp", "seq", None),
            P("dp", "seq", None),
            P("dp", "seq", None),
            P("dp", "seq", None),
            P("dp", "seq", None),
        ),
        out_specs=(
            P("dp", "seq", None),
            P("dp", "seq", None),
            P("dp", "seq", None),
            P("dp", "seq"),
        ),
        check_vma=False,
    )
```

profile of v0, /device:TPU:0, one launch (start us, length us, event | category | flops | bytes accessed | tf_op | source)
XLA Modules:
  0.0 255.6 jit_solution(17739342030090548654)
XLA Ops:
  9.6 6.5 %all-to-all-start.2 = ((bf16[64,8,512]{2,0,1:T(8,128)(2,1)}), bf16[64,8,512]{2,0,1:T(8,128)(2,1)S(1)}, u32[]{:S(2)}, u32[]{:S(2)}) async-start(bf16[64,8,512]{2,0,1:T(8,128)(2,1)} %bitcast.15), calls=%async_computation.2 | async-start | bytes 1048576 | tf_op jit(solution)/shard_map/all_to_all | solution.py:42
  17.4 14.0 %all-to-all-done.2 = bf16[64,8,512]{2,0,1:T(8,128)(2,1)S(1)} async-done(((bf16[64,8,512]{2,0,1:T(8,128)(2,1)}), bf16[64,8,512]{2,0,1:T(8,128)(2,1)S(1)}, u32[]{:S(2)}, u32[]{:S(2)}) %all-to-all-start.2) | async-done | bytes 524320 | tf_op jit(solution)/shard_map/all_to_all | solution.py:42
  31.4 3.6 %all-to-all-start.3 = ((bf16[64,8,512]{2,0,1:T(8,128)(2,1)}), bf16[64,8,512]{2,0,1:T(8,128)(2,1)S(1)}, u32[]{:S(2)}, u32[]{:S(2)}) async-start(bf16[64,8,512]{2,0,1:T(8,128)(2,1)} %bitcast.24), calls=%async_computation.3 | async-start | bytes 1048576 | tf_op jit(solution)/shard_map/all_to_all | solution.py:43
  36.4 13.9 %all-to-all-done.3 = bf16[64,8,512]{2,0,1:T(8,128)(2,1)S(1)} async-done(((bf16[64,8,512]{2,0,1:T(8,128)(2,1)}), bf16[64,8,512]{2,0,1:T(8,128)(2,1)S(1)}, u32[]{:S(2)}, u32[]{:S(2)}) %all-to-all-start.3) | async-done | bytes 524320 | tf_op jit(solution)/shard_map/all_to_all | solution.py:43
  50.4 3.5 %all-to-all-start = ((bf16[64,8,512]{2,0,1:T(8,128)(2,1)}), bf16[64,8,512]{2,0,1:T(8,128)(2,1)S(1)}, u32[]{:S(2)}, u32[]{:S(2)}) async-start(bf16[64,8,512]{2,0,1:T(8,128)(2,1)} %bitcast.1), calls=%async_computation | async-start | bytes 1048576 | tf_op jit(solution)/shard_map/all_to_all | solution.py:41
  55.9 13.2 %all-to-all-done = bf16[64,8,512]{2,0,1:T(8,128)(2,1)S(1)} async-done(((bf16[64,8,512]{2,0,1:T(8,128)(2,1)}), bf16[64,8,512]{2,0,1:T(8,128)(2,1)S(1)}, u32[]{:S(2)}, u32[]{:S(2)}) %all-to-all-start) | async-done | bytes 524320 | tf_op jit(solution)/shard_map/all_to_all | solution.py:41
  69.1 3.5 %all-to-all-start.1 = ((bf16[64,8,512]{2,0,1:T(8,128)(2,1)}), bf16[64,8,512]{2,0,1:T(8,128)(2,1)S(1)}, u32[]{:S(2)}, u32[]{:S(2)}) async-start(bf16[64,8,512]{2,0,1:T(8,128)(2,1)} %bitcast.10), calls=%async_computation.1 | async-start | bytes 1048576 | tf_op jit(solution)/shard_map/all_to_all | solution.py:40
  77.6 10.3 %all-to-all-done.1 = bf16[64,8,512]{2,0,1:T(8,128)(2,1)S(1)} async-done(((bf16[64,8,512]{2,0,1:T(8,128)(2,1)}), bf16[64,8,512]{2,0,1:T(8,128)(2,1)S(1)}, u32[]{:S(2)}, u32[]{:S(2)}) %all-to-all-start.1) | async-done | bytes 524320 | tf_op jit(solution)/shard_map/all_to_all | solution.py:40
  89.5 3.8 %all-to-all-start.7 = ((bf16[64,8,2048]{2,0,1:T(8,128)(2,1)}), bf16[64,8,2048]{2,0,1:T(8,128)(2,1)S(1)}, u32[]{:S(2)}, u32[]{:S(2)}) async-start(bf16[64,8,2048]{2,0,1:T(8,128)(2,1)} %bitcast.65), calls=%async_computation.7 | async-start | bytes 4194304 | tf_op jit(solution)/shard_map/all_to_all | solution.py:118
  114.6 2.5 scatter-add.34
  121.4 2.4 fusion.17
  126.1 2.4 fusion.24
  133.6 2.5 fusion.26
  136.2 3.9 %copy.167 = bf16[1024,4,128]{2,1,0:T(4,128)(2,1)} copy(f32[1024,4,128]{2,0,1:T(8,128)} %fusion.26) | data formatting | bytes 3145728 | tf_op jit(solution)/shard_map/scatter-add | solution.py:97
  141.6 3.0 %fusion.60 = (bf16[512,1,512]{2,1,0:T(2,128)(2,1)S(1)}, f32[512,1,512]{2,1,0:T(1,128)}) fusion(pred[]{:T(512)S(6)} %eq.5, bf16[512,2,512]{2,1,0:T(2,128)(2,1)S(1)} %reshape.498), kind=kLoop, calls=%fused_computation.98 | loop fusion | flops 786432 | bytes 2621441 | tf_op jit(solution)/shard_map/convert_element_type | solution.py:106
  146.0 2.4 fusion.54
  150.4 2.7 %fusion.53 = bf16[128,4,128]{2,0,1:T(8,128)(2,1)} fusion(f32[4,128,256]{1,2,0:T(8,128)} %convolution_bitcast_fusion.9, bf16[256,4,128]{2,1,0:T(4,128)(2,1)} %copy-done.18, f32[4,128,256]{1,2,0:T(8,128)} %get-tuple-element.129, f32[4,128]{1,0:T(4,128)S(1)} %get-tuple-element.128), kind=kOutput, calls=%fused_computation.91 | convolution fusion | flops 34538240 | bytes 1443840 | tf_op jit(solution)/shard_map/hqk,khd->qhd/dot_general | solution.py:90
  154.2 2.7 %fusion.52 = bf16[128,4,128]{2,0,1:T(8,128)(2,1)} fusion(f32[4,128,256]{1,2,0:T(8,128)} %convolution_bitcast_fusion.10, bf16[256,4,128]{2,1,0:T(4,128)(2,1)} %slice.311, f32[4,128,256]{1,2,0:T(8,128)} %get-tuple-element.131, f32[4,128]{1,0:T(4,128)S(1)} %get-tuple-element.130), kind=kOutput, calls=%fused_computation.90 | convolution fusion | flops 34538240 | bytes 1443840 | tf_op jit(solution)/shard_map/hqk,khd->qhd/dot_general | solution.py:90
  160.3 2.4 convolution_bitcast_fusion.7
  162.7 2.6 %scatter-add.26 = f32[1024,4,128]{2,0,1:T(8,128)} pad(f32[256,4,128]{2,0,1:T(8,128)} %convolution_bitcast_fusion.7, f32[]{:T(128)} %constant.216.clone.1), padding=0_768x0_0x0_0 | pad | bytes 2621444 | tf_op jit(solution)/shard_map/scatter-add | solution.py:94
  165.3 2.8 %fusion.18 = f32[1024,4,128]{2,0,1:T(8,128)} fusion(f32[1024,4,128]{2,0,1:T(8,128)} %scatter-add.26, f32[4,128,256]{1,2,0:T(8,128)} %convolution_bitcast_fusion.10, bf16[128,4,128]{2,1,0:T(4,128)(2,1)S(1)} %copy-done.23, f32[4,128,256]{1,2,0:T(8,128)} %get-tuple-element.131, f32[4,128]{1,0:T(4,128)S(1)} %get-tuple-element.130), kind=kOutput, calls=%fused_computation.43 | convolution fusion | flops 34472704 | bytes 2756608 | tf_op jit(solution)/shard_map/hqk,qhd->khd/dot_general | solution.py:95
  170.1 4.8 %all-to-all-start.4 = ((bf16[8,64,1,512]{3,1,2,0:T(8,128)(2,1)}), bf16[8,64,1,512]{3,1,2,0:T(8,128)(2,1)}, u32[]{:S(2)}, u32[]{:S(2)}) async-start(bf16[8,64,1,512]{3,1,2,0:T(8,128)(2,1)} %bitcast.239), calls=%async_computation.4 | async-start | bytes 1048576 | tf_op jit(solution)/shard_map/all_to_all | solution.py:142
  174.9 2.3 fusion.241
  181.4 2.9 %copy.181 = f32[2048,1,256]{2,0,1:T(8,128)} copy(f32[2048,1,256]{0,2,1:T(8,128)} %get-tuple-element.100) | data formatting | bytes 4194304
  187.7 2.8 %fusion.20 = f32[1024,4,128]{2,0,1:T(8,128)} fusion(f32[1024,4,128]{2,0,1:T(8,128)} %fusion.18, f32[4,128,256]{1,2,0:T(8,128)} %convolution_bitcast_fusion.9, bf16[128,4,128]{2,1,0:T(4,128)(2,1)S(1)} %copy-done.22, f32[4,128,256]{1,2,0:T(8,128)} %get-tuple-element.129, f32[4,128]{1,0:T(4,128)S(1)} %get-tuple-element.128), kind=kOutput, calls=%fused_computation.50 | convolution fusion | flops 34603776 | bytes 3280896 | tf_op jit(solution)/shard_map/hqk,qhd->khd/dot_general | solution.py:95
  190.5 2.8 %fusion.22 = f32[1024,4,128]{2,0,1:T(8,128)} fusion(f32[1024,4,128]{2,0,1:T(8,128)} %fusion.20, f32[4,128,256]{1,2,0:T(8,128)} %copy-done.7, bf16[128,4,128]{2,1,0:T(4,128)(2,1)S(1)} %copy-done.20, f32[4,128,256]{1,2,0:T(8,128)} %get-tuple-element.127, f32[4,128]{1,0:T(4,128)S(1)} %get-tuple-element.126), kind=kOutput, calls=%fused_computation.52 | convolution fusion | flops 34603776 | bytes 3280896 | tf_op jit(solution)/shard_map/hqk,qhd->khd/dot_general | solution.py:95
  193.3 3.9 %copy.160 = bf16[1024,4,128]{2,1,0:T(4,128)(2,1)} copy(f32[1024,4,128]{2,0,1:T(8,128)} %fusion.22) | data formatting | bytes 3145728 | tf_op jit(solution)/shard_map/scatter-add | solution.py:94
  198.7 3.0 %fusion.57 = (bf16[512,1,512]{2,1,0:T(2,128)(2,1)S(1)}, f32[512,1,512]{2,1,0:T(1,128)}) fusion(pred[]{:T(512)S(6)} %eq.5, bf16[512,2,512]{2,1,0:T(2,128)(2,1)S(1)} %reshape.494), kind=kLoop, calls=%fused_computation.95 | loop fusion | flops 786432 | bytes 2621441 | tf_op jit(solution)/shard_map/convert_element_type | solution.py:106
  202.7 2.7 %fusion.8 = bf16[2048,256]{1,0:T(8,128)(2,1)} fusion(bf16[2048,256]{1,0:T(8,128)(2,1)} %collective-permute-done.4, f32[2048,1,256]{2,0,1:T(8,128)S(1)} %copy-done, f32[2048,1,256]{2,0,1:T(8,128)S(1)} %copy.182, pred[]{:T(512)S(6)} %eq.5), kind=kLoop, calls=%fused_computation.9 | loop fusion | flops 2097152 | bytes 6291457 | tf_op jit(solution)/shard_map/convert_element_type | solution.py:128
  206.7 19.9 %all_to_all.120 = bf16[8,64,1,512]{3,1,2,0:T(8,128)(2,1)S(1)} all-to-all(bf16[8,64,1,512]{3,1,2,0:T(8,128)(2,1)S(1)} %bitcast.248), channel_id=1, replica_groups=mesh['dp'=4,'seq'=8] {'seq'}, dimensions={0} | all-to-all | bytes 1048576 | tf_op jit(solution)/shard_map/all_to_all | solution.py:143
  226.6 3.8 %all-to-all-start.6 = ((bf16[8,64,1,512]{3,1,2,0:T(8,128)(2,1)}), bf16[8,64,1,512]{3,1,2,0:T(8,128)(2,1)S(1)}, u32[]{:S(2)}, u32[]{:S(2)}) async-start(bf16[8,64,1,512]{3,1,2,0:T(8,128)(2,1)} %bitcast.60), calls=%async_computation.6 | async-start | bytes 1048576 | tf_op jit(solution)/shard_map/all_to_all | solution.py:144
  234.6 10.8 %all-to-all-done.6 = bf16[8,64,1,512]{3,1,2,0:T(8,128)(2,1)S(1)} async-done(((bf16[8,64,1,512]{3,1,2,0:T(8,128)(2,1)}), bf16[8,64,1,512]{3,1,2,0:T(8,128)(2,1)S(1)}, u32[]{:S(2)}, u32[]{:S(2)}) %all-to-all-start.6) | async-done | bytes 524320 | tf_op jit(solution)/shard_map/all_to_all | solution.py:144
  (150 shorter events, 76.6 us)
Async XLA Ops:
  7.2 8.9 %copy-start.12 = (bf16[1,128,2048]{2,1,0:T(8,128)(2,1)S(1)}, bf16[1,128,2048]{2,1,0:T(8,128)(2,1)}, u32[]{:S(2)}) copy-start(bf16[1,128,2048]{2,1,0:T(8,128)(2,1)} %param.24) | copy-start | bytes 1572868
  9.6 25.5 %copy-start.13 = (bf16[1,128,2048]{2,1,0:T(8,128)(2,1)S(1)}, bf16[1,128,2048]{2,1,0:T(8,128)(2,1)}, u32[]{:S(2)}) copy-start(bf16[1,128,2048]{2,1,0:T(8,128)(2,1)} %param.22) | copy-start | bytes 1572868
  9.6 21.8 %all-to-all-start.2 = ((bf16[64,8,512]{2,0,1:T(8,128)(2,1)}), bf16[64,8,512]{2,0,1:T(8,128)(2,1)S(1)}, u32[]{:S(2)}, u32[]{:S(2)}) async-start(bf16[64,8,512]{2,0,1:T(8,128)(2,1)} %bitcast.15), calls=%async_computation.2 | async-start | bytes 1048576 | tf_op jit(solution)/shard_map/all_to_all | solution.py:42
  31.4 22.4 %copy-start.14 = (bf16[1,128,2048]{2,1,0:T(8,128)(2,1)S(1)}, bf16[1,128,2048]{2,1,0:T(8,128)(2,1)}, u32[]{:S(2)}) copy-start(bf16[1,128,2048]{2,1,0:T(8,128)(2,1)} %param.21) | copy-start | bytes 1572868
  31.4 18.9 %all-to-all-start.3 = ((bf16[64,8,512]{2,0,1:T(8,128)(2,1)}), bf16[64,8,512]{2,0,1:T(8,128)(2,1)S(1)}, u32[]{:S(2)}, u32[]{:S(2)}) async-start(bf16[64,8,512]{2,0,1:T(8,128)(2,1)} %bitcast.24), calls=%async_computation.3 | async-start | bytes 1048576 | tf_op jit(solution)/shard_map/all_to_all | solution.py:43
  50.4 18.8 %all-to-all-start = ((bf16[64,8,512]{2,0,1:T(8,128)(2,1)}), bf16[64,8,512]{2,0,1:T(8,128)(2,1)S(1)}, u32[]{:S(2)}, u32[]{:S(2)}) async-start(bf16[64,8,512]{2,0,1:T(8,128)(2,1)} %bitcast.1), calls=%async_computation | async-start | bytes 1048576 | tf_op jit(solution)/shard_map/all_to_all | solution.py:41
  69.1 18.8 %all-to-all-start.1 = ((bf16[64,8,512]{2,0,1:T(8,128)(2,1)}), bf16[64,8,512]{2,0,1:T(8,128)(2,1)S(1)}, u32[]{:S(2)}, u32[]{:S(2)}) async-start(bf16[64,8,512]{2,0,1:T(8,128)(2,1)} %bitcast.10), calls=%async_computation.1 | async-start | bytes 1048576 | tf_op jit(solution)/shard_map/all_to_all | solution.py:40
  74.1 30.5 %collective-permute-start = (bf16[512,512]{1,0:T(8,128)(2,1)S(1)}, bf16[512,512]{1,0:T(8,128)(2,1)}, u32[]{:S(2)}, u32[]{:S(2)}) collective-permute-start(bf16[512,512]{1,0:T(8,128)(2,1)S(1)} %bitcast.238), channel_id=1, source_target_pairs={{0,1},{1,0},{2,3},{3,2},{4,5},{5,4},{6,7},{7,6},{8,9},{9,8},{10,11... | collective-permute-start | bytes 1572872 | tf_op jit(solution)/shard_map/ppermute | solution.py:10
  76.6 51.8 %collective-permute-start.1 = (bf16[512,512]{1,0:T(8,128)(2,1)S(1)}, bf16[512,512]{1,0:T(8,128)(2,1)}, u32[]{:S(2)}, u32[]{:S(2)}) collective-permute-start(bf16[512,512]{1,0:T(8,128)(2,1)S(1)} %bitcast.237), channel_id=1, source_target_pairs={{0,1},{1,0},{2,3},{3,2},{4,5},{5,4},{6,7},{7,6},{8,9},{9,8},{10,11... | collective-permute-start | bytes 1572872 | tf_op jit(solution)/shard_map/ppermute | solution.py:10
  89.5 80.6 %all-to-all-start.7 = ((bf16[64,8,2048]{2,0,1:T(8,128)(2,1)}), bf16[64,8,2048]{2,0,1:T(8,128)(2,1)S(1)}, u32[]{:S(2)}, u32[]{:S(2)}) async-start(bf16[64,8,2048]{2,0,1:T(8,128)(2,1)} %bitcast.65), calls=%async_computation.7 | async-start | bytes 4194304 | tf_op jit(solution)/shard_map/all_to_all | solution.py:118
  110.1 6.9 %copy-start.15 = (bf16[256,4,128]{2,1,0:T(4,128)(2,1)}, bf16[256,4,128]{2,1,0:T(4,128)(2,1)S(1)}, u32[]{:S(2)}) copy-start(bf16[256,4,128]{2,1,0:T(4,128)(2,1)S(1)} %slice.303) | copy-start | bytes 786436
  112.3 4.8 %copy-start.19 = (bf16[128,4,128]{2,1,0:T(4,128)(2,1)S(1)}, bf16[128,4,128]{2,1,0:T(4,128)(2,1)}, u32[]{:S(2)}) copy-start(bf16[128,4,128]{2,1,0:T(4,128)(2,1)} %slice.329) | copy-start | bytes 393220
  117.1 4.3 %copy-start.9 = (bf16[128,4,128]{2,1,0:T(4,128)(2,1)S(1)}, bf16[128,4,128]{2,1,0:T(4,128)(2,1)}, u32[]{:S(2)}) copy-start(bf16[128,4,128]{2,1,0:T(4,128)(2,1)} %slice.317) | copy-start | bytes 393220
  121.4 4.7 %copy-start.11 = (bf16[128,4,128]{2,1,0:T(4,128)(2,1)S(1)}, bf16[128,4,128]{2,1,0:T(4,128)(2,1)}, u32[]{:S(2)}) copy-start(bf16[128,4,128]{2,1,0:T(4,128)(2,1)} %slice.325) | copy-start | bytes 393220
  124.2 4.3 %copy-start.18 = (bf16[256,4,128]{2,1,0:T(4,128)(2,1)}, bf16[256,4,128]{2,1,0:T(4,128)(2,1)S(1)}, u32[]{:S(2)}) copy-start(bf16[256,4,128]{2,1,0:T(4,128)(2,1)S(1)} %slice.319) | copy-start | bytes 786436
  141.5 4.2 %copy-start.6 = (bf16[256,4,128]{2,1,0:T(4,128)(2,1)S(1)}, bf16[256,4,128]{2,1,0:T(4,128)(2,1)}, u32[]{:S(2)}) copy-start(bf16[256,4,128]{2,1,0:T(4,128)(2,1)} %slice.331) | copy-start | bytes 786436
  145.5 22.5 %collective-permute-start.3 = (bf16[512,512]{1,0:T(8,128)(2,1)}, bf16[512,512]{1,0:T(8,128)(2,1)}, u32[]{:S(2)}, u32[]{:S(2)}) collective-permute-start(bf16[512,512]{1,0:T(8,128)(2,1)} %bitcast.233), channel_id=1, source_target_pairs={{0,1},{1,0},{2,3},{3,2},{4,5},{5,4},{6,7},{7,6},{8,9},{9,8},{10,11... | collective-permute-start | bytes 1572872 | tf_op jit(solution)/shard_map/ppermute | solution.py:10
  146.0 7.2 %copy-start.7 = (f32[4,128,256]{1,2,0:T(8,128)}, f32[4,128,256]{1,2,0:T(8,128)S(1)}, u32[]{:S(2)}) copy-start(f32[4,128,256]{1,2,0:T(8,128)S(1)} %convolution_bitcast_fusion.8) | copy-start | bytes 1572868
  148.5 4.7 %copy-start.4 = (bf16[256,4,128]{2,1,0:T(4,128)(2,1)S(1)}, bf16[256,4,128]{2,1,0:T(4,128)(2,1)}, u32[]{:S(2)}) copy-start(bf16[256,4,128]{2,1,0:T(4,128)(2,1)} %slice.315) | copy-start | bytes 786436
  148.5 4.7 %copy-start.10 = (bf16[128,4,128]{2,1,0:T(4,128)(2,1)S(1)}, bf16[128,4,128]{2,1,0:T(4,128)(2,1)}, u32[]{:S(2)}) copy-start(bf16[128,4,128]{2,1,0:T(4,128)(2,1)} %slice.317) | copy-start | bytes 393220
  153.2 3.8 %copy-start.8 = (bf16[128,4,128]{2,1,0:T(4,128)(2,1)S(1)}, bf16[128,4,128]{2,1,0:T(4,128)(2,1)}, u32[]{:S(2)}) copy-start(bf16[128,4,128]{2,1,0:T(4,128)(2,1)} %slice.309) | copy-start | bytes 393220
  154.2 3.0 %copy-start.16 = (bf16[256,4,128]{2,1,0:T(4,128)(2,1)S(1)}, bf16[256,4,128]{2,1,0:T(4,128)(2,1)}, u32[]{:S(2)}) copy-start(bf16[256,4,128]{2,1,0:T(4,128)(2,1)} %copy-done.15) | copy-start | bytes 786436
  160.3 5.0 %copy-start.23 = (bf16[128,4,128]{2,1,0:T(4,128)(2,1)S(1)}, bf16[128,4,128]{2,1,0:T(4,128)(2,1)}, u32[]{:S(2)}) copy-start(bf16[128,4,128]{2,1,0:T(4,128)(2,1)} %slice.313) | copy-start | bytes 393220
  162.7 5.4 %copy-start.1 = (f32[512,1,512]{2,1,0:T(1,128)S(1)}, f32[512,1,512]{2,1,0:T(1,128)}, u32[]{:S(2)}) copy-start(f32[512,1,512]{2,1,0:T(1,128)} %get-tuple-element.103) | copy-start | bytes 3145732
  170.1 36.5 %all-to-all-start.4 = ((bf16[8,64,1,512]{3,1,2,0:T(8,128)(2,1)}), bf16[8,64,1,512]{3,1,2,0:T(8,128)(2,1)}, u32[]{:S(2)}, u32[]{:S(2)}) async-start(bf16[8,64,1,512]{3,1,2,0:T(8,128)(2,1)} %bitcast.239), calls=%async_computation.4 | async-start | bytes 1048576 | tf_op jit(solution)/shard_map/all_to_all | solution.py:142
  174.9 72.1 %reduce-scatter.2.cloned.1.call-start = ((), (), s32[]{:S(2)}) async-start(), calls=%async_computation.9 | async-start | bytes 1310720 | tf_op jit(solution)/shard_map/reduce_scatter | solution.py:127
  184.4 3.3 %copy-start.22 = (bf16[128,4,128]{2,1,0:T(4,128)(2,1)S(1)}, bf16[128,4,128]{2,1,0:T(4,128)(2,1)}, u32[]{:S(2)}) copy-start(bf16[128,4,128]{2,1,0:T(4,128)(2,1)} %slice.321) | copy-start | bytes 393220
  185.6 4.9 %copy-start.20 = (bf16[128,4,128]{2,1,0:T(4,128)(2,1)S(1)}, bf16[128,4,128]{2,1,0:T(4,128)(2,1)}, u32[]{:S(2)}) copy-start(bf16[128,4,128]{2,1,0:T(4,128)(2,1)} %slice.329) | copy-start | bytes 393220
  185.6 17.1 %collective-permute-start.4 = (bf16[2048,256]{1,0:T(8,128)(2,1)}, bf16[2048,256]{1,0:T(8,128)(2,1)}, u32[]{:S(2)}, u32[]{:S(2)}) collective-permute-start(bf16[2048,256]{1,0:T(8,128)(2,1)} %fusion.61), channel_id=1, source_target_pairs={{0,1},{1,0},{2,3},{3,2},{4,5},{5,4},{6,7},{7,6},{8,9},{9,8},{10,11... | collective-permute-start | bytes 3145736 | tf_op jit(solution)/shard_map/ppermute | solution.py:10
  198.7 3.9 %copy-start = (f32[2048,1,256]{2,0,1:T(8,128)S(1)}, f32[2048,1,256]{2,0,1:T(8,128)}, u32[]{:S(2)}) copy-start(f32[2048,1,256]{2,0,1:T(8,128)} %copy.181) | copy-start | bytes 6291460
  202.7 2.8 %collective-permute-start.2 = (bf16[512,512]{1,0:T(8,128)(2,1)}, bf16[512,512]{1,0:T(8,128)(2,1)}, u32[]{:S(2)}, u32[]{:S(2)}) collective-permute-start(bf16[512,512]{1,0:T(8,128)(2,1)} %bitcast.234), channel_id=1, source_target_pairs={{0,1},{1,0},{2,3},{3,2},{4,5},{5,4},{6,7},{7,6},{8,9},{9,8},{10,11... | collective-permute-start | bytes 1572872 | tf_op jit(solution)/shard_map/ppermute | solution.py:10
  226.6 18.8 %all-to-all-start.6 = ((bf16[8,64,1,512]{3,1,2,0:T(8,128)(2,1)}), bf16[8,64,1,512]{3,1,2,0:T(8,128)(2,1)S(1)}, u32[]{:S(2)}, u32[]{:S(2)}) async-start(bf16[8,64,1,512]{3,1,2,0:T(8,128)(2,1)} %bitcast.60), calls=%async_computation.6 | async-start | bytes 1048576 | tf_op jit(solution)/shard_map/all_to_all | solution.py:144
  (9 other events, 18.4 us)
Sparse Core Ops, SparseCore 0:
  205.5 28.9 reduce-scatter.1
where the time goes:
time: 258 us; the launch traced here: 256 us
  waiting for transfers between devices  62.4 us (24%)
  local copies, waits for them, and re-layouts  61.6 us (24%)
  matrix products  44 us (17%)
  starting transfers between devices  32.3 us (13%)
  other arithmetic  21 us (8%)
  blocking collectives  19.9 us (8%)
  between operations  14.5 us (6%)
    all_to_all x1, blocking collectives, body(): lax.all_to_all(to_tokens(key_grad), 'seq', split_axis=0, concat_axis=2, t...  19.9 us
    all_to_all x1, waiting for transfers between devices, body(): lax.all_to_all(to_heads(values), 'seq', split_axis=1, concat_axis=0, tile...  14 us
    all_to_all x1, waiting for transfers between devices, body(): lax.all_to_all(to_heads(out_grad), 'seq', split_axis=1, concat_axis=0, ti...  13.9 us
    all_to_all x1, waiting for transfers between devices, body(): lax.all_to_all(to_heads(key_vectors), 'seq', split_axis=1, concat_axis=0,...  13.2 us
    dot_general x4, matrix products, body(): jnp.einsum('hqk,qhd->khd', dscore, query_block, preferred_element_type=jn...  10.8 us
    all_to_all x1, waiting for transfers between devices, body(): lax.all_to_all(to_tokens(value_grad), 'seq', split_axis=0, concat_axis=2,...  10.8 us
    all_to_all x1, waiting for transfers between devices, body(): lax.all_to_all(to_heads(queries), 'seq', split_axis=1, concat_axis=0, til...  10.3 us
    dot_general x4, matrix products, body(): jnp.einsum('hqk,qhd->khd', probs_low, grad_block, preferred_element_type=...  9.58 us
  transfers between devices with their start and end apart: 13, of which 5 were waited for; matrix products, arithmetic and copies ran while one was open for 48% of the time, Pallas kernels for 0%

commit v1 on v0

--- a/solution.py
+++ b/solution.py
@@ -1,6 +1,8 @@
 import jax
 import jax.numpy as jnp
 from jax import lax
+from jax.experimental import pallas as pl
+from jax.experimental.pallas import tpu as pltpu
 from jax.sharding import PartitionSpec as P
 
 HD = 128
@@ -146,9 +148,197 @@
     return (from_heads(returned[0]), from_heads(returned[1]), from_heads(returned[2]), weight_grad)
 
 
+def swap(value, axis, bit):
+    return lax.ppermute(value, axis, [(i, i ^ bit) for i in range(lax.axis_size(axis))])
+
+
+def dot(a, b, dims):
+    return lax.dot_general(a, b, (dims, ((), ())), preferred_element_type=jnp.float32)
+
+
+def probs_by_key(core, queries, keys):
+    rows = queries.shape[0]
+    scores = dot(keys, queries, ((1,), (1,))) * HD ** (-0.5)
+    key_pos = (lax.broadcasted_iota(jnp.int32, (rows, rows), 0) + core * (rows // 2)) & (rows - 1)
+    query_pos = (lax.broadcasted_iota(jnp.int32, (rows, rows), 1) + core * (rows // 2)) & (rows - 1)
+    scores = jnp.where(key_pos <= query_pos, scores, -jnp.inf)
+    weights = jnp.exp(scores - jnp.max(scores, axis=0, keepdims=True))
+    return weights * (1.0 / jnp.sum(weights, axis=0, keepdims=True))
+
+
+def both(mine, theirs):
+    return jnp.concatenate([mine[...], theirs[...]], axis=0)
+
+
+def value_kernel(place, q0, q1, k0, k1, g0, g1, mine, theirs):
+    half = q0.shape[0]
+    probs = probs_by_key(place[0], both(q0, q1), both(k0, k1))
+    grad = dot(probs.astype(jnp.bfloat16), both(g0, g1), ((1,), (0,))).astype(jnp.bfloat16)
+    mine[...] = grad[:half]
+    theirs[...] = grad[half:]
+
+
+def value_part(place, head, q, k, g):
+    half, width = q[0].shape
+    groups = width // (4 * HD)
+    taken = pl.BlockSpec((half, HD), lambda i, place: (0, 4 * i + 2 * place[0] + head))
+    given = pl.BlockSpec((half, HD), lambda i, place: (0, i))
+    out = jax.ShapeDtypeStruct((half, groups * HD), jnp.bfloat16)
+    return pl.pallas_call(
+        value_kernel,
+        grid_spec=pltpu.PrefetchScalarGridSpec(
+            num_scalar_prefetch=1, grid=(groups,), in_specs=[taken] * 6, out_specs=[given] * 2
+        ),
+        out_shape=[out, out],
+        name=f"value_part_{head}",
+    )(place, *q, *k, *g)
+
+
+def score_kernel(place, q0, q1, k0, k1, v0, v1, g0, g1, q_mine, q_theirs, k_mine, k_theirs):
+    half = q0.shape[0]
+    queries, keys = both(q0, q1), both(k0, k1)
+    probs = probs_by_key(place[0], queries, keys)
+    dprob = dot(both(v0, v1), both(g0, g1), ((1,), (1,)))
+    delta = jnp.sum(probs * dprob, axis=0, keepdims=True)
+    dscore = (probs * (dprob - delta) * HD ** (-0.5)).astype(jnp.bfloat16)
+    key_grad = dot(dscore, queries, ((1,), (0,))).astype(jnp.bfloat16)
+    query_grad = dot(dscore, keys, ((0,), (0,))).astype(jnp.bfloat16)
+    q_mine[...] = query_grad[:half]
+    q_theirs[...] = query_grad[half:]
+    k_mine[...] = key_grad[:half]
+    k_theirs[...] = key_grad[half:]
+
+
+def score_part(place, q, k, v, g):
+    half, width = q[0].shape
+    heads = width // (2 * HD)
+    taken = pl.BlockSpec(
+        (half, HD), lambda i, place: (0, 4 * (i // 2) + 2 * place[0] + i % 2)
+    )
+    given = pl.BlockSpec((half, HD), lambda i, place: (0, i))
+    out = jax.ShapeDtypeStruct((half, heads * HD), jnp.bfloat16)
+    return pl.pallas_call(
+        score_kernel,
+        grid_spec=pltpu.PrefetchScalarGridSpec(
+            num_scalar_prefetch=1, grid=(heads,), in_specs=[taken] * 8, out_specs=[given] * 4
+        ),
+        out_shape=[out] * 4,
+        name="score_part",
+    )(place, *q, *k, *v, *g)
+
+
+def turn_kernel(*refs):
+    out = refs[-1]
+    rows = refs[0].shape[0]
+    for i, piece in enumerate(refs[:-1]):
+        out[:, i * rows : (i + 1) * rows] = piece[...].T
+
+
+def turned(pieces):
+    rows, columns = pieces[0].shape
+    return pl.pallas_call(
+        turn_kernel,
+        out_shape=jax.ShapeDtypeStruct((columns, rows * len(pieces)), jnp.bfloat16),
+        name="turned",
+    )(*pieces)
+
+
+def term_kernel(place, x_ref, *refs):
+    grads, outs, total = refs[:-5], refs[-5:-1], refs[-1]
+    values = jnp.concatenate([ref[...] for ref in grads], axis=0)
+    total[...] = dot(x_ref[...], values, ((1,), (0,)))
+    for apart, out in enumerate(outs):
+        start = pl.multiple_of((place[1] ^ apart) * HD, HD)
+        out[...] = total[:, pl.ds(start, HD)].astype(out.dtype)
+
+
+def term_part(place, x_turned, grads):
+    rows = x_turned.shape[0]
+    vmem = pl.BlockSpec(memory_space=pltpu.VMEM)
+    kept = jax.ShapeDtypeStruct((rows, HD), jnp.float32)
+    sent = jax.ShapeDtypeStruct((rows, HD), jnp.bfloat16)
+    return pl.pallas_call(
+        term_kernel,
+        in_specs=[pl.BlockSpec(memory_space=pltpu.SMEM)] + [vmem] * (1 + len(grads)),
+        out_shape=[kept, sent, sent, sent],
+        scratch_shapes=[pltpu.VMEM((rows, grads[0].shape[1]), jnp.float32)],
+        name="term_part",
+    )(place, x_turned, *grads)
+
+
+def join_kernel(place, *refs):
+    ins, outs = refs[:-3], refs[-3:]
+    for mine, first in ((True, 0), (False, 4)):
+        core = place[0] if mine else 1 - place[0]
+        for out, parts in zip(outs, (ins[first : first + 1], ins[first + 1 : first + 2], ins[first + 2 : first + 4])):
+            step = 2 * HD // len(parts)
+            for j, part in enumerate(parts):
+                for i in range(part.shape[1] // step):
+                    start = pl.multiple_of((4 * i + 2 * core) * HD + j * step, HD)
+                    out[:, pl.ds(start, step)] = part[:, i * step : (i + 1) * step]
+
+
+def joined(place, mine, theirs):
+    half = mine[0].shape[0]
+    width = 2 * mine[0].shape[1]
+    vmem = pl.BlockSpec(memory_space=pltpu.VMEM)
+    out = jax.ShapeDtypeStruct((half, width), jnp.bfloat16)
+    return pl.pallas_call(
+        join_kernel,
+        in_specs=[pl.BlockSpec(memory_space=pltpu.SMEM)] + [vmem] * 8,
+        out_shape=[out] * 3,
+        name="joined",
+    )(place, *mine, *theirs)
+
+
+def chip_body(queries, key_vectors, values, out_grad, inputs):
+    sample = lax.axis_index("dp")
+    spot = lax.axis_index("seq")
+    place = jnp.stack([spot % 2, spot // 2]).astype(jnp.int32)
+    q, k, g, v = ((a[0], swap(a[0], "seq", 1)) for a in (queries, key_vectors, out_grad, values))
+
+    block = inputs.shape[2] // 4
+    x_here = [
+        lax.dynamic_slice_in_dim(inputs[0], (sample ^ apart) * block, block, axis=1)
+        for apart in range(4)
+    ]
+    x_mine = [x_here[0]] + [swap(x_here[apart], "dp", apart) for apart in (1, 2, 3)]
+    x_pieces = []
+    for piece in x_mine:
+        x_pieces += [piece, swap(piece, "seq", 1)]
+    x_turned = turned(x_pieces)
+
+    value_mine, value_theirs, own, received = [], [], [], []
+    for head in range(2):
+        a, b = value_part(place, head, q, k, g)
+        value_mine.append(a)
+        value_theirs.append(b)
+    for head in range(2):
+        a, b = value_mine[head], value_theirs[head]
+        a_y, b_x = swap(a, "dp", 2), swap(b, "dp", 1)
+        b_y, a_x = swap(b, "dp", 2), swap(a, "dp", 1)
+        a_xy, b_xy = swap(a_y, "dp", 1), swap(b_x, "dp", 2)
+        term = term_part(place, x_turned, [a, b, a_x, b_x, a_y, b_y, a_xy, b_xy])
+        own.append(term[0])
+        received.append([swap(term[apart], "seq", 2 * apart) for apart in (1, 2, 3)])
+    weight_grad = jnp.concatenate(
+        [
+            mine + sum(part.astype(jnp.float32) for part in parts)
+            for mine, parts in zip(own, received)
+        ],
+        axis=1,
+    )
+
+    q_mine, q_theirs, k_mine, k_theirs = score_part(place, q, k, v, g)
+    back = [swap(a, "seq", 1) for a in (q_theirs, k_theirs, *value_theirs)]
+    query_grad, key_grad, value_grad = joined(place, [q_mine, k_mine, *value_mine], back)
+    return query_grad[None], key_grad[None], value_grad[None], weight_grad
+
+
 def solution(mesh):
+    on_chip = mesh.shape["dp"] == 4 and mesh.shape["seq"] == 8
     return jax.shard_map(
-        body,
+        chip_body if on_chip else body,
         mesh=mesh,
         in_specs=(
             P("dp", "seq", None),

time: 258 us -> 86.8 us (0.34)
  local copies, waits for them, and re-layouts: 61.6 us -> 2.71 us
  matrix products: 44 us -> 0 us
  waiting for transfers between devices: 62.4 us -> 20.4 us
  Pallas kernels: 0 us -> 29.2 us
  blocking collectives: 19.9 us -> 0 us
  other arithmetic: 21 us -> 1.61 us
  between operations: 14.5 us -> 0.97 us
    all_to_all x7 -> x0, waiting for transfers between devices: 62.3 us -> none  [the longest x1 14 us: body(): lax.all_to_all(to_heads(values), 'seq', split_axis=1, concat_axis=0, tile...]
    dot_general x17 -> x0, matrix products: 35.7 us -> none  [the longest x4 10.8 us: body(): jnp.einsum('hqk,qhd->khd', dscore, query_block, preferred_element_type=jn...]
    all_to_all x7 -> x0, starting transfers between devices: 29.4 us -> none  [the longest x1 6.46 us: body(): lax.all_to_all(to_heads(values), 'seq', split_axis=1, concat_axis=0, tile...]
    pallas_call x0 -> x7, Pallas kernels: none -> 29.2 us  [the longest x2 9.17 us: value_part(): pl.pallas_call(value_kernel, grid_spec=pltpu.PrefetchScalarGridSpec(num_s...]
    ppermute x5 -> x33, starting transfers between devices: 2.89 us -> 30.5 us  [swap(): lax.ppermute(value, axis, [(i, i ^ bit) for i in range(lax.axis_size(axis...]
    slice x27 -> x0, local copies, waits for them, and re-layouts: 22.2 us -> none  [the longest x5 8.26 us: body(): query_block = query_heads[start:stop]]
    ppermute x5 -> x33, waiting for transfers between devices: 0.01 us -> 20.4 us  [swap(): lax.ppermute(value, axis, [(i, i ^ bit) for i in range(lax.axis_size(axis...]
    all_to_all x1 -> x0, blocking collectives: 19.9 us -> none  [body(): lax.all_to_all(to_tokens(key_grad), 'seq', split_axis=0, concat_axis=2, t...]
  transfers between devices with their start and end apart: 13 -> 33, of which waited for: 5 -> 8; matrix products, arithmetic and copies ran while one was open for 48% -> 2% of each run, Pallas kernels for 0% -> 34%
where the time goes in v1:
time: 86.8 us; the launch traced here: 85.4 us
  starting transfers between devices  30.5 us (35%)
  Pallas kernels  29.2 us (34%)
  waiting for transfers between devices  20.4 us (24%)
  local copies, waits for them, and re-layouts  2.71 us (3%)
  other arithmetic  1.61 us (2%)
  between operations  0.97 us (1%)
    ppermute x33, starting transfers between devices, swap(): lax.ppermute(value, axis, [(i, i ^ bit) for i in range(lax.axis_size(axis...  30.5 us
    ppermute x33, waiting for transfers between devices, swap(): lax.ppermute(value, axis, [(i, i ^ bit) for i in range(lax.axis_size(axis...  20.4 us
    pallas_call x2, Pallas kernels, value_part(): pl.pallas_call(value_kernel, grid_spec=pltpu.PrefetchScalarGridSpec(num_s...  9.17 us
    pallas_call x1, Pallas kernels, score_part(): pl.pallas_call(score_kernel, grid_spec=pltpu.PrefetchScalarGridSpec(num_s...  8.24 us
    pallas_call x2, Pallas kernels, term_part(): pl.pallas_call(term_kernel, in_specs=[pl.BlockSpec(memory_space=pltpu.SME...  6.37 us
    pallas_call x1, Pallas kernels, joined(): pl.pallas_call(join_kernel, in_specs=[pl.BlockSpec(memory_space=pltpu.SME...  2.7 us
    pallas_call x1, Pallas kernels, turned(): pl.pallas_call(turn_kernel, out_shape=jax.ShapeDtypeStruct((columns, rows...  2.68 us
  transfers between devices with their start and end apart: 33, of which 8 were waited for; matrix products, arithmetic and copies ran while one was open for 2% of the time, Pallas kernels for 34%

profile of v1, /device:TPU:0, one launch (start us, length us, event | category | flops | bytes accessed | tf_op | source)
XLA Modules:
  0.0 85.4 jit_solution(17967965431842512115)
XLA Ops:
  1.7 1.2 %dynamic-slice_bitcast_fusion = (bf16[128,512]{1,0:T(8,128)(2,1)S(1)}, bf16[128,512]{1,0:T(8,128)(2,1)S(1)}, bf16[128,512]{1,0:T(8,128)(2,1)S(1)}, bf16[128,512]{1,0:T(8,128)(2,1)S(1)}) fusion(bf16[1,128,2048]{2,1,0:T(8,128)(2,1)} %param.9, s32[]{:T(128)S(6)} %select_n.28, s32[]{:T(128)S(6)} %select_n.26, s32[]{:T(128)S(6)} %select_n.25, s32[]{:T(128)S(6)} %select_n.27), kind=kLoop, calls=%fused_computation.3 | loop fusion | bytes 1048592 | tf_op jit(solution)/shard_map/dynamic_slice | solution.py:302
  2.9 2.6 %collective-permute-start.9 = (bf16[128,512]{1,0:T(8,128)(2,1)S(1)}, bf16[128,512]{1,0:T(8,128)(2,1)S(1)}, u32[]{:S(2)}, u32[]{:S(2)}) collective-permute-start(bf16[128,512]{1,0:T(8,128)(2,1)S(1)} %get-tuple-element.43), channel_id=1, source_target_pairs={{0,8},{8,0},{16,24},{24,16},{1,9},{9,1},{17,25},{25,17},{2,10},{10... | collective-permute-start | bytes 393224 | tf_op jit(solution)/shard_map/ppermute | solution.py:152
  5.5 1.5 %collective-permute-start.11 = (bf16[128,512]{1,0:T(8,128)(2,1)S(1)}, bf16[128,512]{1,0:T(8,128)(2,1)S(1)}, u32[]{:S(2)}, u32[]{:S(2)}) collective-permute-start(bf16[128,512]{1,0:T(8,128)(2,1)S(1)} %get-tuple-element.45), channel_id=1, source_target_pairs={{0,16},{8,24},{16,0},{24,8},{1,17},{9,25},{17,1},{25,9},{2,18},{10... | collective-permute-start | bytes 393224 | tf_op jit(solution)/shard_map/ppermute | solution.py:152
  7.0 2.6 %collective-permute-done.9.refs_2_ = bf16[128,512]{1,0:T(8,128)(2,1)S(1)} collective-permute-done((bf16[128,512]{1,0:T(8,128)(2,1)S(1)}, bf16[128,512]{1,0:T(8,128)(2,1)S(1)}, u32[]{:S(2)}, u32[]{:S(2)}) %collective-permute-start.9) | collective-permute-done | bytes 131104 | tf_op jit(solution)/shard_map/ppermute | solution.py:152
  9.6 1.5 %collective-permute-done.11.refs_4_ = bf16[128,512]{1,0:T(8,128)(2,1)S(1)} collective-permute-done((bf16[128,512]{1,0:T(8,128)(2,1)S(1)}, bf16[128,512]{1,0:T(8,128)(2,1)S(1)}, u32[]{:S(2)}, u32[]{:S(2)}) %collective-permute-start.11) | collective-permute-done | bytes 131104 | tf_op jit(solution)/shard_map/ppermute | solution.py:152
  11.1 1.5 %collective-permute-start.13 = (bf16[128,512]{1,0:T(8,128)(2,1)S(1)}, bf16[128,512]{1,0:T(8,128)(2,1)S(1)}, u32[]{:S(2)}, u32[]{:S(2)}) collective-permute-start(bf16[128,512]{1,0:T(8,128)(2,1)S(1)} %get-tuple-element.42), channel_id=1, source_target_pairs={{0,24},{8,16},{16,8},{24,0},{1,25},{9,17},{17,9},{25,1},{2,26},{10... | collective-permute-start | bytes 393224 | tf_op jit(solution)/shard_map/ppermute | solution.py:152
  12.6 4.4 %collective-permute-done.13.refs_6_ = bf16[128,512]{1,0:T(8,128)(2,1)S(1)} collective-permute-done((bf16[128,512]{1,0:T(8,128)(2,1)S(1)}, bf16[128,512]{1,0:T(8,128)(2,1)S(1)}, u32[]{:S(2)}, u32[]{:S(2)}) %collective-permute-start.13) | collective-permute-done | bytes 131104 | tf_op jit(solution)/shard_map/ppermute | solution.py:152
  18.6 4.6 %value_part_0.1 = (bf16[128,512]{1,0:T(8,128)(2,1)}, bf16[128,512]{1,0:T(8,128)(2,1)}) custom-call(s32[2]{0:T(128)} %pad_add_fusion.place, bf16[128,2048]{1,0:T(8,128)(2,1)} %bitcast.18, bf16[128,2048]{1,0:T(8,128)(2,1)} %copy-done, bf16[128,2048]{1,0:T(8,128)(2,1)} %bitcast.22, bf16[128,2048]{1,0:T(8,128)(2,1)} %copy-done.1, bf16[128,2048]{1,0:T(8,128)(2,1)} %bitcast.26, ...), custom_call_target="tpu_custom_call" | custom-call | tf_op jit(solution)/shard_map/value_part_0/pallas_call | solution.py:187
  23.5 4.6 %value_part_1.1 = (bf16[128,512]{1,0:T(8,128)(2,1)}, bf16[128,512]{1,0:T(8,128)(2,1)}) custom-call(s32[2]{0:T(128)} %pad_add_fusion.place, bf16[128,2048]{1,0:T(8,128)(2,1)} %bitcast.19, bf16[128,2048]{1,0:T(8,128)(2,1)} %copy-done, bf16[128,2048]{1,0:T(8,128)(2,1)} %bitcast.23, bf16[128,2048]{1,0:T(8,128)(2,1)} %copy-done.1, bf16[128,2048]{1,0:T(8,128)(2,1)} %bitcast.27, ...), custom_call_target="tpu_custom_call" | custom-call | tf_op jit(solution)/shard_map/value_part_1/pallas_call | solution.py:187
  28.6 1.2 %collective-permute-start.24 = (bf16[128,512]{1,0:T(8,128)(2,1)}, bf16[128,512]{1,0:T(8,128)(2,1)S(1)}, u32[]{:S(2)}, u32[]{:S(2)}) collective-permute-start(bf16[128,512]{1,0:T(8,128)(2,1)} %get-tuple-element.26.refs_3_.refs_0_), channel_id=1, source_target_pairs={{0,8},{8,0},{16,24},{24,16},{1,9},{9,1},{17,25},{25,17},{2,10},{10... | collective-permute-start | bytes 393224 | tf_op jit(solution)/shard_map/ppermute | solution.py:152
  29.8 0.8 collective-permute-start.25
  30.6 1.5 %collective-permute-start.26 = (bf16[128,512]{1,0:T(8,128)(2,1)}, bf16[128,512]{1,0:T(8,128)(2,1)S(1)}, u32[]{:S(2)}, u32[]{:S(2)}) collective-permute-start(bf16[128,512]{1,0:T(8,128)(2,1)} %get-tuple-element.26.refs_3_.refs_0_), channel_id=1, source_target_pairs={{0,16},{8,24},{16,0},{24,8},{1,17},{9,25},{17,1},{25,9},{2,18},{10... | collective-permute-start | bytes 393224 | tf_op jit(solution)/shard_map/ppermute | solution.py:152
  32.6 1.3 %collective-permute-start.15 = (bf16[128,512]{1,0:T(8,128)(2,1)S(1)}, bf16[128,512]{1,0:T(8,128)(2,1)S(1)}, u32[]{:S(2)}, u32[]{:S(2)}) collective-permute-start(bf16[128,512]{1,0:T(8,128)(2,1)S(1)} %copy-done.5), channel_id=1, source_target_pairs={{0,8},{8,0},{16,24},{24,16},{1,9},{9,1},{17,25},{25,17},{2,10},{10... | collective-permute-start | bytes 393224 | tf_op jit(solution)/shard_map/ppermute | solution.py:152
  33.9 1.2 %collective-permute-done.24.refs_2_ = bf16[128,512]{1,0:T(8,128)(2,1)S(1)} collective-permute-done((bf16[128,512]{1,0:T(8,128)(2,1)}, bf16[128,512]{1,0:T(8,128)(2,1)S(1)}, u32[]{:S(2)}, u32[]{:S(2)}) %collective-permute-start.24) | collective-permute-done | bytes 131104 | tf_op jit(solution)/shard_map/ppermute | solution.py:152
  35.1 1.2 %collective-permute-start.16 = (bf16[128,512]{1,0:T(8,128)(2,1)S(1)}, bf16[128,512]{1,0:T(8,128)(2,1)S(1)}, u32[]{:S(2)}, u32[]{:S(2)}) collective-permute-start(bf16[128,512]{1,0:T(8,128)(2,1)S(1)} %copy-done.14), channel_id=1, source_target_pairs={{0,8},{8,0},{16,24},{24,16},{1,9},{9,1},{17,25},{25,17},{2,10},{10... | collective-permute-start | bytes 393224 | tf_op jit(solution)/shard_map/ppermute | solution.py:152
  36.4 1.6 %collective-permute-done.25.refs_3_ = bf16[128,512]{1,0:T(8,128)(2,1)S(1)} collective-permute-done((bf16[128,512]{1,0:T(8,128)(2,1)}, bf16[128,512]{1,0:T(8,128)(2,1)S(1)}, u32[]{:S(2)}, u32[]{:S(2)}) %collective-permute-start.25) | collective-permute-done | bytes 131104 | tf_op jit(solution)/shard_map/ppermute | solution.py:152
  37.9 1.5 %collective-permute-start.17 = (bf16[128,512]{1,0:T(8,128)(2,1)S(1)}, bf16[128,512]{1,0:T(8,128)(2,1)S(1)}, u32[]{:S(2)}, u32[]{:S(2)}) collective-permute-start(bf16[128,512]{1,0:T(8,128)(2,1)S(1)} %copy-done.5), channel_id=1, source_target_pairs={{0,16},{8,24},{16,0},{24,8},{1,17},{9,25},{17,1},{25,9},{2,18},{10... | collective-permute-start | bytes 393224 | tf_op jit(solution)/shard_map/ppermute | solution.py:152
  39.5 8.2 %score_part.1 = (bf16[128,1024]{1,0:T(8,128)(2,1)}, bf16[128,1024]{1,0:T(8,128)(2,1)}, bf16[128,1024]{1,0:T(8,128)(2,1)}, bf16[128,1024]{1,0:T(8,128)(2,1)}) custom-call(s32[2]{0:T(128)} %pad_add_fusion.place, bf16[128,2048]{1,0:T(8,128)(2,1)} %bitcast.20, bf16[128,2048]{1,0:T(8,128)(2,1)} %copy-done, bf16[128,2048]{1,0:T(8,128)(2,1)} %bitcast.24, ...), custom_call_target="tpu_custom_call" | custom-call | tf_op jit(solution)/shard_map/score_part/pallas_call | solution.py:220
  48.4 1.2 %collective-permute-start.28 = (bf16[128,512]{1,0:T(8,128)(2,1)S(1)}, bf16[128,512]{1,0:T(8,128)(2,1)S(1)}, u32[]{:S(2)}, u32[]{:S(2)}) collective-permute-start(bf16[128,512]{1,0:T(8,128)(2,1)S(1)} %collective-permute-done.26.refs_4_), channel_id=1, source_target_pairs={{0,8},{8,0},{16,24},{24,16},{1,9},{9,1},{17,25},{25,17},{2,10},{10... | collective-permute-start | bytes 393224 | tf_op jit(solution)/shard_map/ppermute | solution.py:152
  50.2 1.5 %collective-permute-start.18 = (bf16[128,512]{1,0:T(8,128)(2,1)S(1)}, bf16[128,512]{1,0:T(8,128)(2,1)S(1)}, u32[]{:S(2)}, u32[]{:S(2)}) collective-permute-start(bf16[128,512]{1,0:T(8,128)(2,1)S(1)} %copy-done.14), channel_id=1, source_target_pairs={{0,16},{8,24},{16,0},{24,8},{1,17},{9,25},{17,1},{25,9},{2,18},{10... | collective-permute-start | bytes 393224 | tf_op jit(solution)/shard_map/ppermute | solution.py:152
  51.7 2.7 %turned.1.x_ref = bf16[512,1024]{1,0:T(8,128)(2,1)} custom-call(bf16[128,512]{1,0:T(8,128)(2,1)} %copy-done.6, bf16[128,512]{1,0:T(8,128)(2,1)} %copy-done.15, bf16[128,512]{1,0:T(8,128)(2,1)} %copy-done.11, bf16[128,512]{1,0:T(8,128)(2,1)} %copy-done.19, bf16[128,512]{1,0:T(8,128)(2,1)} %copy-done.12, bf16[128,512]{1,0:T(8,128)(2,1)} %copy-done.21, ...), custom_call_target="tpu_custom_call" | custom-call | tf_op jit(solution)/shard_map/turned/pallas_call | solution.py:239
  54.4 0.9 %collective-permute-start.19 = (bf16[128,512]{1,0:T(8,128)(2,1)S(1)}, bf16[128,512]{1,0:T(8,128)(2,1)S(1)}, u32[]{:S(2)}, u32[]{:S(2)}) collective-permute-start(bf16[128,512]{1,0:T(8,128)(2,1)S(1)} %collective-permute-done.17.refs_4_), channel_id=1, source_target_pairs={{0,8},{8,0},{16,24},{24,16},{1,9},{9,1},{17,25},{25,17},{2,10},{10... | collective-permute-start | bytes 393224 | tf_op jit(solution)/shard_map/ppermute | solution.py:152
  55.3 0.8 collective-permute-done.29.refs_7_
  56.7 3.2 %term_part.3 = (f32[512,128]{1,0:T(8,128)}, bf16[512,128]{1,0:T(8,128)(2,1)}, bf16[512,128]{1,0:T(8,128)(2,1)}, bf16[512,128]{1,0:T(8,128)(2,1)}) custom-call(s32[2]{0:T(128)} %pad_add_fusion.place, bf16[512,1024]{1,0:T(8,128)(2,1)} %turned.1.x_ref, bf16[128,512]{1,0:T(8,128)(2,1)} %get-tuple-element.26.refs_3_.refs_0_, ...), custom_call_target="tpu_custom_call" | custom-call | tf_op jit(solution)/shard_map/term_part/pallas_call | solution.py:260
  59.9 3.7 %collective-permute-start.32 = (bf16[512,128]{1,0:T(8,128)(2,1)}, bf16[512,128]{1,0:T(8,128)(2,1)S(1)}, u32[]{:S(2)}, u32[]{:S(2)}) collective-permute-start(bf16[512,128]{1,0:T(8,128)(2,1)} %get-tuple-element.41), channel_id=1, source_target_pairs={{0,6},{1,7},{2,4},{3,5},{4,2},{5,3},{6,0},{7,1},{8,14},{9,15},{10,... | collective-permute-start | bytes 393224 | tf_op jit(solution)/shard_map/ppermute | solution.py:152
  64.4 2.7 %joined.1 = (bf16[128,2048]{1,0:T(8,128)(2,1)}, bf16[128,2048]{1,0:T(8,128)(2,1)}, bf16[128,2048]{1,0:T(8,128)(2,1)}) custom-call(s32[2]{0:T(128)} %pad_add_fusion.place, bf16[128,1024]{1,0:T(8,128)(2,1)} %get-tuple-element.23.refs_0_, bf16[128,1024]{1,0:T(8,128)(2,1)} %get-tuple-element.24.refs_1_, bf16[128,512]{1,0:T(8,128)(2,1)} %get-tuple-element.25.refs_2_.refs_0_, ...), custom_call_target="tpu_custom_call" | custom-call | tf_op jit(solution)/shard_map/joined/pallas_call | solution.py:286
  68.4 3.2 %term_part.2 = (f32[512,128]{1,0:T(8,128)}, bf16[512,128]{1,0:T(8,128)(2,1)}, bf16[512,128]{1,0:T(8,128)(2,1)}, bf16[512,128]{1,0:T(8,128)(2,1)}) custom-call(s32[2]{0:T(128)} %pad_add_fusion.place, bf16[512,1024]{1,0:T(8,128)(2,1)} %turned.1.x_ref, bf16[128,512]{1,0:T(8,128)(2,1)} %get-tuple-element.25.refs_2_.refs_0_, ...), custom_call_target="tpu_custom_call" | custom-call | tf_op jit(solution)/shard_map/term_part/pallas_call | solution.py:260
  71.6 3.6 %collective-permute-start.23 = (bf16[512,128]{1,0:T(8,128)(2,1)}, bf16[512,128]{1,0:T(8,128)(2,1)S(1)}, u32[]{:S(2)}, u32[]{:S(2)}) collective-permute-start(bf16[512,128]{1,0:T(8,128)(2,1)} %get-tuple-element.37), channel_id=1, source_target_pairs={{0,6},{1,7},{2,4},{3,5},{4,2},{5,3},{6,0},{7,1},{8,14},{9,15},{10,... | collective-permute-start | bytes 393224 | tf_op jit(solution)/shard_map/ppermute | solution.py:152
  75.2 0.8 collective-permute-start.21
  76.1 3.9 %collective-permute-done.23 = bf16[512,128]{1,0:T(8,128)(2,1)S(1)} collective-permute-done((bf16[512,128]{1,0:T(8,128)(2,1)}, bf16[512,128]{1,0:T(8,128)(2,1)S(1)}, u32[]{:S(2)}, u32[]{:S(2)}) %collective-permute-start.23) | collective-permute-done | bytes 131104 | tf_op jit(solution)/shard_map/ppermute | solution.py:152
  80.0 4.5 %collective-permute-done.22 = bf16[512,128]{1,0:T(8,128)(2,1)S(1)} collective-permute-done((bf16[512,128]{1,0:T(8,128)(2,1)}, bf16[512,128]{1,0:T(8,128)(2,1)S(1)}, u32[]{:S(2)}, u32[]{:S(2)}) %collective-permute-start.22) | collective-permute-done | bytes 131104 | tf_op jit(solution)/shard_map/ppermute | solution.py:152
  84.5 0.8 pad_maximum_fusion
  (110 shorter events, 8.0 us)
Async XLA Ops:
  0.6 16.3 %collective-permute-start = (bf16[128,2048]{1,0:T(8,128)(2,1)}, bf16[128,2048]{1,0:T(8,128)(2,1)S(1)}, u32[]{:S(2)}, u32[]{:S(2)}) collective-permute-start(bf16[128,2048]{1,0:T(8,128)(2,1)} %bitcast.17), channel_id=1, source_target_pairs={{0,1},{1,0},{2,3},{3,2},{4,5},{5,4},{6,7},{7,6},{8,9},{9,8},{10,11... | collective-permute-start | bytes 1572872 | tf_op jit(solution)/shard_map/ppermute | solution.py:152
  1.1 16.3 %collective-permute-start.1 = (bf16[128,2048]{1,0:T(8,128)(2,1)}, bf16[128,2048]{1,0:T(8,128)(2,1)S(1)}, u32[]{:S(2)}, u32[]{:S(2)}) collective-permute-start(bf16[128,2048]{1,0:T(8,128)(2,1)} %bitcast.21), channel_id=1, source_target_pairs={{0,1},{1,0},{2,3},{3,2},{4,5},{5,4},{6,7},{7,6},{8,9},{9,8},{10,11... | collective-permute-start | bytes 1572872 | tf_op jit(solution)/shard_map/ppermute | solution.py:152
  1.2 16.3 %collective-permute-start.3 = (bf16[128,2048]{1,0:T(8,128)(2,1)}, bf16[128,2048]{1,0:T(8,128)(2,1)S(1)}, u32[]{:S(2)}, u32[]{:S(2)}) collective-permute-start(bf16[128,2048]{1,0:T(8,128)(2,1)} %bitcast.25), channel_id=1, source_target_pairs={{0,1},{1,0},{2,3},{3,2},{4,5},{5,4},{6,7},{7,6},{8,9},{9,8},{10,11... | collective-permute-start | bytes 1572872 | tf_op jit(solution)/shard_map/ppermute | solution.py:152
  2.9 6.7 %collective-permute-start.9 = (bf16[128,512]{1,0:T(8,128)(2,1)S(1)}, bf16[128,512]{1,0:T(8,128)(2,1)S(1)}, u32[]{:S(2)}, u32[]{:S(2)}) collective-permute-start(bf16[128,512]{1,0:T(8,128)(2,1)S(1)} %get-tuple-element.43), channel_id=1, source_target_pairs={{0,8},{8,0},{16,24},{24,16},{1,9},{9,1},{17,25},{25,17},{2,10},{10... | collective-permute-start | bytes 393224 | tf_op jit(solution)/shard_map/ppermute | solution.py:152
  5.5 5.6 %collective-permute-start.11 = (bf16[128,512]{1,0:T(8,128)(2,1)S(1)}, bf16[128,512]{1,0:T(8,128)(2,1)S(1)}, u32[]{:S(2)}, u32[]{:S(2)}) collective-permute-start(bf16[128,512]{1,0:T(8,128)(2,1)S(1)} %get-tuple-element.45), channel_id=1, source_target_pairs={{0,16},{8,24},{16,0},{24,8},{1,17},{9,25},{17,1},{25,9},{2,18},{10... | collective-permute-start | bytes 393224 | tf_op jit(solution)/shard_map/ppermute | solution.py:152
  9.6 21.0 %collective-permute-start.2 = (bf16[128,2048]{1,0:T(8,128)(2,1)S(1)}, bf16[128,2048]{1,0:T(8,128)(2,1)S(1)}, u32[]{:S(2)}, u32[]{:S(2)}) collective-permute-start(bf16[128,2048]{1,0:T(8,128)(2,1)S(1)} %bitcast.30), channel_id=1, source_target_pairs={{0,1},{1,0},{2,3},{3,2},{4,5},{5,4},{6,7},{7,6},{8,9},{9,8},{10,11... | collective-permute-start | bytes 1572872 | tf_op jit(solution)/shard_map/ppermute | solution.py:152
  11.1 5.9 %collective-permute-start.13 = (bf16[128,512]{1,0:T(8,128)(2,1)S(1)}, bf16[128,512]{1,0:T(8,128)(2,1)S(1)}, u32[]{:S(2)}, u32[]{:S(2)}) collective-permute-start(bf16[128,512]{1,0:T(8,128)(2,1)S(1)} %get-tuple-element.42), channel_id=1, source_target_pairs={{0,24},{8,16},{16,8},{24,0},{1,25},{9,17},{17,9},{25,1},{2,26},{10... | collective-permute-start | bytes 393224 | tf_op jit(solution)/shard_map/ppermute | solution.py:152
  16.9 6.3 %collective-permute-start.8 = (bf16[128,512]{1,0:T(8,128)(2,1)S(1)}, bf16[128,512]{1,0:T(8,128)(2,1)S(1)}, u32[]{:S(2)}, u32[]{:S(2)}) collective-permute-start(bf16[128,512]{1,0:T(8,128)(2,1)S(1)} %get-tuple-element.44.refs_0_), channel_id=1, source_target_pairs={{0,1},{1,0},{2,3},{3,2},{4,5},{5,4},{6,7},{7,6},{8,9},{9,8},{10,11... | collective-permute-start | bytes 393224 | tf_op jit(solution)/shard_map/ppermute | solution.py:152
  17.0 11.1 %collective-permute-start.10 = (bf16[128,512]{1,0:T(8,128)(2,1)S(1)}, bf16[128,512]{1,0:T(8,128)(2,1)S(1)}, u32[]{:S(2)}, u32[]{:S(2)}) collective-permute-start(bf16[128,512]{1,0:T(8,128)(2,1)S(1)} %collective-permute-done.9.refs_2_), channel_id=1, source_target_pairs={{0,1},{1,0},{2,3},{3,2},{4,5},{5,4},{6,7},{7,6},{8,9},{9,8},{10,11... | collective-permute-start | bytes 393224 | tf_op jit(solution)/shard_map/ppermute | solution.py:152
  17.5 11.1 %collective-permute-start.12 = (bf16[128,512]{1,0:T(8,128)(2,1)S(1)}, bf16[128,512]{1,0:T(8,128)(2,1)S(1)}, u32[]{:S(2)}, u32[]{:S(2)}) collective-permute-start(bf16[128,512]{1,0:T(8,128)(2,1)S(1)} %collective-permute-done.11.refs_4_), channel_id=1, source_target_pairs={{0,1},{1,0},{2,3},{3,2},{4,5},{5,4},{6,7},{7,6},{8,9},{9,8},{10,11... | collective-permute-start | bytes 393224 | tf_op jit(solution)/shard_map/ppermute | solution.py:152
  17.5 12.3 %collective-permute-start.14 = (bf16[128,512]{1,0:T(8,128)(2,1)S(1)}, bf16[128,512]{1,0:T(8,128)(2,1)}, u32[]{:S(2)}, u32[]{:S(2)}) collective-permute-start(bf16[128,512]{1,0:T(8,128)(2,1)S(1)} %collective-permute-done.13.refs_6_), channel_id=1, source_target_pairs={{0,1},{1,0},{2,3},{3,2},{4,5},{5,4},{6,7},{7,6},{8,9},{9,8},{10,11... | collective-permute-start | bytes 393224 | tf_op jit(solution)/shard_map/ppermute | solution.py:152
  23.3 8.8 %collective-permute-start.6 = (bf16[128,512]{1,0:T(8,128)(2,1)}, bf16[128,512]{1,0:T(8,128)(2,1)S(1)}, u32[]{:S(2)}, u32[]{:S(2)}) collective-permute-start(bf16[128,512]{1,0:T(8,128)(2,1)} %get-tuple-element.29.refs_1_), channel_id=1, source_target_pairs={{0,1},{1,0},{2,3},{3,2},{4,5},{5,4},{6,7},{7,6},{8,9},{9,8},{10,11... | collective-permute-start | bytes 393224 | tf_op jit(solution)/shard_map/ppermute | solution.py:152
  28.6 6.6 %collective-permute-start.24 = (bf16[128,512]{1,0:T(8,128)(2,1)}, bf16[128,512]{1,0:T(8,128)(2,1)S(1)}, u32[]{:S(2)}, u32[]{:S(2)}) collective-permute-start(bf16[128,512]{1,0:T(8,128)(2,1)} %get-tuple-element.26.refs_3_.refs_0_), channel_id=1, source_target_pairs={{0,8},{8,0},{16,24},{24,16},{1,9},{9,1},{17,25},{25,17},{2,10},{10... | collective-permute-start | bytes 393224 | tf_op jit(solution)/shard_map/ppermute | solution.py:152
  29.8 8.1 %collective-permute-start.25 = (bf16[128,512]{1,0:T(8,128)(2,1)}, bf16[128,512]{1,0:T(8,128)(2,1)S(1)}, u32[]{:S(2)}, u32[]{:S(2)}) collective-permute-start(bf16[128,512]{1,0:T(8,128)(2,1)} %get-tuple-element.30.refs_1_), channel_id=1, source_target_pairs={{0,8},{8,0},{16,24},{24,16},{1,9},{9,1},{17,25},{25,17},{2,10},{10... | collective-permute-start | bytes 393224 | tf_op jit(solution)/shard_map/ppermute | solution.py:152
  30.6 17.1 %collective-permute-start.26 = (bf16[128,512]{1,0:T(8,128)(2,1)}, bf16[128,512]{1,0:T(8,128)(2,1)S(1)}, u32[]{:S(2)}, u32[]{:S(2)}) collective-permute-start(bf16[128,512]{1,0:T(8,128)(2,1)} %get-tuple-element.26.refs_3_.refs_0_), channel_id=1, source_target_pairs={{0,16},{8,24},{16,0},{24,8},{1,17},{9,25},{17,1},{25,9},{2,18},{10... | collective-permute-start | bytes 393224 | tf_op jit(solution)/shard_map/ppermute | solution.py:152
  32.1 15.7 %collective-permute-start.27 = (bf16[128,512]{1,0:T(8,128)(2,1)}, bf16[128,512]{1,0:T(8,128)(2,1)S(1)}, u32[]{:S(2)}, u32[]{:S(2)}) collective-permute-start(bf16[128,512]{1,0:T(8,128)(2,1)} %get-tuple-element.30.refs_1_), channel_id=1, source_target_pairs={{0,16},{8,24},{16,0},{24,8},{1,17},{9,25},{17,1},{25,9},{2,18},{10... | collective-permute-start | bytes 393224 | tf_op jit(solution)/shard_map/ppermute | solution.py:152
  32.6 15.7 %collective-permute-start.15 = (bf16[128,512]{1,0:T(8,128)(2,1)S(1)}, bf16[128,512]{1,0:T(8,128)(2,1)S(1)}, u32[]{:S(2)}, u32[]{:S(2)}) collective-permute-start(bf16[128,512]{1,0:T(8,128)(2,1)S(1)} %copy-done.5), channel_id=1, source_target_pairs={{0,8},{8,0},{16,24},{24,16},{1,9},{9,1},{17,25},{25,17},{2,10},{10... | collective-permute-start | bytes 393224 | tf_op jit(solution)/shard_map/ppermute | solution.py:152
  35.1 14.5 %collective-permute-start.16 = (bf16[128,512]{1,0:T(8,128)(2,1)S(1)}, bf16[128,512]{1,0:T(8,128)(2,1)S(1)}, u32[]{:S(2)}, u32[]{:S(2)}) collective-permute-start(bf16[128,512]{1,0:T(8,128)(2,1)S(1)} %copy-done.14), channel_id=1, source_target_pairs={{0,8},{8,0},{16,24},{24,16},{1,9},{9,1},{17,25},{25,17},{2,10},{10... | collective-permute-start | bytes 393224 | tf_op jit(solution)/shard_map/ppermute | solution.py:152
  37.9 12.3 %collective-permute-start.17 = (bf16[128,512]{1,0:T(8,128)(2,1)S(1)}, bf16[128,512]{1,0:T(8,128)(2,1)S(1)}, u32[]{:S(2)}, u32[]{:S(2)}) collective-permute-start(bf16[128,512]{1,0:T(8,128)(2,1)S(1)} %copy-done.5), channel_id=1, source_target_pairs={{0,16},{8,24},{16,0},{24,8},{1,17},{9,25},{17,1},{25,9},{2,18},{10... | collective-permute-start | bytes 393224 | tf_op jit(solution)/shard_map/ppermute | solution.py:152
  47.8 15.8 %collective-permute-start.4 = (bf16[128,1024]{1,0:T(8,128)(2,1)}, bf16[128,1024]{1,0:T(8,128)(2,1)S(1)}, u32[]{:S(2)}, u32[]{:S(2)}) collective-permute-start(bf16[128,1024]{1,0:T(8,128)(2,1)} %get-tuple-element.27), channel_id=1, source_target_pairs={{0,1},{1,0},{2,3},{3,2},{4,5},{5,4},{6,7},{7,6},{8,9},{9,8},{10,11... | collective-permute-start | bytes 786440 | tf_op jit(solution)/shard_map/ppermute | solution.py:152
  47.9 15.7 %collective-permute-start.5 = (bf16[128,1024]{1,0:T(8,128)(2,1)}, bf16[128,1024]{1,0:T(8,128)(2,1)S(1)}, u32[]{:S(2)}, u32[]{:S(2)}) collective-permute-start(bf16[128,1024]{1,0:T(8,128)(2,1)} %get-tuple-element.28), channel_id=1, source_target_pairs={{0,1},{1,0},{2,3},{3,2},{4,5},{5,4},{6,7},{7,6},{8,9},{9,8},{10,11... | collective-permute-start | bytes 786440 | tf_op jit(solution)/shard_map/ppermute | solution.py:152
  48.4 6.0 %collective-permute-start.28 = (bf16[128,512]{1,0:T(8,128)(2,1)S(1)}, bf16[128,512]{1,0:T(8,128)(2,1)S(1)}, u32[]{:S(2)}, u32[]{:S(2)}) collective-permute-start(bf16[128,512]{1,0:T(8,128)(2,1)S(1)} %collective-permute-done.26.refs_4_), channel_id=1, source_target_pairs={{0,8},{8,0},{16,24},{24,16},{1,9},{9,1},{17,25},{25,17},{2,10},{10... | collective-permute-start | bytes 393224 | tf_op jit(solution)/shard_map/ppermute | solution.py:152
  49.6 6.5 %collective-permute-start.29 = (bf16[128,512]{1,0:T(8,128)(2,1)S(1)}, bf16[128,512]{1,0:T(8,128)(2,1)S(1)}, u32[]{:S(2)}, u32[]{:S(2)}) collective-permute-start(bf16[128,512]{1,0:T(8,128)(2,1)S(1)} %collective-permute-done.25.refs_3_), channel_id=1, source_target_pairs={{0,16},{8,24},{16,0},{24,8},{1,17},{9,25},{17,1},{25,9},{2,18},{10... | collective-permute-start | bytes 393224 | tf_op jit(solution)/shard_map/ppermute | solution.py:152
  50.2 9.7 %collective-permute-start.18 = (bf16[128,512]{1,0:T(8,128)(2,1)S(1)}, bf16[128,512]{1,0:T(8,128)(2,1)S(1)}, u32[]{:S(2)}, u32[]{:S(2)}) collective-permute-start(bf16[128,512]{1,0:T(8,128)(2,1)S(1)} %copy-done.14), channel_id=1, source_target_pairs={{0,16},{8,24},{16,0},{24,8},{1,17},{9,25},{17,1},{25,9},{2,18},{10... | collective-permute-start | bytes 393224 | tf_op jit(solution)/shard_map/ppermute | solution.py:152
  54.4 12.7 %collective-permute-start.19 = (bf16[128,512]{1,0:T(8,128)(2,1)S(1)}, bf16[128,512]{1,0:T(8,128)(2,1)S(1)}, u32[]{:S(2)}, u32[]{:S(2)}) collective-permute-start(bf16[128,512]{1,0:T(8,128)(2,1)S(1)} %collective-permute-done.17.refs_4_), channel_id=1, source_target_pairs={{0,8},{8,0},{16,24},{24,16},{1,9},{9,1},{17,25},{25,17},{2,10},{10... | collective-permute-start | bytes 393224 | tf_op jit(solution)/shard_map/ppermute | solution.py:152
  56.0 11.1 %collective-permute-start.20 = (bf16[128,512]{1,0:T(8,128)(2,1)S(1)}, bf16[128,512]{1,0:T(8,128)(2,1)S(1)}, u32[]{:S(2)}, u32[]{:S(2)}) collective-permute-start(bf16[128,512]{1,0:T(8,128)(2,1)S(1)} %collective-permute-done.16.refs_3_), channel_id=1, source_target_pairs={{0,16},{8,24},{16,0},{24,8},{1,17},{9,25},{17,1},{25,9},{2,18},{10... | collective-permute-start | bytes 393224 | tf_op jit(solution)/shard_map/ppermute | solution.py:152
  59.9 15.3 %collective-permute-start.32 = (bf16[512,128]{1,0:T(8,128)(2,1)}, bf16[512,128]{1,0:T(8,128)(2,1)S(1)}, u32[]{:S(2)}, u32[]{:S(2)}) collective-permute-start(bf16[512,128]{1,0:T(8,128)(2,1)} %get-tuple-element.41), channel_id=1, source_target_pairs={{0,6},{1,7},{2,4},{3,5},{4,2},{5,3},{6,0},{7,1},{8,14},{9,15},{10,... | collective-permute-start | bytes 393224 | tf_op jit(solution)/shard_map/ppermute | solution.py:152
  63.6 12.4 %collective-permute-start.31 = (bf16[512,128]{1,0:T(8,128)(2,1)}, bf16[512,128]{1,0:T(8,128)(2,1)S(1)}, u32[]{:S(2)}, u32[]{:S(2)}) collective-permute-start(bf16[512,128]{1,0:T(8,128)(2,1)} %get-tuple-element.40), channel_id=1, source_target_pairs={{0,4},{1,5},{2,6},{3,7},{4,0},{5,1},{6,2},{7,3},{8,12},{9,13},{10,... | collective-permute-start | bytes 393224 | tf_op jit(solution)/shard_map/ppermute | solution.py:152
  63.6 12.4 %collective-permute-start.30 = (bf16[512,128]{1,0:T(8,128)(2,1)}, bf16[512,128]{1,0:T(8,128)(2,1)S(1)}, u32[]{:S(2)}, u32[]{:S(2)}) collective-permute-start(bf16[512,128]{1,0:T(8,128)(2,1)} %get-tuple-element.39), channel_id=1, source_target_pairs={{0,2},{1,3},{2,0},{3,1},{4,6},{5,7},{6,4},{7,5},{8,10},{9,11},{10,... | collective-permute-start | bytes 393224 | tf_op jit(solution)/shard_map/ppermute | solution.py:152
  71.6 8.4 %collective-permute-start.23 = (bf16[512,128]{1,0:T(8,128)(2,1)}, bf16[512,128]{1,0:T(8,128)(2,1)S(1)}, u32[]{:S(2)}, u32[]{:S(2)}) collective-permute-start(bf16[512,128]{1,0:T(8,128)(2,1)} %get-tuple-element.37), channel_id=1, source_target_pairs={{0,6},{1,7},{2,4},{3,5},{4,2},{5,3},{6,0},{7,1},{8,14},{9,15},{10,... | collective-permute-start | bytes 393224 | tf_op jit(solution)/shard_map/ppermute | solution.py:152
  75.2 9.3 %collective-permute-start.22 = (bf16[512,128]{1,0:T(8,128)(2,1)}, bf16[512,128]{1,0:T(8,128)(2,1)S(1)}, u32[]{:S(2)}, u32[]{:S(2)}) collective-permute-start(bf16[512,128]{1,0:T(8,128)(2,1)} %get-tuple-element.36), channel_id=1, source_target_pairs={{0,4},{1,5},{2,6},{3,7},{4,0},{5,1},{6,2},{7,3},{8,12},{9,13},{10,... | collective-permute-start | bytes 393224 | tf_op jit(solution)/shard_map/ppermute | solution.py:152
  75.2 9.3 %collective-permute-start.21 = (bf16[512,128]{1,0:T(8,128)(2,1)}, bf16[512,128]{1,0:T(8,128)(2,1)S(1)}, u32[]{:S(2)}, u32[]{:S(2)}) collective-permute-start(bf16[512,128]{1,0:T(8,128)(2,1)} %get-tuple-element.35), channel_id=1, source_target_pairs={{0,2},{1,3},{2,0},{3,1},{4,6},{5,7},{6,4},{7,5},{8,10},{9,11},{10,... | collective-permute-start | bytes 393224 | tf_op jit(solution)/shard_map/ppermute | solution.py:152
  (33 other events, 257.6 us)

commit v2 on v0

--- a/solution.py
+++ b/solution.py
@@ -1,6 +1,8 @@
 import jax
 import jax.numpy as jnp
 from jax import lax
+from jax.experimental import pallas as pl
+from jax.experimental.pallas import tpu as pltpu
 from jax.sharding import PartitionSpec as P
 
 HD = 128
@@ -146,9 +148,182 @@
     return (from_heads(returned[0]), from_heads(returned[1]), from_heads(returned[2]), weight_grad)
 
 
+def swap(value, axis, bit):
+    return lax.ppermute(value, axis, [(i, i ^ bit) for i in range(lax.axis_size(axis))])
+
+
+def dot(a, b, dims):
+    return lax.dot_general(a, b, (dims, ((), ())), preferred_element_type=jnp.float32)
+
+
+def local_call(kernel, name, outs, scratch=()):
+    in_vmem = pl.BlockSpec(memory_space=pltpu.VMEM)
+
+    def call(*operands):
+        return pl.pallas_call(
+            kernel,
+            in_specs=[in_vmem] * len(operands),
+            out_specs=[in_vmem] * len(outs),
+            out_shape=outs,
+            scratch_shapes=scratch,
+            compiler_params=pltpu.CompilerParams(vmem_limit_bytes=16 << 20),
+            name=name,
+        )(*(pltpu.with_memory_space_constraint(a, pltpu.VMEM) for a in operands))
+
+    return call
+
+
+def columns(start):
+    return pl.ds(pl.multiple_of(start * HD, HD), HD)
+
+
+def both(mine, theirs, where):
+    return jnp.concatenate([mine[:, where], theirs[:, where]], axis=0)
+
+
+def probs_by_key(core, queries, keys):
+    rows = queries.shape[0]
+    scores = dot(keys, queries, ((1,), (1,))) * HD ** (-0.5)
+    key_pos = (lax.broadcasted_iota(jnp.int32, (rows, rows), 0) + core * (rows // 2)) & (rows - 1)
+    query_pos = (lax.broadcasted_iota(jnp.int32, (rows, rows), 1) + core * (rows // 2)) & (rows - 1)
+    scores = jnp.where(key_pos <= query_pos, scores, -jnp.inf)
+    weights = jnp.exp(scores - jnp.max(scores, axis=0, keepdims=True))
+    return weights * (1.0 / jnp.sum(weights, axis=0, keepdims=True))
+
+
+def value_part(head, q, k, g):
+    half, width = q[0].shape
+    groups = width // (4 * HD)
+
+    def kernel(q0, q1, k0, k1, g0, g1, out):
+        core = lax.axis_index("seq") % 2
+        for group in range(groups):
+            where = columns(4 * group + 2 * core + head)
+            probs = probs_by_key(core, both(q0, q1, where), both(k0, k1, where))
+            grad = dot(probs.astype(jnp.bfloat16), both(g0, g1, where), ((1,), (0,)))
+            out[:, group * HD : (group + 1) * HD] = grad.astype(jnp.bfloat16)
+
+    out = pltpu.VMEM((2 * half, groups * HD), jnp.bfloat16)
+    return local_call(kernel, f"value_part_{head}", [out])(*q, *k, *g)[0]
+
+
+def score_part(q, k, v, g):
+    half, width = q[0].shape
+    heads = width // (2 * HD)
+
+    def kernel(q0, q1, k0, k1, v0, v1, g0, g1, q_mine, q_theirs, k_mine, k_theirs):
+        core = lax.axis_index("seq") % 2
+        for head in range(heads):
+            where = columns(4 * (head // 2) + 2 * core + head % 2)
+            queries, keys = both(q0, q1, where), both(k0, k1, where)
+            probs = probs_by_key(core, queries, keys)
+            dprob = dot(both(v0, v1, where), both(g0, g1, where), ((1,), (1,)))
+            delta = jnp.sum(probs * dprob, axis=0, keepdims=True)
+            dscore = (probs * (dprob - delta) * HD ** (-0.5)).astype(jnp.bfloat16)
+            key_grad = dot(dscore, queries, ((1,), (0,))).astype(jnp.bfloat16)
+            query_grad = dot(dscore, keys, ((0,), (0,))).astype(jnp.bfloat16)
+            there = slice(head * HD, (head + 1) * HD)
+            q_mine[:, there] = query_grad[:half]
+            q_theirs[:, there] = query_grad[half:]
+            k_mine[:, there] = key_grad[:half]
+            k_theirs[:, there] = key_grad[half:]
+
+    out = pltpu.VMEM((half, heads * HD), jnp.bfloat16)
+    return local_call(kernel, "score_part", [out] * 4)(*q, *k, *v, *g)
+
+
+def turned(pieces):
+    rows, width = pieces[0].shape
+
+    def kernel(*refs):
+        for i, piece in enumerate(refs[:-1]):
+            refs[-1][:, i * rows : (i + 1) * rows] = piece[...].T
+
+    out = pltpu.VMEM((width, rows * len(pieces)), jnp.bfloat16)
+    return local_call(kernel, "turned", [out])(*pieces)[0]
+
+
+def term_part(x_turned, grads):
+    rows = x_turned.shape[0]
+
+    def kernel(x_ref, *refs):
+        grads, outs, total = refs[:-5], refs[-5:-1], refs[-1]
+        chip = lax.axis_index("seq") // 2
+        values = jnp.concatenate([ref[...] for ref in grads], axis=0)
+        total[...] = dot(x_ref[...], values, ((1,), (0,)))
+        for apart, out in enumerate(outs):
+            out[...] = total[:, columns(chip ^ apart)].astype(out.dtype)
+
+    kept = pltpu.VMEM((rows, HD), jnp.float32)
+    sent = pltpu.VMEM((rows, HD), jnp.bfloat16)
+    scratch = [pltpu.VMEM((rows, grads[0].shape[1]), jnp.float32)]
+    return local_call(kernel, "term_part", [kept, sent, sent, sent], scratch)(x_turned, *grads)
+
+
+def joined(mine, theirs):
+    half = mine[0].shape[0]
+    width = 2 * mine[0].shape[1]
+
+    def kernel(*refs):
+        outs = refs[-3:]
+        core = lax.axis_index("seq") % 2
+        for ins, owner in ((refs[:4], core), (refs[4:8], 1 - core)):
+            for i in range(width // (4 * HD)):
+                for j in range(2):
+                    where = columns(4 * i + 2 * owner + j)
+                    here = slice((2 * i + j) * HD, (2 * i + j + 1) * HD)
+                    outs[0][:, where] = ins[0][:, here]
+                    outs[1][:, where] = ins[1][:, here]
+                    outs[2][:, where] = ins[2 + j][:, i * HD : (i + 1) * HD]
+
+    out = jax.ShapeDtypeStruct((half, width), jnp.bfloat16)
+    return local_call(kernel, "joined", [out] * 3)(*mine, *theirs)
+
+
+def chip_body(queries, key_vectors, values, out_grad, inputs):
+    sample = lax.axis_index("dp")
+    q, k, g, v = ((a[0], swap(a[0], "seq", 1)) for a in (queries, key_vectors, out_grad, values))
+
+    block = inputs.shape[2] // 4
+    x_here = [
+        lax.dynamic_slice_in_dim(inputs[0], (sample ^ apart) * block, block, axis=1)
+        for apart in range(4)
+    ]
+    x_mine = [x_here[0]] + [swap(x_here[apart], "dp", apart) for apart in (1, 2, 3)]
+
+    grads = [value_part(head, q, k, g) for head in range(2)]
+    *x_mine, grads[1] = lax.optimization_barrier((*x_mine, grads[1]))
+    x_pieces = [a for piece in x_mine for a in (piece, swap(piece, "seq", 1))]
+    x_turned = turned(x_pieces)
+
+    half = queries.shape[1]
+    own, received = [], []
+    for grad in grads:
+        by_x, by_y = swap(grad, "dp", 1), swap(grad, "dp", 2)
+        first, second = swap(by_y[:half], "dp", 1), swap(by_x[half:], "dp", 2)
+        term = term_part(x_turned, [grad, by_x, by_y, first, second])
+        own.append(term[0])
+        received.append([swap(term[apart], "seq", 2 * apart) for apart in (1, 2, 3)])
+    weight_grad = jnp.concatenate(
+        [
+            mine + sum(part.astype(jnp.float32) for part in parts)
+            for mine, parts in zip(own, received)
+        ],
+        axis=1,
+    )
+
+    q_mine, q_theirs, k_mine, k_theirs = score_part(q, k, v, g)
+    back = [swap(a, "seq", 1) for a in (q_theirs, k_theirs, grads[0][half:], grads[1][half:])]
+    query_grad, key_grad, value_grad = joined(
+        [q_mine, k_mine, grads[0][:half], grads[1][:half]], back
+    )
+    return query_grad[None], key_grad[None], value_grad[None], weight_grad
+
+
 def solution(mesh):
+    on_chip = mesh.shape["dp"] == 4 and mesh.shape["seq"] == 8
     return jax.shard_map(
-        body,
+        chip_body if on_chip else body,
         mesh=mesh,
         in_specs=(
             P("dp", "seq", None),

time: 258 us -> 59.3 us (0.23)
  local copies, waits for them, and re-layouts: 61.6 us -> 2.35 us
  waiting for transfers between devices: 62.4 us -> 16.8 us
  matrix products: 44 us -> 0 us
  other arithmetic: 21 us -> 0.94 us
  blocking collectives: 19.9 us -> 0 us
  between operations: 14.5 us -> 0.83 us
  Pallas kernels: 0 us -> 8.84 us
  starting transfers between devices: 32.3 us -> 29.3 us
    all_to_all x7 -> x0, waiting for transfers between devices: 62.3 us -> none  [the longest x1 14 us: body(): lax.all_to_all(to_heads(values), 'seq', split_axis=1, concat_axis=0, tile...]
    dot_general x17 -> x0, matrix products: 35.7 us -> none  [the longest x4 10.8 us: body(): jnp.einsum('hqk,qhd->khd', dscore, query_block, preferred_element_type=jn...]
    all_to_all x7 -> x0, starting transfers between devices: 29.4 us -> none  [the longest x1 6.46 us: body(): lax.all_to_all(to_heads(values), 'seq', split_axis=1, concat_axis=0, tile...]
    ppermute x5 -> x29, starting transfers between devices: 2.89 us -> 29.3 us  [swap(): lax.ppermute(value, axis, [(i, i ^ bit) for i in range(lax.axis_size(axis...]
    slice x27 -> x6, local copies, waits for them, and re-layouts: 22.2 us -> 0.08 us  [the longest x4 0.04 us: chip_body(): first, second = (swap(by_y[:half], 'dp', 1), swap(by_x[half:], 'dp', 2))]
    all_to_all x1 -> x0, blocking collectives: 19.9 us -> none  [body(): lax.all_to_all(to_tokens(key_grad), 'seq', split_axis=0, concat_axis=2, t...]
    ppermute x5 -> x29, waiting for transfers between devices: 0.01 us -> 16.8 us  [swap(): lax.ppermute(value, axis, [(i, i ^ bit) for i in range(lax.axis_size(axis...]
    convert_element_type x7 -> x0, other arithmetic: 15 us -> none  [the longest x2 6.03 us: by_parity(): return (mine.astype(jnp.bfloat16), theirs.astype(jnp.bfloat16))]
  transfers between devices with their start and end apart: 13 -> 29, of which waited for: 5 -> 8; matrix products, arithmetic and copies ran while one was open for 48% -> 2% of each run, Pallas kernels for 0% -> 15%
where the time goes in v2:
time: 59.3 us; the launch traced here: 59.1 us
  starting transfers between devices  29.3 us (49%)
  waiting for transfers between devices  16.8 us (28%)
  Pallas kernels  8.84 us (15%)
  local copies, waits for them, and re-layouts  2.35 us (4%)
  other arithmetic  0.94 us (2%)
  between operations  0.83 us (1%)
    ppermute x29, starting transfers between devices, swap(): lax.ppermute(value, axis, [(i, i ^ bit) for i in range(lax.axis_size(axis...  29.3 us
    ppermute x29, waiting for transfers between devices, swap(): lax.ppermute(value, axis, [(i, i ^ bit) for i in range(lax.axis_size(axis...  16.8 us
    pallas_call x7, Pallas kernels, call(): pl.pallas_call(kernel, in_specs=[in_vmem] * len(operands), out_specs=[in_...  8.84 us
    dynamic_slice x1, local copies, waits for them, and re-layouts, chip_body(): lax.dynamic_slice_in_dim(inputs[0], (sample ^ apart) * block, block, axis=1)  1.22 us
  transfers between devices with their start and end apart: 29, of which 8 were waited for; matrix products, arithmetic and copies ran while one was open for 2% of the time, Pallas kernels for 15%

profile of v2, /device:TPU:0, one launch (start us, length us, event | category | flops | bytes accessed | tf_op | source)
XLA Modules:
  0.0 59.1 jit_solution(16303651655017124393)
XLA Ops:
  0.6 0.5 collective-permute-start
  1.7 1.2 %dynamic-slice_bitcast_fusion = (bf16[128,512]{1,0:T(8,128)(2,1)S(1)}, bf16[128,512]{1,0:T(8,128)(2,1)S(1)}, bf16[128,512]{1,0:T(8,128)(2,1)S(1)}, bf16[128,512]{1,0:T(8,128)(2,1)S(1)}) fusion(bf16[1,128,2048]{2,1,0:T(8,128)(2,1)} %param.9, s32[]{:T(128)S(6)} %select_n.15, s32[]{:T(128)S(6)} %select_n.13, s32[]{:T(128)S(6)} %select_n.12, s32[]{:T(128)S(6)} %select_n.14), kind=kLoop, calls=%fused_computation.3 | loop fusion | bytes 1048592 | tf_op jit(solution)/shard_map/dynamic_slice | solution.py:289
  3.0 3.0 %collective-permute-start.4 = (bf16[128,512]{1,0:T(8,128)(2,1)S(1)}, bf16[128,512]{1,0:T(8,128)(2,1)S(1)}, u32[]{:S(2)}, u32[]{:S(2)}) collective-permute-start(bf16[128,512]{1,0:T(8,128)(2,1)S(1)} %get-tuple-element.45), channel_id=1, source_target_pairs={{0,8},{8,0},{16,24},{24,16},{1,9},{9,1},{17,25},{25,17},{2,10},{10... | collective-permute-start | bytes 393224 | tf_op jit(solution)/shard_map/ppermute | solution.py:152
  6.0 1.5 %collective-permute-start.5 = (bf16[128,512]{1,0:T(8,128)(2,1)S(1)}, bf16[128,512]{1,0:T(8,128)(2,1)S(1)}, u32[]{:S(2)}, u32[]{:S(2)}) collective-permute-start(bf16[128,512]{1,0:T(8,128)(2,1)S(1)} %get-tuple-element.47), channel_id=1, source_target_pairs={{0,16},{8,24},{16,0},{24,8},{1,17},{9,25},{17,1},{25,9},{2,18},{10... | collective-permute-start | bytes 393224 | tf_op jit(solution)/shard_map/ppermute | solution.py:152
  7.5 1.0 %copy-done.2 = bf16[1,128,2048]{2,1,0:T(8,128)(2,1)S(1)} copy-done((bf16[1,128,2048]{2,1,0:T(8,128)(2,1)S(1)}, bf16[1,128,2048]{2,1,0:T(8,128)(2,1)}, u32[]{:S(2)}) %copy-start.2) | copy-done | bytes 524312
  8.6 1.0 %value_part_0.1.refs_0_ = bf16[256,512]{1,0:T(8,128)(2,1)S(1)} custom-call(bf16[128,2048]{1,0:T(8,128)(2,1)S(1)} %bitcast.16, bf16[128,2048]{1,0:T(8,128)(2,1)S(1)} %collective-permute-done.q1, bf16[128,2048]{1,0:T(8,128)(2,1)S(1)} %bitcast.20, bf16[128,2048]{1,0:T(8,128)(2,1)S(1)} %collective-permute-done.1.k1, bf16[128,2048]{1,0:T(8,128)(2,1)S(1)} %bitcast.24, ...), custom_call_target="tpu_custom_call" | custom-call | tf_op jit(solution)/shard_map/value_part_0/pallas_call | solution.py:163
  9.7 1.0 %value_part_1.1.refs_0_ = bf16[256,512]{1,0:T(8,128)(2,1)S(1)} custom-call(bf16[128,2048]{1,0:T(8,128)(2,1)S(1)} %bitcast.17, bf16[128,2048]{1,0:T(8,128)(2,1)S(1)} %collective-permute-done.q1, bf16[128,2048]{1,0:T(8,128)(2,1)S(1)} %bitcast.21, bf16[128,2048]{1,0:T(8,128)(2,1)S(1)} %collective-permute-done.1.k1, bf16[128,2048]{1,0:T(8,128)(2,1)S(1)} %bitcast.25, ...), custom_call_target="tpu_custom_call" | custom-call | tf_op jit(solution)/shard_map/value_part_1/pallas_call | solution.py:163
  10.7 3.3 %collective-permute-done.5.refs_4_ = bf16[128,512]{1,0:T(8,128)(2,1)S(1)} collective-permute-done((bf16[128,512]{1,0:T(8,128)(2,1)S(1)}, bf16[128,512]{1,0:T(8,128)(2,1)S(1)}, u32[]{:S(2)}, u32[]{:S(2)}) %collective-permute-start.5) | collective-permute-done | bytes 131104 | tf_op jit(solution)/shard_map/ppermute | solution.py:152
  14.0 1.2 %collective-permute-start.22 = (bf16[256,512]{1,0:T(8,128)(2,1)S(1)}, bf16[256,512]{1,0:T(8,128)(2,1)S(1)}, u32[]{:S(2)}, u32[]{:S(2)}) collective-permute-start(bf16[256,512]{1,0:T(8,128)(2,1)S(1)} %value_part_1.1.refs_0_), channel_id=1, source_target_pairs={{0,8},{8,0},{16,24},{24,16},{1,9},{9,1},{17,25},{25,17},{2,10},{10... | collective-permute-start | bytes 786440 | tf_op jit(solution)/shard_map/ppermute | solution.py:152
  15.2 0.8 %collective-permute-start.23 = (bf16[256,512]{1,0:T(8,128)(2,1)S(1)}, bf16[256,512]{1,0:T(8,128)(2,1)S(1)}, u32[]{:S(2)}, u32[]{:S(2)}) collective-permute-start(bf16[256,512]{1,0:T(8,128)(2,1)S(1)} %value_part_1.1.refs_0_), channel_id=1, source_target_pairs={{0,16},{8,24},{16,0},{24,8},{1,17},{9,25},{17,1},{25,9},{2,18},{10... | collective-permute-start | bytes 786440 | tf_op jit(solution)/shard_map/ppermute | solution.py:152
  16.0 0.5 collective-permute-start.12
  16.6 0.8 %collective-permute-done.11.refs_1_ = bf16[128,512]{1,0:T(8,128)(2,1)S(1)} collective-permute-done((bf16[128,512]{1,0:T(8,128)(2,1)S(1)}, bf16[128,512]{1,0:T(8,128)(2,1)S(1)}, u32[]{:S(2)}, u32[]{:S(2)}) %collective-permute-start.11) | collective-permute-done | bytes 131104 | tf_op jit(solution)/shard_map/ppermute | solution.py:152
  17.4 1.5 %collective-permute-start.15 = (bf16[256,512]{1,0:T(8,128)(2,1)S(1)}, bf16[256,512]{1,0:T(8,128)(2,1)S(1)}, u32[]{:S(2)}, u32[]{:S(2)}) collective-permute-start(bf16[256,512]{1,0:T(8,128)(2,1)S(1)} %value_part_0.1.refs_0_), channel_id=1, source_target_pairs={{0,8},{8,0},{16,24},{24,16},{1,9},{9,1},{17,25},{25,17},{2,10},{10... | collective-permute-start | bytes 786440 | tf_op jit(solution)/shard_map/ppermute | solution.py:152
  18.9 0.5 collective-permute-start.16
  19.4 3.3 %score_part.1 = (bf16[128,1024]{1,0:T(8,128)(2,1)S(1)}, bf16[128,1024]{1,0:T(8,128)(2,1)S(1)}, bf16[128,1024]{1,0:T(8,128)(2,1)S(1)}, bf16[128,1024]{1,0:T(8,128)(2,1)S(1)}) custom-call(bf16[128,2048]{1,0:T(8,128)(2,1)S(1)} %bitcast.18, bf16[128,2048]{1,0:T(8,128)(2,1)S(1)} %collective-permute-done.q1, bf16[128,2048]{1,0:T(8,128)(2,1)S(1)} %bitcast.22, ...), custom_call_target="tpu_custom_call" | custom-call | tf_op jit(solution)/shard_map/score_part/pallas_call | solution.py:163
  23.4 1.4 %collective-permute-done.14.refs_7_ = bf16[128,512]{1,0:T(8,128)(2,1)S(1)} collective-permute-done((bf16[128,512]{1,0:T(8,128)(2,1)S(1)}, bf16[128,512]{1,0:T(8,128)(2,1)S(1)}, u32[]{:S(2)}, u32[]{:S(2)}) %collective-permute-start.14) | collective-permute-done | bytes 131104 | tf_op jit(solution)/shard_map/ppermute | solution.py:152
  24.8 1.2 %collective-permute-start.24 = (bf16[128,512]{1,0:T(8,128)(2,1)S(1)}, bf16[128,512]{1,0:T(8,128)(2,1)S(1)}, u32[]{:S(2)}, u32[]{:S(2)}) collective-permute-start(bf16[128,512]{1,0:T(8,128)(2,1)S(1)} %slice.36), channel_id=1, source_target_pairs={{0,8},{8,0},{16,24},{24,16},{1,9},{9,1},{17,25},{25,17},{2,10},{10... | collective-permute-start | bytes 393224 | tf_op jit(solution)/shard_map/ppermute | solution.py:152
  26.1 0.5 collective-permute-done.15.refs_1_
  26.6 1.7 %collective-permute-start.25 = (bf16[128,512]{1,0:T(8,128)(2,1)S(1)}, bf16[128,512]{1,0:T(8,128)(2,1)S(1)}, u32[]{:S(2)}, u32[]{:S(2)}) collective-permute-start(bf16[128,512]{1,0:T(8,128)(2,1)S(1)} %slice.37), channel_id=1, source_target_pairs={{0,16},{8,24},{16,0},{24,8},{1,17},{9,25},{17,1},{25,9},{2,18},{10... | collective-permute-start | bytes 393224 | tf_op jit(solution)/shard_map/ppermute | solution.py:152
  28.6 1.7 %collective-permute-done.24.refs_3_ = bf16[128,512]{1,0:T(8,128)(2,1)S(1)} collective-permute-done((bf16[128,512]{1,0:T(8,128)(2,1)S(1)}, bf16[128,512]{1,0:T(8,128)(2,1)S(1)}, u32[]{:S(2)}, u32[]{:S(2)}) %collective-permute-start.24) | collective-permute-done | bytes 131104 | tf_op jit(solution)/shard_map/ppermute | solution.py:152
  30.4 1.2 %collective-permute-start.17 = (bf16[128,512]{1,0:T(8,128)(2,1)S(1)}, bf16[128,512]{1,0:T(8,128)(2,1)S(1)}, u32[]{:S(2)}, u32[]{:S(2)}) collective-permute-start(bf16[128,512]{1,0:T(8,128)(2,1)S(1)} %slice.34), channel_id=1, source_target_pairs={{0,8},{8,0},{16,24},{24,16},{1,9},{9,1},{17,25},{25,17},{2,10},{10... | collective-permute-start | bytes 393224 | tf_op jit(solution)/shard_map/ppermute | solution.py:152
  31.6 1.6 %collective-permute-start.18 = (bf16[128,512]{1,0:T(8,128)(2,1)S(1)}, bf16[128,512]{1,0:T(8,128)(2,1)S(1)}, u32[]{:S(2)}, u32[]{:S(2)}) collective-permute-start(bf16[128,512]{1,0:T(8,128)(2,1)S(1)} %slice.35), channel_id=1, source_target_pairs={{0,16},{8,24},{16,0},{24,8},{1,17},{9,25},{17,1},{25,9},{2,18},{10... | collective-permute-start | bytes 393224 | tf_op jit(solution)/shard_map/ppermute | solution.py:152
  33.2 0.8 %term_part.3 = (f32[512,128]{1,0:T(8,128)S(1)}, bf16[512,128]{1,0:T(8,128)(2,1)S(1)}, bf16[512,128]{1,0:T(8,128)(2,1)S(1)}, bf16[512,128]{1,0:T(8,128)(2,1)S(1)}) custom-call(bf16[512,1024]{1,0:T(8,128)(2,1)S(1)} %turned.1.x_ref, bf16[256,512]{1,0:T(8,128)(2,1)S(1)} %value_part_1.1.refs_0_, bf16[256,512]{1,0:T(8,128)(2,1)S(1)} %collective-permute-done.22.refs_1_, ...), custom_call_target="tpu_custom_call" | custom-call | tf_op jit(solution)/shard_map/term_part/pallas_call | solution.py:163
  34.1 3.0 %collective-permute-start.28 = (bf16[512,128]{1,0:T(8,128)(2,1)S(1)}, bf16[512,128]{1,0:T(8,128)(2,1)S(1)}, u32[]{:S(2)}, u32[]{:S(2)}) collective-permute-start(bf16[512,128]{1,0:T(8,128)(2,1)S(1)} %get-tuple-element.43), channel_id=1, source_target_pairs={{0,6},{1,7},{2,4},{3,5},{4,2},{5,3},{6,0},{7,1},{8,14},{9,15},{10,... | collective-permute-start | bytes 393224 | tf_op jit(solution)/shard_map/ppermute | solution.py:152
  37.0 1.5 %collective-permute-start.26 = (bf16[512,128]{1,0:T(8,128)(2,1)S(1)}, bf16[512,128]{1,0:T(8,128)(2,1)S(1)}, u32[]{:S(2)}, u32[]{:S(2)}) collective-permute-start(bf16[512,128]{1,0:T(8,128)(2,1)S(1)} %get-tuple-element.41), channel_id=1, source_target_pairs={{0,2},{1,3},{2,0},{3,1},{4,6},{5,7},{6,4},{7,5},{8,10},{9,11},{10,... | collective-permute-start | bytes 393224 | tf_op jit(solution)/shard_map/ppermute | solution.py:152
  38.5 1.5 %joined.1 = (bf16[128,2048]{1,0:T(8,128)(2,1)}, bf16[128,2048]{1,0:T(8,128)(2,1)}, bf16[128,2048]{1,0:T(8,128)(2,1)}) custom-call(bf16[128,1024]{1,0:T(8,128)(2,1)S(1)} %get-tuple-element.24.refs_0_, bf16[128,1024]{1,0:T(8,128)(2,1)S(1)} %get-tuple-element.25.refs_1_, bf16[128,512]{1,0:T(8,128)(2,1)S(1)} %get-tuple-element.51.refs_2_, ...), custom_call_target="tpu_custom_call" | custom-call | tf_op jit(solution)/shard_map/joined/pallas_call | solution.py:163
  40.1 0.8 %term_part.2 = (f32[512,128]{1,0:T(8,128)S(1)}, bf16[512,128]{1,0:T(8,128)(2,1)S(1)}, bf16[512,128]{1,0:T(8,128)(2,1)S(1)}, bf16[512,128]{1,0:T(8,128)(2,1)S(1)}) custom-call(bf16[512,1024]{1,0:T(8,128)(2,1)S(1)} %turned.1.x_ref, bf16[256,512]{1,0:T(8,128)(2,1)S(1)} %value_part_0.1.refs_0_, bf16[256,512]{1,0:T(8,128)(2,1)S(1)} %collective-permute-done.15.refs_1_, ...), custom_call_target="tpu_custom_call" | custom-call | tf_op jit(solution)/shard_map/term_part/pallas_call | solution.py:163
  40.9 3.0 %collective-permute-start.21 = (bf16[512,128]{1,0:T(8,128)(2,1)S(1)}, bf16[512,128]{1,0:T(8,128)(2,1)S(1)}, u32[]{:S(2)}, u32[]{:S(2)}) collective-permute-start(bf16[512,128]{1,0:T(8,128)(2,1)S(1)} %get-tuple-element.39), channel_id=1, source_target_pairs={{0,6},{1,7},{2,4},{3,5},{4,2},{5,3},{6,0},{7,1},{8,14},{9,15},{10,... | collective-permute-start | bytes 393224 | tf_op jit(solution)/shard_map/ppermute | solution.py:152
  43.9 5.3 %collective-permute-start.19 = (bf16[512,128]{1,0:T(8,128)(2,1)S(1)}, bf16[512,128]{1,0:T(8,128)(2,1)S(1)}, u32[]{:S(2)}, u32[]{:S(2)}) collective-permute-start(bf16[512,128]{1,0:T(8,128)(2,1)S(1)} %get-tuple-element.37), channel_id=1, source_target_pairs={{0,2},{1,3},{2,0},{3,1},{4,6},{5,7},{6,4},{7,5},{8,10},{9,11},{10,... | collective-permute-start | bytes 393224 | tf_op jit(solution)/shard_map/ppermute | solution.py:152
  49.2 4.4 %collective-permute-done.27 = bf16[512,128]{1,0:T(8,128)(2,1)S(1)} collective-permute-done((bf16[512,128]{1,0:T(8,128)(2,1)S(1)}, bf16[512,128]{1,0:T(8,128)(2,1)S(1)}, u32[]{:S(2)}, u32[]{:S(2)}) %collective-permute-start.27) | collective-permute-done | bytes 131104 | tf_op jit(solution)/shard_map/ppermute | solution.py:152
  53.7 4.5 %collective-permute-done.20 = bf16[512,128]{1,0:T(8,128)(2,1)S(1)} collective-permute-done((bf16[512,128]{1,0:T(8,128)(2,1)S(1)}, bf16[512,128]{1,0:T(8,128)(2,1)S(1)}, u32[]{:S(2)}, u32[]{:S(2)}) %collective-permute-start.20) | collective-permute-done | bytes 131104 | tf_op jit(solution)/shard_map/ppermute | solution.py:152
  58.2 0.8 %pad_maximum_fusion = f32[512,256]{1,0:T(8,128)} fusion(f32[512,128]{1,0:T(8,128)S(1)} %add_add_fusion, f32[512,128]{1,0:T(8,128)S(1)} %add_add_fusion.1), kind=kLoop, calls=%fused_computation | loop fusion | flops 131072 | bytes 1048576 | tf_op jit(solution)/shard_map/concatenate | solution.py:307
  (51 shorter events, 2.1 us)
Async XLA Ops:
  0.6 5.3 %collective-permute-start = (bf16[128,2048]{1,0:T(8,128)(2,1)}, bf16[128,2048]{1,0:T(8,128)(2,1)S(1)}, u32[]{:S(2)}, u32[]{:S(2)}) collective-permute-start(bf16[128,2048]{1,0:T(8,128)(2,1)} %bitcast.15), channel_id=1, source_target_pairs={{0,1},{1,0},{2,3},{3,2},{4,5},{5,4},{6,7},{7,6},{8,9},{9,8},{10,11... | collective-permute-start | bytes 1572872 | tf_op jit(solution)/shard_map/ppermute | solution.py:152
  1.1 6.3 %collective-permute-start.1 = (bf16[128,2048]{1,0:T(8,128)(2,1)}, bf16[128,2048]{1,0:T(8,128)(2,1)S(1)}, u32[]{:S(2)}, u32[]{:S(2)}) collective-permute-start(bf16[128,2048]{1,0:T(8,128)(2,1)} %bitcast.19), channel_id=1, source_target_pairs={{0,1},{1,0},{2,3},{3,2},{4,5},{5,4},{6,7},{7,6},{8,9},{9,8},{10,11... | collective-permute-start | bytes 1572872 | tf_op jit(solution)/shard_map/ppermute | solution.py:152
  1.2 6.3 %collective-permute-start.3 = (bf16[128,2048]{1,0:T(8,128)(2,1)}, bf16[128,2048]{1,0:T(8,128)(2,1)S(1)}, u32[]{:S(2)}, u32[]{:S(2)}) collective-permute-start(bf16[128,2048]{1,0:T(8,128)(2,1)} %bitcast.23), channel_id=1, source_target_pairs={{0,1},{1,0},{2,3},{3,2},{4,5},{5,4},{6,7},{7,6},{8,9},{9,8},{10,11... | collective-permute-start | bytes 1572872 | tf_op jit(solution)/shard_map/ppermute | solution.py:152
  1.7 14.4 %collective-permute-start.2 = (bf16[128,2048]{1,0:T(8,128)(2,1)}, bf16[128,2048]{1,0:T(8,128)(2,1)S(1)}, u32[]{:S(2)}, u32[]{:S(2)}) collective-permute-start(bf16[128,2048]{1,0:T(8,128)(2,1)} %bitcast.27), channel_id=1, source_target_pairs={{0,1},{1,0},{2,3},{3,2},{4,5},{5,4},{6,7},{7,6},{8,9},{9,8},{10,11... | collective-permute-start | bytes 1572872 | tf_op jit(solution)/shard_map/ppermute | solution.py:152
  1.7 5.8 %copy-start = (bf16[1,128,2048]{2,1,0:T(8,128)(2,1)S(1)}, bf16[1,128,2048]{2,1,0:T(8,128)(2,1)}, u32[]{:S(2)}) copy-start(bf16[1,128,2048]{2,1,0:T(8,128)(2,1)} %param.5) | copy-start | bytes 1572868
  1.7 5.8 %copy-start.1 = (bf16[1,128,2048]{2,1,0:T(8,128)(2,1)S(1)}, bf16[1,128,2048]{2,1,0:T(8,128)(2,1)}, u32[]{:S(2)}) copy-start(bf16[1,128,2048]{2,1,0:T(8,128)(2,1)} %param.6) | copy-start | bytes 1572868
  3.0 7.7 %collective-permute-start.4 = (bf16[128,512]{1,0:T(8,128)(2,1)S(1)}, bf16[128,512]{1,0:T(8,128)(2,1)S(1)}, u32[]{:S(2)}, u32[]{:S(2)}) collective-permute-start(bf16[128,512]{1,0:T(8,128)(2,1)S(1)} %get-tuple-element.45), channel_id=1, source_target_pairs={{0,8},{8,0},{16,24},{24,16},{1,9},{9,1},{17,25},{25,17},{2,10},{10... | collective-permute-start | bytes 393224 | tf_op jit(solution)/shard_map/ppermute | solution.py:152
  6.0 8.0 %collective-permute-start.5 = (bf16[128,512]{1,0:T(8,128)(2,1)S(1)}, bf16[128,512]{1,0:T(8,128)(2,1)S(1)}, u32[]{:S(2)}, u32[]{:S(2)}) collective-permute-start(bf16[128,512]{1,0:T(8,128)(2,1)S(1)} %get-tuple-element.47), channel_id=1, source_target_pairs={{0,16},{8,24},{16,0},{24,8},{1,17},{9,25},{17,1},{25,9},{2,18},{10... | collective-permute-start | bytes 393224 | tf_op jit(solution)/shard_map/ppermute | solution.py:152
  7.5 6.5 %collective-permute-start.6 = (bf16[128,512]{1,0:T(8,128)(2,1)S(1)}, bf16[128,512]{1,0:T(8,128)(2,1)S(1)}, u32[]{:S(2)}, u32[]{:S(2)}) collective-permute-start(bf16[128,512]{1,0:T(8,128)(2,1)S(1)} %get-tuple-element.44), channel_id=1, source_target_pairs={{0,24},{8,16},{16,8},{24,0},{1,25},{9,17},{17,9},{25,1},{2,26},{10... | collective-permute-start | bytes 393224 | tf_op jit(solution)/shard_map/ppermute | solution.py:152
  9.6 9.8 %copy-start.3 = (bf16[1,128,2048]{2,1,0:T(8,128)(2,1)S(1)}, bf16[1,128,2048]{2,1,0:T(8,128)(2,1)}, u32[]{:S(2)}) copy-start(bf16[1,128,2048]{2,1,0:T(8,128)(2,1)} %param.7) | copy-start | bytes 1572868
  9.6 6.9 %collective-permute-start.9 = (bf16[128,512]{1,0:T(8,128)(2,1)S(1)}, bf16[128,512]{1,0:T(8,128)(2,1)S(1)}, u32[]{:S(2)}, u32[]{:S(2)}) collective-permute-start(bf16[128,512]{1,0:T(8,128)(2,1)S(1)} %get-tuple-element.50), channel_id=1, source_target_pairs={{0,1},{1,0},{2,3},{3,2},{4,5},{5,4},{6,7},{7,6},{8,9},{9,8},{10,11... | collective-permute-start | bytes 393224 | tf_op jit(solution)/shard_map/ppermute | solution.py:152
  14.0 8.8 %collective-permute-start.22 = (bf16[256,512]{1,0:T(8,128)(2,1)S(1)}, bf16[256,512]{1,0:T(8,128)(2,1)S(1)}, u32[]{:S(2)}, u32[]{:S(2)}) collective-permute-start(bf16[256,512]{1,0:T(8,128)(2,1)S(1)} %value_part_1.1.refs_0_), channel_id=1, source_target_pairs={{0,8},{8,0},{16,24},{24,16},{1,9},{9,1},{17,25},{25,17},{2,10},{10... | collective-permute-start | bytes 786440 | tf_op jit(solution)/shard_map/ppermute | solution.py:152
  15.2 8.1 %collective-permute-start.23 = (bf16[256,512]{1,0:T(8,128)(2,1)S(1)}, bf16[256,512]{1,0:T(8,128)(2,1)S(1)}, u32[]{:S(2)}, u32[]{:S(2)}) collective-permute-start(bf16[256,512]{1,0:T(8,128)(2,1)S(1)} %value_part_1.1.refs_0_), channel_id=1, source_target_pairs={{0,16},{8,24},{16,0},{24,8},{1,17},{9,25},{17,1},{25,9},{2,18},{10... | collective-permute-start | bytes 786440 | tf_op jit(solution)/shard_map/ppermute | solution.py:152
  16.0 1.3 %collective-permute-start.11 = (bf16[128,512]{1,0:T(8,128)(2,1)S(1)}, bf16[128,512]{1,0:T(8,128)(2,1)S(1)}, u32[]{:S(2)}, u32[]{:S(2)}) collective-permute-start(bf16[128,512]{1,0:T(8,128)(2,1)S(1)} %get-tuple-element.32.refs_0_), channel_id=1, source_target_pairs={{0,1},{1,0},{2,3},{3,2},{4,5},{5,4},{6,7},{7,6},{8,9},{9,8},{10,11... | collective-permute-start | bytes 393224 | tf_op jit(solution)/shard_map/ppermute | solution.py:152
  16.0 2.8 %collective-permute-start.12 = (bf16[128,512]{1,0:T(8,128)(2,1)S(1)}, bf16[128,512]{1,0:T(8,128)(2,1)S(1)}, u32[]{:S(2)}, u32[]{:S(2)}) collective-permute-start(bf16[128,512]{1,0:T(8,128)(2,1)S(1)} %collective-permute-done.4.refs_2_), channel_id=1, source_target_pairs={{0,1},{1,0},{2,3},{3,2},{4,5},{5,4},{6,7},{7,6},{8,9},{9,8},{10,11... | collective-permute-start | bytes 393224 | tf_op jit(solution)/shard_map/ppermute | solution.py:152
  16.5 6.1 %collective-permute-start.13 = (bf16[128,512]{1,0:T(8,128)(2,1)S(1)}, bf16[128,512]{1,0:T(8,128)(2,1)S(1)}, u32[]{:S(2)}, u32[]{:S(2)}) collective-permute-start(bf16[128,512]{1,0:T(8,128)(2,1)S(1)} %collective-permute-done.5.refs_4_), channel_id=1, source_target_pairs={{0,1},{1,0},{2,3},{3,2},{4,5},{5,4},{6,7},{7,6},{8,9},{9,8},{10,11... | collective-permute-start | bytes 393224 | tf_op jit(solution)/shard_map/ppermute | solution.py:152
  17.4 9.2 %collective-permute-start.15 = (bf16[256,512]{1,0:T(8,128)(2,1)S(1)}, bf16[256,512]{1,0:T(8,128)(2,1)S(1)}, u32[]{:S(2)}, u32[]{:S(2)}) collective-permute-start(bf16[256,512]{1,0:T(8,128)(2,1)S(1)} %value_part_0.1.refs_0_), channel_id=1, source_target_pairs={{0,8},{8,0},{16,24},{24,16},{1,9},{9,1},{17,25},{25,17},{2,10},{10... | collective-permute-start | bytes 786440 | tf_op jit(solution)/shard_map/ppermute | solution.py:152
  18.9 9.4 %collective-permute-start.16 = (bf16[256,512]{1,0:T(8,128)(2,1)S(1)}, bf16[256,512]{1,0:T(8,128)(2,1)S(1)}, u32[]{:S(2)}, u32[]{:S(2)}) collective-permute-start(bf16[256,512]{1,0:T(8,128)(2,1)S(1)} %value_part_0.1.refs_0_), channel_id=1, source_target_pairs={{0,16},{8,24},{16,0},{24,8},{1,17},{9,25},{17,1},{25,9},{2,18},{10... | collective-permute-start | bytes 786440 | tf_op jit(solution)/shard_map/ppermute | solution.py:152
  22.7 14.4 %collective-permute-start.7 = (bf16[128,1024]{1,0:T(8,128)(2,1)S(1)}, bf16[128,1024]{1,0:T(8,128)(2,1)S(1)}, u32[]{:S(2)}, u32[]{:S(2)}) collective-permute-start(bf16[128,1024]{1,0:T(8,128)(2,1)S(1)} %get-tuple-element.27), channel_id=1, source_target_pairs={{0,1},{1,0},{2,3},{3,2},{4,5},{5,4},{6,7},{7,6},{8,9},{9,8},{10,11... | collective-permute-start | bytes 786440 | tf_op jit(solution)/shard_map/ppermute | solution.py:152
  22.8 14.3 %collective-permute-start.8 = (bf16[128,1024]{1,0:T(8,128)(2,1)S(1)}, bf16[128,1024]{1,0:T(8,128)(2,1)S(1)}, u32[]{:S(2)}, u32[]{:S(2)}) collective-permute-start(bf16[128,1024]{1,0:T(8,128)(2,1)S(1)} %get-tuple-element.28), channel_id=1, source_target_pairs={{0,1},{1,0},{2,3},{3,2},{4,5},{5,4},{6,7},{7,6},{8,9},{9,8},{10,11... | collective-permute-start | bytes 786440 | tf_op jit(solution)/shard_map/ppermute | solution.py:152
  23.3 1.5 %collective-permute-start.14 = (bf16[128,512]{1,0:T(8,128)(2,1)S(1)}, bf16[128,512]{1,0:T(8,128)(2,1)S(1)}, u32[]{:S(2)}, u32[]{:S(2)}) collective-permute-start(bf16[128,512]{1,0:T(8,128)(2,1)S(1)} %collective-permute-done.6.refs_6_), channel_id=1, source_target_pairs={{0,1},{1,0},{2,3},{3,2},{4,5},{5,4},{6,7},{7,6},{8,9},{9,8},{10,11... | collective-permute-start | bytes 393224 | tf_op jit(solution)/shard_map/ppermute | solution.py:152
  24.8 5.5 %collective-permute-start.24 = (bf16[128,512]{1,0:T(8,128)(2,1)S(1)}, bf16[128,512]{1,0:T(8,128)(2,1)S(1)}, u32[]{:S(2)}, u32[]{:S(2)}) collective-permute-start(bf16[128,512]{1,0:T(8,128)(2,1)S(1)} %slice.36), channel_id=1, source_target_pairs={{0,8},{8,0},{16,24},{24,16},{1,9},{9,1},{17,25},{25,17},{2,10},{10... | collective-permute-start | bytes 393224 | tf_op jit(solution)/shard_map/ppermute | solution.py:152
  26.6 5.0 %collective-permute-start.25 = (bf16[128,512]{1,0:T(8,128)(2,1)S(1)}, bf16[128,512]{1,0:T(8,128)(2,1)S(1)}, u32[]{:S(2)}, u32[]{:S(2)}) collective-permute-start(bf16[128,512]{1,0:T(8,128)(2,1)S(1)} %slice.37), channel_id=1, source_target_pairs={{0,16},{8,24},{16,0},{24,8},{1,17},{9,25},{17,1},{25,9},{2,18},{10... | collective-permute-start | bytes 393224 | tf_op jit(solution)/shard_map/ppermute | solution.py:152
  28.2 5.8 %collective-permute-start.10 = (bf16[128,512]{1,0:T(8,128)(2,1)S(1)}, bf16[128,512]{1,0:T(8,128)(2,1)S(1)}, u32[]{:S(2)}, u32[]{:S(2)}) collective-permute-start(bf16[128,512]{1,0:T(8,128)(2,1)S(1)} %get-tuple-element.48), channel_id=1, source_target_pairs={{0,1},{1,0},{2,3},{3,2},{4,5},{5,4},{6,7},{7,6},{8,9},{9,8},{10,11... | collective-permute-start | bytes 393224 | tf_op jit(solution)/shard_map/ppermute | solution.py:152
  30.4 9.7 %collective-permute-start.17 = (bf16[128,512]{1,0:T(8,128)(2,1)S(1)}, bf16[128,512]{1,0:T(8,128)(2,1)S(1)}, u32[]{:S(2)}, u32[]{:S(2)}) collective-permute-start(bf16[128,512]{1,0:T(8,128)(2,1)S(1)} %slice.34), channel_id=1, source_target_pairs={{0,8},{8,0},{16,24},{24,16},{1,9},{9,1},{17,25},{25,17},{2,10},{10... | collective-permute-start | bytes 393224 | tf_op jit(solution)/shard_map/ppermute | solution.py:152
  31.6 8.4 %collective-permute-start.18 = (bf16[128,512]{1,0:T(8,128)(2,1)S(1)}, bf16[128,512]{1,0:T(8,128)(2,1)S(1)}, u32[]{:S(2)}, u32[]{:S(2)}) collective-permute-start(bf16[128,512]{1,0:T(8,128)(2,1)S(1)} %slice.35), channel_id=1, source_target_pairs={{0,16},{8,24},{16,0},{24,8},{1,17},{9,25},{17,1},{25,9},{2,18},{10... | collective-permute-start | bytes 393224 | tf_op jit(solution)/shard_map/ppermute | solution.py:152
  34.1 9.8 %collective-permute-start.28 = (bf16[512,128]{1,0:T(8,128)(2,1)S(1)}, bf16[512,128]{1,0:T(8,128)(2,1)S(1)}, u32[]{:S(2)}, u32[]{:S(2)}) collective-permute-start(bf16[512,128]{1,0:T(8,128)(2,1)S(1)} %get-tuple-element.43), channel_id=1, source_target_pairs={{0,6},{1,7},{2,4},{3,5},{4,2},{5,3},{6,0},{7,1},{8,14},{9,15},{10,... | collective-permute-start | bytes 393224 | tf_op jit(solution)/shard_map/ppermute | solution.py:152
  37.0 16.5 %collective-permute-start.27 = (bf16[512,128]{1,0:T(8,128)(2,1)S(1)}, bf16[512,128]{1,0:T(8,128)(2,1)S(1)}, u32[]{:S(2)}, u32[]{:S(2)}) collective-permute-start(bf16[512,128]{1,0:T(8,128)(2,1)S(1)} %get-tuple-element.42), channel_id=1, source_target_pairs={{0,4},{1,5},{2,6},{3,7},{4,0},{5,1},{6,2},{7,3},{8,12},{9,13},{10,... | collective-permute-start | bytes 393224 | tf_op jit(solution)/shard_map/ppermute | solution.py:152
  37.0 16.5 %collective-permute-start.26 = (bf16[512,128]{1,0:T(8,128)(2,1)S(1)}, bf16[512,128]{1,0:T(8,128)(2,1)S(1)}, u32[]{:S(2)}, u32[]{:S(2)}) collective-permute-start(bf16[512,128]{1,0:T(8,128)(2,1)S(1)} %get-tuple-element.41), channel_id=1, source_target_pairs={{0,2},{1,3},{2,0},{3,1},{4,6},{5,7},{6,4},{7,5},{8,10},{9,11},{10,... | collective-permute-start | bytes 393224 | tf_op jit(solution)/shard_map/ppermute | solution.py:152
  40.9 12.7 %collective-permute-start.21 = (bf16[512,128]{1,0:T(8,128)(2,1)S(1)}, bf16[512,128]{1,0:T(8,128)(2,1)S(1)}, u32[]{:S(2)}, u32[]{:S(2)}) collective-permute-start(bf16[512,128]{1,0:T(8,128)(2,1)S(1)} %get-tuple-element.39), channel_id=1, source_target_pairs={{0,6},{1,7},{2,4},{3,5},{4,2},{5,3},{6,0},{7,1},{8,14},{9,15},{10,... | collective-permute-start | bytes 393224 | tf_op jit(solution)/shard_map/ppermute | solution.py:152
  43.9 14.3 %collective-permute-start.20 = (bf16[512,128]{1,0:T(8,128)(2,1)S(1)}, bf16[512,128]{1,0:T(8,128)(2,1)S(1)}, u32[]{:S(2)}, u32[]{:S(2)}) collective-permute-start(bf16[512,128]{1,0:T(8,128)(2,1)S(1)} %get-tuple-element.38), channel_id=1, source_target_pairs={{0,4},{1,5},{2,6},{3,7},{4,0},{5,1},{6,2},{7,3},{8,12},{9,13},{10,... | collective-permute-start | bytes 393224 | tf_op jit(solution)/shard_map/ppermute | solution.py:152
  43.9 14.3 %collective-permute-start.19 = (bf16[512,128]{1,0:T(8,128)(2,1)S(1)}, bf16[512,128]{1,0:T(8,128)(2,1)S(1)}, u32[]{:S(2)}, u32[]{:S(2)}) collective-permute-start(bf16[512,128]{1,0:T(8,128)(2,1)S(1)} %get-tuple-element.37), channel_id=1, source_target_pairs={{0,2},{1,3},{2,0},{3,1},{4,6},{5,7},{6,4},{7,5},{8,10},{9,11},{10,... | collective-permute-start | bytes 393224 | tf_op jit(solution)/shard_map/ppermute | solution.py:152
  (1 other events, 1.0 us)

commit v3 on v2

--- a/solution.py
+++ b/solution.py
@@ -177,8 +177,45 @@
     return pl.ds(pl.multiple_of(start * HD, HD), HD)
 
 
-def both(mine, theirs, where):
-    return jnp.concatenate([mine[:, where], theirs[:, where]], axis=0)
+def both(mine, theirs, group, core, head):
+    packed, spread = columns(2 * group + head), columns(4 * group + 2 * core + head)
+    return jnp.concatenate([mine[:, packed], theirs[:, spread]], axis=0)
+
+
+def packed_inputs(arrays, inputs):
+    half, width = arrays[0].shape
+    block = inputs.shape[1] // 4
+    count = len(arrays)
+    groups = width // (4 * HD)
+
+    def kernel(*refs):
+        core, sample = lax.axis_index("seq") % 2, lax.axis_index("dp")
+        outs, sems = refs[count + 1 : -1], refs[-1]
+        copies = []
+        for apart, out in enumerate(outs[count:]):
+            start = pl.multiple_of((sample ^ apart) * block, block)
+            copies.append((refs[count].at[:, pl.ds(start, block)], out))
+        for source, out in zip(refs[:count], outs):
+            for group in range(groups):
+                start = pl.multiple_of((4 * group + 2 * core) * HD, 2 * HD)
+                here = slice(2 * group * HD, 2 * (group + 1) * HD)
+                copies.append((source.at[:, pl.ds(start, 2 * HD)], out.at[:, here]))
+        copies = [pltpu.make_async_copy(a, b, sems.at[i]) for i, (a, b) in enumerate(copies)]
+        for copy in copies:
+            copy.start()
+        for copy in copies:
+            copy.wait()
+
+    return pl.pallas_call(
+        kernel,
+        in_specs=[pl.BlockSpec(memory_space=pl.ANY)] * (count + 1),
+        out_specs=[pl.BlockSpec(memory_space=pltpu.VMEM)] * (count + 4),
+        out_shape=[pltpu.VMEM((half, width // 2), jnp.bfloat16)] * count
+        + [pltpu.VMEM((half, block), jnp.bfloat16)] * 4,
+        scratch_shapes=[pltpu.SemaphoreType.DMA((4 + count * groups,))],
+        compiler_params=pltpu.CompilerParams(vmem_limit_bytes=16 << 20),
+        name="packed_inputs",
+    )(*(pltpu.with_memory_space_constraint(a, pltpu.HBM) for a in (*arrays, inputs)))
 
 
 def probs_by_key(core, queries, keys):
@@ -191,33 +228,35 @@
     return weights * (1.0 / jnp.sum(weights, axis=0, keepdims=True))
 
 
-def value_part(head, q, k, g):
-    half, width = q[0].shape
-    groups = width // (4 * HD)
-
-    def kernel(q0, q1, k0, k1, g0, g1, out):
-        core = lax.axis_index("seq") % 2
-        for group in range(groups):
-            where = columns(4 * group + 2 * core + head)
-            probs = probs_by_key(core, both(q0, q1, where), both(k0, k1, where))
-            grad = dot(probs.astype(jnp.bfloat16), both(g0, g1, where), ((1,), (0,)))
-            out[:, group * HD : (group + 1) * HD] = grad.astype(jnp.bfloat16)
-
-    out = pltpu.VMEM((2 * half, groups * HD), jnp.bfloat16)
-    return local_call(kernel, f"value_part_{head}", [out])(*q, *k, *g)[0]
+def value_part(q, k, g):
+    half, width = q[1].shape
+    order = (0, 2, 1, 3)
+
+    def kernel(q0, q1, k0, k1, g0, g1, kept, given):
+        core, chip = lax.axis_index("seq") % 2, lax.axis_index("seq") // 2
+        for at, apart in enumerate(order):
+            for head in range(2):
+                where = chip ^ apart, core, head
+                probs = probs_by_key(core, both(q0, q1, *where), both(k0, k1, *where))
+                grad = dot(probs.astype(jnp.bfloat16), both(g0, g1, *where), ((1,), (0,)))
+                here = (2 * head + at % 2) * HD
+                (kept, given)[at // 2][:, here : here + HD] = grad.astype(jnp.bfloat16)
+
+    out = pltpu.VMEM((2 * half, width // 4), jnp.bfloat16)
+    return local_call(kernel, "value_part", [out] * 2)(*q, *k, *g)
 
 
 def score_part(q, k, v, g):
-    half, width = q[0].shape
+    half, width = q[1].shape
     heads = width // (2 * HD)
 
     def kernel(q0, q1, k0, k1, v0, v1, g0, g1, q_mine, q_theirs, k_mine, k_theirs):
         core = lax.axis_index("seq") % 2
         for head in range(heads):
-            where = columns(4 * (head // 2) + 2 * core + head % 2)
-            queries, keys = both(q0, q1, where), both(k0, k1, where)
+            where = head // 2, core, head % 2
+            queries, keys = both(q0, q1, *where), both(k0, k1, *where)
             probs = probs_by_key(core, queries, keys)
-            dprob = dot(both(v0, v1, where), both(g0, g1, where), ((1,), (1,)))
+            dprob = dot(both(v0, v1, *where), both(g0, g1, *where), ((1,), (1,)))
             delta = jnp.sum(probs * dprob, axis=0, keepdims=True)
             dscore = (probs * (dprob - delta) * HD ** (-0.5)).astype(jnp.bfloat16)
             key_grad = dot(dscore, queries, ((1,), (0,))).astype(jnp.bfloat16)
@@ -243,21 +282,26 @@
     return local_call(kernel, "turned", [out])(*pieces)[0]
 
 
-def term_part(x_turned, grads):
-    rows = x_turned.shape[0]
-
-    def kernel(x_ref, *refs):
-        grads, outs, total = refs[:-5], refs[-5:-1], refs[-1]
-        chip = lax.axis_index("seq") // 2
-        values = jnp.concatenate([ref[...] for ref in grads], axis=0)
-        total[...] = dot(x_ref[...], values, ((1,), (0,)))
-        for apart, out in enumerate(outs):
-            out[...] = total[:, columns(chip ^ apart)].astype(out.dtype)
-
-    kept = pltpu.VMEM((rows, HD), jnp.float32)
-    sent = pltpu.VMEM((rows, HD), jnp.bfloat16)
-    scratch = [pltpu.VMEM((rows, grads[0].shape[1]), jnp.float32)]
-    return local_call(kernel, "term_part", [kept, sent, sent, sent], scratch)(x_turned, *grads)
+def term_part(turned_inputs, near, far):
+    rows = turned_inputs[0].shape[0]
+    width = near[0].shape[1] // 2
+    half = near[0].shape[0] // 2
+    count = len(near)
+
+    def kernel(*refs):
+        outs = refs[-2:]
+        total = None
+        for i, x_ref in enumerate(refs[:4]):
+            values = refs[4 + i // 2 * count : 4 + (i // 2 + 1) * count]
+            here = slice(i % 2 * half, (i % 2 + 1) * half)
+            part = jnp.concatenate([ref[here, :] for ref in values], axis=0)
+            product = dot(x_ref[...], part, ((1,), (0,)))
+            total = product if total is None else total + product
+        for i, out in enumerate(outs):
+            out[...] = total[:, i * width : (i + 1) * width].astype(out.dtype)
+
+    outs = [pltpu.VMEM((rows, width), kind) for kind in (jnp.float32, jnp.bfloat16)]
+    return local_call(kernel, "term_part", outs)(*turned_inputs, *near, *far)
 
 
 def joined(mine, theirs):
@@ -266,7 +310,7 @@
 
     def kernel(*refs):
         outs = refs[-3:]
-        core = lax.axis_index("seq") % 2
+        core, chip = lax.axis_index("seq") % 2, lax.axis_index("seq") // 2
         for ins, owner in ((refs[:4], core), (refs[4:8], 1 - core)):
             for i in range(width // (4 * HD)):
                 for j in range(2):
@@ -274,49 +318,51 @@
                     here = slice((2 * i + j) * HD, (2 * i + j + 1) * HD)
                     outs[0][:, where] = ins[0][:, here]
                     outs[1][:, where] = ins[1][:, here]
-                    outs[2][:, where] = ins[2 + j][:, i * HD : (i + 1) * HD]
+                    where = columns(4 * (chip ^ i) + 2 * owner + j)
+                    here = slice((2 * j + i // 2) * HD, (2 * j + i // 2 + 1) * HD)
+                    outs[2][:, where] = ins[2 + i % 2][:, here]
 
     out = jax.ShapeDtypeStruct((half, width), jnp.bfloat16)
     return local_call(kernel, "joined", [out] * 3)(*mine, *theirs)
 
 
+def after(values, *earlier):
+    return list(lax.optimization_barrier((*values, *earlier))[: len(values)])
+
+
 def chip_body(queries, key_vectors, values, out_grad, inputs):
-    sample = lax.axis_index("dp")
-    q, k, g, v = ((a[0], swap(a[0], "seq", 1)) for a in (queries, key_vectors, out_grad, values))
-
-    block = inputs.shape[2] // 4
-    x_here = [
-        lax.dynamic_slice_in_dim(inputs[0], (sample ^ apart) * block, block, axis=1)
-        for apart in range(4)
-    ]
-    x_mine = [x_here[0]] + [swap(x_here[apart], "dp", apart) for apart in (1, 2, 3)]
-
-    grads = [value_part(head, q, k, g) for head in range(2)]
-    *x_mine, grads[1] = lax.optimization_barrier((*x_mine, grads[1]))
-    x_pieces = [a for piece in x_mine for a in (piece, swap(piece, "seq", 1))]
-    x_turned = turned(x_pieces)
-
     half = queries.shape[1]
-    own, received = [], []
-    for grad in grads:
-        by_x, by_y = swap(grad, "dp", 1), swap(grad, "dp", 2)
-        first, second = swap(by_y[:half], "dp", 1), swap(by_x[half:], "dp", 2)
-        term = term_part(x_turned, [grad, by_x, by_y, first, second])
-        own.append(term[0])
-        received.append([swap(term[apart], "seq", 2 * apart) for apart in (1, 2, 3)])
-    weight_grad = jnp.concatenate(
-        [
-            mine + sum(part.astype(jnp.float32) for part in parts)
-            for mine, parts in zip(own, received)
-        ],
-        axis=1,
-    )
-
+    arrays = [a[0] for a in (queries, key_vectors, out_grad, values)]
+    *own, x_here, x_1, x_2, x_3 = packed_inputs(arrays, inputs[0])
+    q, k, g, v = ((mine, swap(a, "seq", 1)) for mine, a in zip(own, arrays))
+    x_mine = [x_here, swap(x_1, "dp", 1), swap(x_2, "dp", 2), swap(x_3, "dp", 3)]
+
+    kept, given = value_part(q, k, g)
     q_mine, q_theirs, k_mine, k_theirs = score_part(q, k, v, g)
-    back = [swap(a, "seq", 1) for a in (q_theirs, k_theirs, grads[0][half:], grads[1][half:])]
-    query_grad, key_grad, value_grad = joined(
-        [q_mine, k_mine, grads[0][:half], grads[1][:half]], back
-    )
+    back = [swap(a, "seq", 1) for a in (q_theirs, k_theirs, kept[half:], given[half:])]
+    query_grad, key_grad, value_grad = joined([q_mine, k_mine, kept[:half], given[:half]], back)
+    got = swap(given, "seq", 2)
+    sides = []
+    for head in range(2):
+        here = slice(2 * head * HD, 2 * (head + 1) * HD)
+        paired = jnp.concatenate([kept[:, here], got[:, here]], axis=0)
+        by_x, by_y = after([swap(paired, "dp", 1), swap(paired, "dp", 2)])
+        first, second = after([swap(by_y[: 2 * half], "dp", 1), swap(by_x[2 * half :], "dp", 2)])
+        near = [paired[: 2 * half], by_x[: 2 * half], by_y[: 2 * half], first]
+        far = [paired[2 * half :], by_x[2 * half :], by_y[2 * half :], second]
+        sides.append((near, far))
+
+    x_mine = after(x_mine, got, q_theirs)
+    x_own = turned(x_mine)
+    x_next = swap([x_own][0], "seq", 2)
+    x_turned = [x_own, swap(x_own, "seq", 1), x_next, swap(after([x_next], query_grad)[0], "seq", 1)]
+
+    blocks = []
+    for near, far in sides:
+        mine, sent = term_part(x_turned, near, far)
+        blocks.append(mine + swap(sent, "seq", 4).astype(jnp.float32))
+    weight_grad = jnp.concatenate(blocks, axis=1)
+
     return query_grad[None], key_grad[None], value_grad[None], weight_grad
 
 

time: 59.3 us -> 53.7 us (0.906)
  waiting for transfers between devices: 16.8 us -> 13.2 us
  local copies, waits for them, and re-layouts: 2.35 us -> 0.15 us
  Pallas kernels: 8.84 us -> 9.48 us
    ppermute x29 -> x25, waiting for transfers between devices: 16.8 us -> 13.2 us  [swap(): lax.ppermute(value, axis, [(i, i ^ bit) for i in range(lax.axis_size(axis...]
    pallas_call x0 -> x1, Pallas kernels: none -> 1.58 us  [packed_inputs(): pl.pallas_call(kernel, in_specs=[pl.BlockSpec(memory_space=pl.ANY)] * (co...]
    dynamic_slice x1 -> x0, local copies, waits for them, and re-layouts: 1.22 us -> none  [chip_body(): lax.dynamic_slice_in_dim(inputs[0], (sample ^ apart) * block, block, axis=1)]
    unnamed x8 -> x0, local copies, waits for them, and re-layouts: 1.05 us -> none
    pallas_call x7 -> x6, Pallas kernels: 8.84 us -> 7.9 us  [call(): pl.pallas_call(kernel, in_specs=[in_vmem] * len(operands), out_specs=[in_...]
    ppermute x29 -> x25, starting transfers between devices: 29.3 us -> 28.9 us  [swap(): lax.ppermute(value, axis, [(i, i ^ bit) for i in range(lax.axis_size(axis...]
  transfers between devices with their start and end apart: 29 -> 25, of which waited for: 8 -> 6; matrix products, arithmetic and copies ran while one was open for 2% -> 0% of each run, Pallas kernels for 15% -> 18%
where the time goes in v3:
time: 53.7 us; the launch traced here: 53.5 us
  starting transfers between devices  28.9 us (54%)
  waiting for transfers between devices  13.2 us (25%)
  Pallas kernels  9.48 us (18%)
  other arithmetic  0.91 us (2%)
  between operations  0.81 us (2%)
    ppermute x25, starting transfers between devices, swap(): lax.ppermute(value, axis, [(i, i ^ bit) for i in range(lax.axis_size(axis...  28.9 us
    ppermute x25, waiting for transfers between devices, swap(): lax.ppermute(value, axis, [(i, i ^ bit) for i in range(lax.axis_size(axis...  13.2 us
    pallas_call x6, Pallas kernels, call(): pl.pallas_call(kernel, in_specs=[in_vmem] * len(operands), out_specs=[in_...  7.9 us
    pallas_call x1, Pallas kernels, packed_inputs(): pl.pallas_call(kernel, in_specs=[pl.BlockSpec(memory_space=pl.ANY)] * (co...  1.58 us
  transfers between devices with their start and end apart: 25, of which 6 were waited for; matrix products, arithmetic and copies ran while one was open for 0% of the time, Pallas kernels for 18%

profile of v3, /device:TPU:0, one launch (start us, length us, event | category | flops | bytes accessed | tf_op | source)
XLA Modules:
  0.0 53.5 jit_solution(8068394855963758841)
XLA Ops:
  0.6 0.5 collective-permute-start
  1.2 0.4 collective-permute-start.3
  1.7 1.6 %packed_inputs.1 = (bf16[128,1024]{1,0:T(8,128)(2,1)S(1)}, bf16[128,1024]{1,0:T(8,128)(2,1)S(1)}, bf16[128,1024]{1,0:T(8,128)(2,1)S(1)}, bf16[128,1024]{1,0:T(8,...) custom-call(bf16[128,2048]{1,0:T(8,128)(2,1)} %bitcast.10, ...), custom_call_target="tpu_custom_call" | custom-call | tf_op jit(solution)/shard_map/packed_inputs/pallas_call | solution.py:209
  3.3 3.0 %collective-permute-start.8 = (bf16[128,512]{1,0:T(8,128)(2,1)S(1)}, bf16[128,512]{1,0:T(8,128)(2,1)S(1)}, u32[]{:S(2)}, u32[]{:S(2)}) collective-permute-start(bf16[128,512]{1,0:T(8,128)(2,1)S(1)} %get-tuple-element.52), channel_id=1, source_target_pairs={{0,8},{8,0},{16,24},{24,16},{1,9},{9,1},{17,25},{25,17},{2,10},{10... | collective-permute-start | bytes 393224 | tf_op jit(solution)/shard_map/ppermute | solution.py:152
  6.3 1.5 %collective-permute-start.9 = (bf16[128,512]{1,0:T(8,128)(2,1)S(1)}, bf16[128,512]{1,0:T(8,128)(2,1)S(1)}, u32[]{:S(2)}, u32[]{:S(2)}) collective-permute-start(bf16[128,512]{1,0:T(8,128)(2,1)S(1)} %get-tuple-element.53), channel_id=1, source_target_pairs={{0,16},{8,24},{16,0},{24,8},{1,17},{9,25},{17,1},{25,9},{2,18},{10... | collective-permute-start | bytes 393224 | tf_op jit(solution)/shard_map/ppermute | solution.py:152
  7.9 1.5 %value_part.1 = (bf16[256,512]{1,0:T(8,128)(2,1)S(1)}, bf16[256,512]{1,0:T(8,128)(2,1)S(1)}) custom-call(bf16[128,1024]{1,0:T(8,128)(2,1)S(1)} %get-tuple-element.38.q0, bf16[128,2048]{1,0:T(8,128)(2,1)S(1)} %collective-permute-done.q1, bf16[128,1024]{1,0:T(8,128)(2,1)S(1)} %get-tuple-element.39.k0, bf16[128,2048]{1,0:T(8,128)(2,1)S(1)} %collective-permute-done.1.k1, ...), custom_call_target="tpu_custom_call" | custom-call | tf_op jit(solution)/shard_map/value_part/pallas_call | solution.py:163
  9.4 2.1 %collective-permute-start.11 = (bf16[256,512]{1,0:T(8,128)(2,1)S(1)}, bf16[256,512]{1,0:T(8,128)(2,1)S(1)}, u32[]{:S(2)}, u32[]{:S(2)}) collective-permute-start(bf16[256,512]{1,0:T(8,128)(2,1)S(1)} %get-tuple-element.45), channel_id=1, source_target_pairs={{0,2},{1,3},{2,0},{3,1},{4,6},{5,7},{6,4},{7,5},{8,10},{9,11},{10,... | collective-permute-start | bytes 786440 | tf_op jit(solution)/shard_map/ppermute | solution.py:152
  11.5 3.3 %score_part.1 = (bf16[128,1024]{1,0:T(8,128)(2,1)S(1)}, bf16[128,1024]{1,0:T(8,128)(2,1)S(1)}, bf16[128,1024]{1,0:T(8,128)(2,1)S(1)}, bf16[128,1024]{1,0:T(8,128)(2,1)S(1)}) custom-call(bf16[128,1024]{1,0:T(8,128)(2,1)S(1)} %get-tuple-element.38.q0, bf16[128,2048]{1,0:T(8,128)(2,1)S(1)} %collective-permute-done.q1, ...), custom_call_target="tpu_custom_call" | custom-call | tf_op jit(solution)/shard_map/score_part/pallas_call | solution.py:163
  14.9 0.6 %collective-permute-start.5 = (bf16[128,1024]{1,0:T(8,128)(2,1)S(1)}, bf16[128,1024]{1,0:T(8,128)(2,1)S(1)}, u32[]{:S(2)}, u32[]{:S(2)}) collective-permute-start(bf16[128,1024]{1,0:T(8,128)(2,1)S(1)} %get-tuple-element.47), channel_id=1, source_target_pairs={{0,1},{1,0},{2,3},{3,2},{4,5},{5,4},{6,7},{7,6},{8,9},{9,8},{10,11... | collective-permute-start | bytes 786440 | tf_op jit(solution)/shard_map/ppermute | solution.py:152
  15.6 0.4 collective-permute-start.7
  16.0 1.2 %collective-permute-done.11 = bf16[256,512]{1,0:T(8,128)(2,1)S(1)} collective-permute-done((bf16[256,512]{1,0:T(8,128)(2,1)S(1)}, bf16[256,512]{1,0:T(8,128)(2,1)S(1)}, u32[]{:S(2)}, u32[]{:S(2)}) %collective-permute-start.11) | collective-permute-done | bytes 262176 | tf_op jit(solution)/shard_map/ppermute | solution.py:152
  17.2 0.2 turned.1.refs_0_
  17.4 1.8 %collective-permute-start.13 = (bf16[512,512]{1,0:T(8,128)(2,1)S(1)}, bf16[512,512]{1,0:T(8,128)(2,1)S(1)}, u32[]{:S(2)}, u32[]{:S(2)}) collective-permute-start(bf16[512,512]{1,0:T(8,128)(2,1)S(1)} %turned.1.refs_0_), channel_id=1, source_target_pairs={{0,2},{1,3},{2,0},{3,1},{4,6},{5,7},{6,4},{7,5},{8,10},{9,11},{10,... | collective-permute-start | bytes 1572872 | tf_op jit(solution)/shard_map/ppermute | solution.py:152
  19.2 1.6 %collective-permute-start.20 = (bf16[512,256]{1,0:T(8,128)(2,1)S(1)}, bf16[512,256]{1,0:T(8,128)(2,1)S(1)}, u32[]{:S(2)}, u32[]{:S(2)}) collective-permute-start(bf16[512,256]{1,0:T(8,128)(2,1)S(1)} %pad_maximum_fusion.2), channel_id=1, source_target_pairs={{0,8},{8,0},{16,24},{24,16},{1,9},{9,1},{17,25},{25,17},{2,10},{10... | collective-permute-start | bytes 786440 | tf_op jit(solution)/shard_map/ppermute | solution.py:152
  20.8 1.5 %collective-permute-start.21 = (bf16[512,256]{1,0:T(8,128)(2,1)S(1)}, bf16[512,256]{1,0:T(8,128)(2,1)S(1)}, u32[]{:S(2)}, u32[]{:S(2)}) collective-permute-start(bf16[512,256]{1,0:T(8,128)(2,1)S(1)} %pad_maximum_fusion.2), channel_id=1, source_target_pairs={{0,16},{8,24},{16,0},{24,8},{1,17},{9,25},{17,1},{25,9},{2,18},{10... | collective-permute-start | bytes 786440 | tf_op jit(solution)/shard_map/ppermute | solution.py:152
  22.4 0.6 %collective-permute-start.15 = (bf16[512,256]{1,0:T(8,128)(2,1)S(1)}, bf16[512,256]{1,0:T(8,128)(2,1)S(1)}, u32[]{:S(2)}, u32[]{:S(2)}) collective-permute-start(bf16[512,256]{1,0:T(8,128)(2,1)S(1)} %pad_maximum_fusion.1), channel_id=1, source_target_pairs={{0,8},{8,0},{16,24},{24,16},{1,9},{9,1},{17,25},{25,17},{2,10},{10... | collective-permute-start | bytes 786440 | tf_op jit(solution)/shard_map/ppermute | solution.py:152
  23.0 1.5 %joined.1 = (bf16[128,2048]{1,0:T(8,128)(2,1)}, bf16[128,2048]{1,0:T(8,128)(2,1)}, bf16[128,2048]{1,0:T(8,128)(2,1)}) custom-call(bf16[128,1024]{1,0:T(8,128)(2,1)S(1)} %get-tuple-element.42.refs_0_, bf16[128,1024]{1,0:T(8,128)(2,1)S(1)} %get-tuple-element.43.refs_1_, bf16[128,512]{1,0:T(8,128)(2,1)S(1)} %get-tuple-element.87.refs_2_, ...), custom_call_target="tpu_custom_call" | custom-call | tf_op jit(solution)/shard_map/joined/pallas_call | solution.py:163
  24.5 1.2 %collective-permute-done.20 = bf16[512,256]{1,0:T(8,128)(2,1)S(1)} collective-permute-done((bf16[512,256]{1,0:T(8,128)(2,1)S(1)}, bf16[512,256]{1,0:T(8,128)(2,1)S(1)}, u32[]{:S(2)}, u32[]{:S(2)}) %collective-permute-start.20) | collective-permute-done | bytes 262176 | tf_op jit(solution)/shard_map/ppermute | solution.py:152
  25.7 2.6 %collective-permute-start.16 = (bf16[512,256]{1,0:T(8,128)(2,1)S(1)}, bf16[512,256]{1,0:T(8,128)(2,1)S(1)}, u32[]{:S(2)}, u32[]{:S(2)}) collective-permute-start(bf16[512,256]{1,0:T(8,128)(2,1)S(1)} %pad_maximum_fusion.1), channel_id=1, source_target_pairs={{0,16},{8,24},{16,0},{24,8},{1,17},{9,25},{17,1},{25,9},{2,18},{10... | collective-permute-start | bytes 786440 | tf_op jit(solution)/shard_map/ppermute | solution.py:152
  28.4 1.8 %collective-permute-done.13.refs_2_ = bf16[512,512]{1,0:T(8,128)(2,1)S(1)} collective-permute-done((bf16[512,512]{1,0:T(8,128)(2,1)S(1)}, bf16[512,512]{1,0:T(8,128)(2,1)S(1)}, u32[]{:S(2)}, u32[]{:S(2)}) %collective-permute-start.13) | collective-permute-done | bytes 524320 | tf_op jit(solution)/shard_map/ppermute | solution.py:152
  30.2 1.6 %collective-permute-start.22 = (bf16[256,256]{1,0:T(8,128)(2,1)S(1)}, bf16[256,256]{1,0:T(8,128)(2,1)S(1)}, u32[]{:S(2)}, u32[]{:S(2)}) collective-permute-start(bf16[256,256]{1,0:T(8,128)(2,1)S(1)} %get-tuple-element.81.refs_6_), channel_id=1, source_target_pairs={{0,8},{8,0},{16,24},{24,16},{1,9},{9,1},{17,25},{25,17},{2,10},{10... | collective-permute-start | bytes 393224 | tf_op jit(solution)/shard_map/ppermute | solution.py:152
  31.8 1.5 %collective-permute-start.23 = (bf16[256,256]{1,0:T(8,128)(2,1)S(1)}, bf16[256,256]{1,0:T(8,128)(2,1)S(1)}, u32[]{:S(2)}, u32[]{:S(2)}) collective-permute-start(bf16[256,256]{1,0:T(8,128)(2,1)S(1)} %get-tuple-element.82.refs_9_), channel_id=1, source_target_pairs={{0,16},{8,24},{16,0},{24,8},{1,17},{9,25},{17,1},{25,9},{2,18},{10... | collective-permute-start | bytes 393224 | tf_op jit(solution)/shard_map/ppermute | solution.py:152
  33.3 2.0 %collective-permute-start.17 = (bf16[256,256]{1,0:T(8,128)(2,1)S(1)}, bf16[256,256]{1,0:T(8,128)(2,1)S(1)}, u32[]{:S(2)}, u32[]{:S(2)}) collective-permute-start(bf16[256,256]{1,0:T(8,128)(2,1)S(1)} %get-tuple-element.73.refs_6_), channel_id=1, source_target_pairs={{0,8},{8,0},{16,24},{24,16},{1,9},{9,1},{17,25},{25,17},{2,10},{10... | collective-permute-start | bytes 393224 | tf_op jit(solution)/shard_map/ppermute | solution.py:152
  35.3 1.1 %collective-permute-done.22.refs_7_ = bf16[256,256]{1,0:T(8,128)(2,1)S(1)} collective-permute-done((bf16[256,256]{1,0:T(8,128)(2,1)S(1)}, bf16[256,256]{1,0:T(8,128)(2,1)S(1)}, u32[]{:S(2)}, u32[]{:S(2)}) %collective-permute-start.22) | collective-permute-done | bytes 131104 | tf_op jit(solution)/shard_map/ppermute | solution.py:152
  36.4 1.7 %collective-permute-start.18 = (bf16[256,256]{1,0:T(8,128)(2,1)S(1)}, bf16[256,256]{1,0:T(8,128)(2,1)S(1)}, u32[]{:S(2)}, u32[]{:S(2)}) collective-permute-start(bf16[256,256]{1,0:T(8,128)(2,1)S(1)} %get-tuple-element.74.refs_9_), channel_id=1, source_target_pairs={{0,16},{8,24},{16,0},{24,8},{1,17},{9,25},{17,1},{25,9},{2,18},{10... | collective-permute-start | bytes 393224 | tf_op jit(solution)/shard_map/ppermute | solution.py:152
  38.1 0.7 %term_part.3 = (f32[512,128]{1,0:T(8,128)S(1)}, bf16[512,128]{1,0:T(8,128)(2,1)S(1)}) custom-call(bf16[512,512]{1,0:T(8,128)(2,1)S(1)} %turned.1.refs_0_, bf16[512,512]{1,0:T(8,128)(2,1)S(1)} %collective-permute-done.12.refs_1_, bf16[512,512]{1,0:T(8,128)(2,1)S(1)} %collective-permute-done.13.refs_2_, bf16[512,512]{1,0:T(8,128)(2,1)S(1)} %collective-permute-done.14.refs_3_, ...), custom_call_target="tpu_custom_call" | custom-call | tf_op jit(solution)/shard_map/term_part/pallas_call | solution.py:163
  38.8 2.6 %collective-permute-start.24 = (bf16[512,128]{1,0:T(8,128)(2,1)S(1)}, bf16[512,128]{1,0:T(8,128)(2,1)S(1)}, u32[]{:S(2)}, u32[]{:S(2)}) collective-permute-start(bf16[512,128]{1,0:T(8,128)(2,1)S(1)} %get-tuple-element.71), channel_id=1, source_target_pairs={{0,4},{1,5},{2,6},{3,7},{4,0},{5,1},{6,2},{7,3},{8,12},{9,13},{10,... | collective-permute-start | bytes 393224 | tf_op jit(solution)/shard_map/ppermute | solution.py:152
  41.5 0.7 %term_part.2 = (f32[512,128]{1,0:T(8,128)S(1)}, bf16[512,128]{1,0:T(8,128)(2,1)S(1)}) custom-call(bf16[512,512]{1,0:T(8,128)(2,1)S(1)} %turned.1.refs_0_, bf16[512,512]{1,0:T(8,128)(2,1)S(1)} %collective-permute-done.12.refs_1_, bf16[512,512]{1,0:T(8,128)(2,1)S(1)} %collective-permute-done.13.refs_2_, bf16[512,512]{1,0:T(8,128)(2,1)S(1)} %collective-permute-done.14.refs_3_, ...), custom_call_target="tpu_custom_call" | custom-call | tf_op jit(solution)/shard_map/term_part/pallas_call | solution.py:163
  42.2 2.5 %collective-permute-start.19 = (bf16[512,128]{1,0:T(8,128)(2,1)S(1)}, bf16[512,128]{1,0:T(8,128)(2,1)S(1)}, u32[]{:S(2)}, u32[]{:S(2)}) collective-permute-start(bf16[512,128]{1,0:T(8,128)(2,1)S(1)} %get-tuple-element.65), channel_id=1, source_target_pairs={{0,4},{1,5},{2,6},{3,7},{4,0},{5,1},{6,2},{7,3},{8,12},{9,13},{10,... | collective-permute-start | bytes 393224 | tf_op jit(solution)/shard_map/ppermute | solution.py:152
  44.7 5.9 %collective-permute-done.24 = bf16[512,128]{1,0:T(8,128)(2,1)S(1)} collective-permute-done((bf16[512,128]{1,0:T(8,128)(2,1)S(1)}, bf16[512,128]{1,0:T(8,128)(2,1)S(1)}, u32[]{:S(2)}, u32[]{:S(2)}) %collective-permute-start.24) | collective-permute-done | bytes 131104 | tf_op jit(solution)/shard_map/ppermute | solution.py:152
  50.6 2.0 %collective-permute-done.19 = bf16[512,128]{1,0:T(8,128)(2,1)S(1)} collective-permute-done((bf16[512,128]{1,0:T(8,128)(2,1)S(1)}, bf16[512,128]{1,0:T(8,128)(2,1)S(1)}, u32[]{:S(2)}, u32[]{:S(2)}) %collective-permute-start.19) | collective-permute-done | bytes 131104 | tf_op jit(solution)/shard_map/ppermute | solution.py:152
  52.7 0.8 %pad_maximum_fusion = f32[512,256]{1,0:T(8,128)} fusion(f32[512,128]{1,0:T(8,128)S(1)} %convert_add_fusion, f32[512,128]{1,0:T(8,128)S(1)} %convert_add_fusion.1), kind=kLoop, calls=%fused_computation | loop fusion | flops 131072 | bytes 1048576 | tf_op jit(solution)/shard_map/concatenate | solution.py:364
  (38 shorter events, 0.7 us)
Async XLA Ops:
  0.6 5.7 %collective-permute-start = (bf16[128,2048]{1,0:T(8,128)(2,1)}, bf16[128,2048]{1,0:T(8,128)(2,1)S(1)}, u32[]{:S(2)}, u32[]{:S(2)}) collective-permute-start(bf16[128,2048]{1,0:T(8,128)(2,1)} %bitcast.9), channel_id=1, source_target_pairs={{0,1},{1,0},{2,3},{3,2},{4,5},{5,4},{6,7},{7,6},{8,9},{9,8},{10,11... | collective-permute-start | bytes 1572872 | tf_op jit(solution)/shard_map/ppermute | solution.py:152
  1.1 6.7 %collective-permute-start.1 = (bf16[128,2048]{1,0:T(8,128)(2,1)}, bf16[128,2048]{1,0:T(8,128)(2,1)S(1)}, u32[]{:S(2)}, u32[]{:S(2)}) collective-permute-start(bf16[128,2048]{1,0:T(8,128)(2,1)} %bitcast.11), channel_id=1, source_target_pairs={{0,1},{1,0},{2,3},{3,2},{4,5},{5,4},{6,7},{7,6},{8,9},{9,8},{10,11... | collective-permute-start | bytes 1572872 | tf_op jit(solution)/shard_map/ppermute | solution.py:152
  1.2 6.7 %collective-permute-start.3 = (bf16[128,2048]{1,0:T(8,128)(2,1)}, bf16[128,2048]{1,0:T(8,128)(2,1)S(1)}, u32[]{:S(2)}, u32[]{:S(2)}) collective-permute-start(bf16[128,2048]{1,0:T(8,128)(2,1)} %bitcast.13), channel_id=1, source_target_pairs={{0,1},{1,0},{2,3},{3,2},{4,5},{5,4},{6,7},{7,6},{8,9},{9,8},{10,11... | collective-permute-start | bytes 1572872 | tf_op jit(solution)/shard_map/ppermute | solution.py:152
  1.7 9.8 %collective-permute-start.2 = (bf16[128,2048]{1,0:T(8,128)(2,1)}, bf16[128,2048]{1,0:T(8,128)(2,1)S(1)}, u32[]{:S(2)}, u32[]{:S(2)}) collective-permute-start(bf16[128,2048]{1,0:T(8,128)(2,1)} %bitcast.15), channel_id=1, source_target_pairs={{0,1},{1,0},{2,3},{3,2},{4,5},{5,4},{6,7},{7,6},{8,9},{9,8},{10,11... | collective-permute-start | bytes 1572872 | tf_op jit(solution)/shard_map/ppermute | solution.py:152
  3.3 11.6 %collective-permute-start.8 = (bf16[128,512]{1,0:T(8,128)(2,1)S(1)}, bf16[128,512]{1,0:T(8,128)(2,1)S(1)}, u32[]{:S(2)}, u32[]{:S(2)}) collective-permute-start(bf16[128,512]{1,0:T(8,128)(2,1)S(1)} %get-tuple-element.52), channel_id=1, source_target_pairs={{0,8},{8,0},{16,24},{24,16},{1,9},{9,1},{17,25},{25,17},{2,10},{10... | collective-permute-start | bytes 393224 | tf_op jit(solution)/shard_map/ppermute | solution.py:152
  6.3 9.2 %collective-permute-start.9 = (bf16[128,512]{1,0:T(8,128)(2,1)S(1)}, bf16[128,512]{1,0:T(8,128)(2,1)S(1)}, u32[]{:S(2)}, u32[]{:S(2)}) collective-permute-start(bf16[128,512]{1,0:T(8,128)(2,1)S(1)} %get-tuple-element.53), channel_id=1, source_target_pairs={{0,16},{8,24},{16,0},{24,8},{1,17},{9,25},{17,1},{25,9},{2,18},{10... | collective-permute-start | bytes 393224 | tf_op jit(solution)/shard_map/ppermute | solution.py:152
  7.8 7.7 %collective-permute-start.10 = (bf16[128,512]{1,0:T(8,128)(2,1)S(1)}, bf16[128,512]{1,0:T(8,128)(2,1)S(1)}, u32[]{:S(2)}, u32[]{:S(2)}) collective-permute-start(bf16[128,512]{1,0:T(8,128)(2,1)S(1)} %get-tuple-element.54), channel_id=1, source_target_pairs={{0,24},{8,16},{16,8},{24,0},{1,25},{9,17},{17,9},{25,1},{2,26},{10... | collective-permute-start | bytes 393224 | tf_op jit(solution)/shard_map/ppermute | solution.py:152
  9.4 7.8 %collective-permute-start.11 = (bf16[256,512]{1,0:T(8,128)(2,1)S(1)}, bf16[256,512]{1,0:T(8,128)(2,1)S(1)}, u32[]{:S(2)}, u32[]{:S(2)}) collective-permute-start(bf16[256,512]{1,0:T(8,128)(2,1)S(1)} %get-tuple-element.45), channel_id=1, source_target_pairs={{0,2},{1,3},{2,0},{3,1},{4,6},{5,7},{6,4},{7,5},{8,10},{9,11},{10,... | collective-permute-start | bytes 786440 | tf_op jit(solution)/shard_map/ppermute | solution.py:152
  14.8 7.5 %collective-permute-start.4 = (bf16[128,1024]{1,0:T(8,128)(2,1)S(1)}, bf16[128,1024]{1,0:T(8,128)(2,1)S(1)}, u32[]{:S(2)}, u32[]{:S(2)}) collective-permute-start(bf16[128,1024]{1,0:T(8,128)(2,1)S(1)} %get-tuple-element.46), channel_id=1, source_target_pairs={{0,1},{1,0},{2,3},{3,2},{4,5},{5,4},{6,7},{7,6},{8,9},{9,8},{10,11... | collective-permute-start | bytes 786440 | tf_op jit(solution)/shard_map/ppermute | solution.py:152
  14.9 7.5 %collective-permute-start.5 = (bf16[128,1024]{1,0:T(8,128)(2,1)S(1)}, bf16[128,1024]{1,0:T(8,128)(2,1)S(1)}, u32[]{:S(2)}, u32[]{:S(2)}) collective-permute-start(bf16[128,1024]{1,0:T(8,128)(2,1)S(1)} %get-tuple-element.47), channel_id=1, source_target_pairs={{0,1},{1,0},{2,3},{3,2},{4,5},{5,4},{6,7},{7,6},{8,9},{9,8},{10,11... | collective-permute-start | bytes 786440 | tf_op jit(solution)/shard_map/ppermute | solution.py:152
  15.5 3.7 %collective-permute-start.6 = (bf16[128,512]{1,0:T(8,128)(2,1)S(1)}, bf16[128,512]{1,0:T(8,128)(2,1)S(1)}, u32[]{:S(2)}, u32[]{:S(2)}) collective-permute-start(bf16[128,512]{1,0:T(8,128)(2,1)S(1)} %get-tuple-element.86), channel_id=1, source_target_pairs={{0,1},{1,0},{2,3},{3,2},{4,5},{5,4},{6,7},{7,6},{8,9},{9,8},{10,11... | collective-permute-start | bytes 393224 | tf_op jit(solution)/shard_map/ppermute | solution.py:152
  15.6 5.2 %collective-permute-start.7 = (bf16[128,512]{1,0:T(8,128)(2,1)S(1)}, bf16[128,512]{1,0:T(8,128)(2,1)S(1)}, u32[]{:S(2)}, u32[]{:S(2)}) collective-permute-start(bf16[128,512]{1,0:T(8,128)(2,1)S(1)} %get-tuple-element.84), channel_id=1, source_target_pairs={{0,1},{1,0},{2,3},{3,2},{4,5},{5,4},{6,7},{7,6},{8,9},{9,8},{10,11... | collective-permute-start | bytes 393224 | tf_op jit(solution)/shard_map/ppermute | solution.py:152
  17.4 12.8 %collective-permute-start.13 = (bf16[512,512]{1,0:T(8,128)(2,1)S(1)}, bf16[512,512]{1,0:T(8,128)(2,1)S(1)}, u32[]{:S(2)}, u32[]{:S(2)}) collective-permute-start(bf16[512,512]{1,0:T(8,128)(2,1)S(1)} %turned.1.refs_0_), channel_id=1, source_target_pairs={{0,2},{1,3},{2,0},{3,1},{4,6},{5,7},{6,4},{7,5},{8,10},{9,11},{10,... | collective-permute-start | bytes 1572872 | tf_op jit(solution)/shard_map/ppermute | solution.py:152
  19.2 6.5 %collective-permute-start.20 = (bf16[512,256]{1,0:T(8,128)(2,1)S(1)}, bf16[512,256]{1,0:T(8,128)(2,1)S(1)}, u32[]{:S(2)}, u32[]{:S(2)}) collective-permute-start(bf16[512,256]{1,0:T(8,128)(2,1)S(1)} %pad_maximum_fusion.2), channel_id=1, source_target_pairs={{0,8},{8,0},{16,24},{24,16},{1,9},{9,1},{17,25},{25,17},{2,10},{10... | collective-permute-start | bytes 786440 | tf_op jit(solution)/shard_map/ppermute | solution.py:152
  20.8 7.6 %collective-permute-start.21 = (bf16[512,256]{1,0:T(8,128)(2,1)S(1)}, bf16[512,256]{1,0:T(8,128)(2,1)S(1)}, u32[]{:S(2)}, u32[]{:S(2)}) collective-permute-start(bf16[512,256]{1,0:T(8,128)(2,1)S(1)} %pad_maximum_fusion.2), channel_id=1, source_target_pairs={{0,16},{8,24},{16,0},{24,8},{1,17},{9,25},{17,1},{25,9},{2,18},{10... | collective-permute-start | bytes 786440 | tf_op jit(solution)/shard_map/ppermute | solution.py:152
  22.3 15.8 %collective-permute-start.12 = (bf16[512,512]{1,0:T(8,128)(2,1)S(1)}, bf16[512,512]{1,0:T(8,128)(2,1)S(1)}, u32[]{:S(2)}, u32[]{:S(2)}) collective-permute-start(bf16[512,512]{1,0:T(8,128)(2,1)S(1)} %turned.1.refs_0_), channel_id=1, source_target_pairs={{0,1},{1,0},{2,3},{3,2},{4,5},{5,4},{6,7},{7,6},{8,9},{9,8},{10,11... | collective-permute-start | bytes 1572872 | tf_op jit(solution)/shard_map/ppermute | solution.py:152
  22.4 9.3 %collective-permute-start.15 = (bf16[512,256]{1,0:T(8,128)(2,1)S(1)}, bf16[512,256]{1,0:T(8,128)(2,1)S(1)}, u32[]{:S(2)}, u32[]{:S(2)}) collective-permute-start(bf16[512,256]{1,0:T(8,128)(2,1)S(1)} %pad_maximum_fusion.1), channel_id=1, source_target_pairs={{0,8},{8,0},{16,24},{24,16},{1,9},{9,1},{17,25},{25,17},{2,10},{10... | collective-permute-start | bytes 786440 | tf_op jit(solution)/shard_map/ppermute | solution.py:152
  25.7 7.6 %collective-permute-start.16 = (bf16[512,256]{1,0:T(8,128)(2,1)S(1)}, bf16[512,256]{1,0:T(8,128)(2,1)S(1)}, u32[]{:S(2)}, u32[]{:S(2)}) collective-permute-start(bf16[512,256]{1,0:T(8,128)(2,1)S(1)} %pad_maximum_fusion.1), channel_id=1, source_target_pairs={{0,16},{8,24},{16,0},{24,8},{1,17},{9,25},{17,1},{25,9},{2,18},{10... | collective-permute-start | bytes 786440 | tf_op jit(solution)/shard_map/ppermute | solution.py:152
  30.2 7.9 %collective-permute-start.14 = (bf16[512,512]{1,0:T(8,128)(2,1)S(1)}, bf16[512,512]{1,0:T(8,128)(2,1)S(1)}, u32[]{:S(2)}, u32[]{:S(2)}) collective-permute-start(bf16[512,512]{1,0:T(8,128)(2,1)S(1)} %collective-permute-done.13.refs_2_), channel_id=1, source_target_pairs={{0,1},{1,0},{2,3},{3,2},{4,5},{5,4},{6,7},{7,6},{8,9},{9,8},{10,11... | collective-permute-start | bytes 1572872 | tf_op jit(solution)/shard_map/ppermute | solution.py:152
  30.2 6.2 %collective-permute-start.22 = (bf16[256,256]{1,0:T(8,128)(2,1)S(1)}, bf16[256,256]{1,0:T(8,128)(2,1)S(1)}, u32[]{:S(2)}, u32[]{:S(2)}) collective-permute-start(bf16[256,256]{1,0:T(8,128)(2,1)S(1)} %get-tuple-element.81.refs_6_), channel_id=1, source_target_pairs={{0,8},{8,0},{16,24},{24,16},{1,9},{9,1},{17,25},{25,17},{2,10},{10... | collective-permute-start | bytes 393224 | tf_op jit(solution)/shard_map/ppermute | solution.py:152
  31.8 6.3 %collective-permute-start.23 = (bf16[256,256]{1,0:T(8,128)(2,1)S(1)}, bf16[256,256]{1,0:T(8,128)(2,1)S(1)}, u32[]{:S(2)}, u32[]{:S(2)}) collective-permute-start(bf16[256,256]{1,0:T(8,128)(2,1)S(1)} %get-tuple-element.82.refs_9_), channel_id=1, source_target_pairs={{0,16},{8,24},{16,0},{24,8},{1,17},{9,25},{17,1},{25,9},{2,18},{10... | collective-permute-start | bytes 393224 | tf_op jit(solution)/shard_map/ppermute | solution.py:152
  33.3 8.2 %collective-permute-start.17 = (bf16[256,256]{1,0:T(8,128)(2,1)S(1)}, bf16[256,256]{1,0:T(8,128)(2,1)S(1)}, u32[]{:S(2)}, u32[]{:S(2)}) collective-permute-start(bf16[256,256]{1,0:T(8,128)(2,1)S(1)} %get-tuple-element.73.refs_6_), channel_id=1, source_target_pairs={{0,8},{8,0},{16,24},{24,16},{1,9},{9,1},{17,25},{25,17},{2,10},{10... | collective-permute-start | bytes 393224 | tf_op jit(solution)/shard_map/ppermute | solution.py:152
  36.4 5.1 %collective-permute-start.18 = (bf16[256,256]{1,0:T(8,128)(2,1)S(1)}, bf16[256,256]{1,0:T(8,128)(2,1)S(1)}, u32[]{:S(2)}, u32[]{:S(2)}) collective-permute-start(bf16[256,256]{1,0:T(8,128)(2,1)S(1)} %get-tuple-element.74.refs_9_), channel_id=1, source_target_pairs={{0,16},{8,24},{16,0},{24,8},{1,17},{9,25},{17,1},{25,9},{2,18},{10... | collective-permute-start | bytes 393224 | tf_op jit(solution)/shard_map/ppermute | solution.py:152
  38.8 11.8 %collective-permute-start.24 = (bf16[512,128]{1,0:T(8,128)(2,1)S(1)}, bf16[512,128]{1,0:T(8,128)(2,1)S(1)}, u32[]{:S(2)}, u32[]{:S(2)}) collective-permute-start(bf16[512,128]{1,0:T(8,128)(2,1)S(1)} %get-tuple-element.71), channel_id=1, source_target_pairs={{0,4},{1,5},{2,6},{3,7},{4,0},{5,1},{6,2},{7,3},{8,12},{9,13},{10,... | collective-permute-start | bytes 393224 | tf_op jit(solution)/shard_map/ppermute | solution.py:152
  42.2 10.5 %collective-permute-start.19 = (bf16[512,128]{1,0:T(8,128)(2,1)S(1)}, bf16[512,128]{1,0:T(8,128)(2,1)S(1)}, u32[]{:S(2)}, u32[]{:S(2)}) collective-permute-start(bf16[512,128]{1,0:T(8,128)(2,1)S(1)} %get-tuple-element.65), channel_id=1, source_target_pairs={{0,4},{1,5},{2,6},{3,7},{4,0},{5,1},{6,2},{7,3},{8,12},{9,13},{10,... | collective-permute-start | bytes 393224 | tf_op jit(solution)/shard_map/ppermute | solution.py:152

commit v4 on v3

--- a/solution.py
+++ b/solution.py
@@ -179,11 +179,12 @@
 
 def both(mine, theirs, group, core, head):
     packed, spread = columns(2 * group + head), columns(4 * group + 2 * core + head)
-    return jnp.concatenate([mine[:, packed], theirs[:, spread]], axis=0)
+    own = packed if mine.shape[1] < theirs.shape[1] else spread
+    return jnp.concatenate([mine[:, own], theirs[:, spread]], axis=0)
 
 
 def packed_inputs(arrays, inputs):
-    half, width = arrays[0].shape
+    half, width = inputs.shape
     block = inputs.shape[1] // 4
     count = len(arrays)
     groups = width // (4 * HD)
@@ -228,19 +229,43 @@
     return weights * (1.0 / jnp.sum(weights, axis=0, keepdims=True))
 
 
+def causal_probs(queries, keys, before):
+    scores = dot(keys, queries, ((1,), (1,))) * HD ** (-0.5)
+    key_pos = lax.broadcasted_iota(jnp.int32, scores.shape, 0)
+    query_pos = lax.broadcasted_iota(jnp.int32, scores.shape, 1) + before
+    scores = jnp.where(key_pos <= query_pos, scores, -jnp.inf)
+    weights = jnp.exp(scores - jnp.max(scores, axis=0, keepdims=True))
+    probs = weights * (1.0 / jnp.sum(weights, axis=0, keepdims=True))
+    return probs.astype(jnp.bfloat16)
+
+
 def value_part(q, k, g):
     half, width = q[1].shape
     order = (0, 2, 1, 3)
 
-    def kernel(q0, q1, k0, k1, g0, g1, kept, given):
-        core, chip = lax.axis_index("seq") % 2, lax.axis_index("seq") // 2
+    def run(core, chip, q0, q1, k0, k1, g0, g1, kept, given):
         for at, apart in enumerate(order):
             for head in range(2):
-                where = chip ^ apart, core, head
-                probs = probs_by_key(core, both(q0, q1, *where), both(k0, k1, *where))
-                grad = dot(probs.astype(jnp.bfloat16), both(g0, g1, *where), ((1,), (0,)))
-                here = (2 * head + at % 2) * HD
-                (kept, given)[at // 2][:, here : here + HD] = grad.astype(jnp.bfloat16)
+                group = chip ^ apart
+                packed, spread = columns(2 * group + head), columns(4 * group + 2 * core + head)
+                mine = [ref[:, packed if ref.shape[1] < width else spread] for ref in (q0, k0, g0)]
+                theirs = [ref[:, spread] for ref in (q1, k1, g1)]
+                low, high = (theirs, mine) if core else (mine, theirs)
+                late = causal_probs(high[0], jnp.concatenate([low[1], high[1]], axis=0), half)
+                early = causal_probs(low[0], low[1], 0)
+                both_grads = dot(late, high[2], ((1,), (0,)))
+                low_grad = both_grads[:half] + dot(early, low[2], ((1,), (0,)))
+                here = slice((2 * head + at % 2) * HD, (2 * head + at % 2 + 1) * HD)
+                out = (kept, given)[at // 2]
+                out[core * half : (core + 1) * half, here] = low_grad.astype(jnp.bfloat16)
+                out[(1 - core) * half : (2 - core) * half, here] = both_grads[half:].astype(
+                    jnp.bfloat16
+                )
+
+    def kernel(*refs):
+        chip = lax.axis_index("seq") // 2
+        for core in range(2):
+            pl.when(lax.axis_index("seq") % 2 == core)(lambda core=core: run(core, chip, *refs))
 
     out = pltpu.VMEM((2 * half, width // 4), jnp.bfloat16)
     return local_call(kernel, "value_part", [out] * 2)(*q, *k, *g)
@@ -333,8 +358,9 @@
 def chip_body(queries, key_vectors, values, out_grad, inputs):
     half = queries.shape[1]
     arrays = [a[0] for a in (queries, key_vectors, out_grad, values)]
-    *own, x_here, x_1, x_2, x_3 = packed_inputs(arrays, inputs[0])
-    q, k, g, v = ((mine, swap(a, "seq", 1)) for mine, a in zip(own, arrays))
+    *packed, x_here, x_1, x_2, x_3 = packed_inputs([arrays[i] for i in (2,)], inputs[0])
+    own = dict(zip((2,), packed))
+    q, k, g, v = ((own.get(i, a), swap(a, "seq", 1)) for i, a in enumerate(arrays))
     x_mine = [x_here, swap(x_1, "dp", 1), swap(x_2, "dp", 2), swap(x_3, "dp", 3)]
 
     kept, given = value_part(q, k, g)
@@ -347,9 +373,9 @@
         here = slice(2 * head * HD, 2 * (head + 1) * HD)
         paired = jnp.concatenate([kept[:, here], got[:, here]], axis=0)
         by_x, by_y = after([swap(paired, "dp", 1), swap(paired, "dp", 2)])
-        first, second = after([swap(by_y[: 2 * half], "dp", 1), swap(by_x[2 * half :], "dp", 2)])
-        near = [paired[: 2 * half], by_x[: 2 * half], by_y[: 2 * half], first]
-        far = [paired[2 * half :], by_x[2 * half :], by_y[2 * half :], second]
+        cross = swap(by_x, "dp", 2) if head else swap(by_y, "dp", 1)
+        near = [paired[: 2 * half], by_x[: 2 * half], by_y[: 2 * half], cross[: 2 * half]]
+        far = [paired[2 * half :], by_x[2 * half :], by_y[2 * half :], cross[2 * half :]]
         sides.append((near, far))
 
     x_mine = after(x_mine, got, q_theirs)

time: 53.7 us -> 53.6 us (level)
  waiting for transfers between devices: 13.2 us -> 22.3 us
  starting transfers between devices: 28.9 us -> 20 us
    ppermute x25 -> x23, waiting for transfers between devices: 13.2 us -> 22.3 us  [swap(): lax.ppermute(value, axis, [(i, i ^ bit) for i in range(lax.axis_size(axis...]
    ppermute x25 -> x23, starting transfers between devices: 28.9 us -> 20 us  [swap(): lax.ppermute(value, axis, [(i, i ^ bit) for i in range(lax.axis_size(axis...]
  transfers between devices with their start and end apart: 25 -> 23, of which waited for: 6 -> 8; matrix products, arithmetic and copies ran while one was open for 0% -> 0% of each run, Pallas kernels for 18% -> 17%
where the time goes in v4:
time: 53.6 us; the launch traced here: 53.5 us
  waiting for transfers between devices  22.3 us (42%)
  starting transfers between devices  20 us (37%)
  Pallas kernels  9.2 us (17%)
  other arithmetic  0.91 us (2%)
  between operations  0.83 us (2%)
    ppermute x23, waiting for transfers between devices, swap(): lax.ppermute(value, axis, [(i, i ^ bit) for i in range(lax.axis_size(axis...  22.3 us
    ppermute x23, starting transfers between devices, swap(): lax.ppermute(value, axis, [(i, i ^ bit) for i in range(lax.axis_size(axis...  20 us
    pallas_call x6, Pallas kernels, call(): pl.pallas_call(kernel, in_specs=[in_vmem] * len(operands), out_specs=[in_...  7.89 us
    pallas_call x1, Pallas kernels, packed_inputs(): pl.pallas_call(kernel, in_specs=[pl.BlockSpec(memory_space=pl.ANY)] * (co...  1.31 us
  transfers between devices with their start and end apart: 23, of which 8 were waited for; matrix products, arithmetic and copies ran while one was open for 0% of the time, Pallas kernels for 17%

profile of v4, /device:TPU:0, one launch (start us, length us, event | category | flops | bytes accessed | tf_op | source)
XLA Modules:
  0.0 53.5 jit_solution(12403152355460445613)
XLA Ops:
  0.6 0.5 collective-permute-start
  1.2 0.4 collective-permute-start.3
  1.7 1.3 %packed_inputs.1 = (bf16[128,1024]{1,0:T(8,128)(2,1)S(1)}, bf16[128,512]{1,0:T(8,128)(2,1)S(1)}, bf16[128,512]{1,0:T(8,128)(2,1)S(1)}, bf16[128,512]{1,0:T(8,128)(2,1)S(1)}, bf16[128,512]{1,0:T(8,128)(2,1)S(1)}) custom-call(bf16[128,2048]{1,0:T(8,128)(2,1)} %bitcast.18, bf16[128,2048]{1,0:T(8,128)(2,1)} %bitcast.16), custom_call_target="tpu_custom_call" | custom-call | tf_op jit(solution)/shard_map/packed_inputs/pallas_call | solution.py:210
  3.1 3.0 %collective-permute-start.8 = (bf16[128,512]{1,0:T(8,128)(2,1)S(1)}, bf16[128,512]{1,0:T(8,128)(2,1)S(1)}, u32[]{:S(2)}, u32[]{:S(2)}) collective-permute-start(bf16[128,512]{1,0:T(8,128)(2,1)S(1)} %get-tuple-element.42), channel_id=1, source_target_pairs={{0,8},{8,0},{16,24},{24,16},{1,9},{9,1},{17,25},{25,17},{2,10},{10... | collective-permute-start | bytes 393224 | tf_op jit(solution)/shard_map/ppermute | solution.py:152
  6.1 1.5 %collective-permute-start.9 = (bf16[128,512]{1,0:T(8,128)(2,1)S(1)}, bf16[128,512]{1,0:T(8,128)(2,1)S(1)}, u32[]{:S(2)}, u32[]{:S(2)}) collective-permute-start(bf16[128,512]{1,0:T(8,128)(2,1)S(1)} %get-tuple-element.43), channel_id=1, source_target_pairs={{0,16},{8,24},{16,0},{24,8},{1,17},{9,25},{17,1},{25,9},{2,18},{10... | collective-permute-start | bytes 393224 | tf_op jit(solution)/shard_map/ppermute | solution.py:152
  7.6 1.5 %value_part.1 = (bf16[256,512]{1,0:T(8,128)(2,1)S(1)}, bf16[256,512]{1,0:T(8,128)(2,1)S(1)}) custom-call(bf16[128,2048]{1,0:T(8,128)(2,1)S(1)} %bitcast.9, bf16[128,2048]{1,0:T(8,128)(2,1)S(1)} %collective-permute-done.q1.refs_1_, bf16[128,2048]{1,0:T(8,128)(2,1)S(1)} %bitcast.12, bf16[128,2048]{1,0:T(8,128)(2,1)S(1)} %collective-permute-done.1.k1.refs_3_, ...), custom_call_target="tpu_custom_call" | custom-call | tf_op jit(solution)/shard_map/value_part/pallas_call | solution.py:163
  9.1 2.1 %collective-permute-start.11 = (bf16[256,512]{1,0:T(8,128)(2,1)S(1)}, bf16[256,512]{1,0:T(8,128)(2,1)S(1)}, u32[]{:S(2)}, u32[]{:S(2)}) collective-permute-start(bf16[256,512]{1,0:T(8,128)(2,1)S(1)} %get-tuple-element.35), channel_id=1, source_target_pairs={{0,2},{1,3},{2,0},{3,1},{4,6},{5,7},{6,4},{7,5},{8,10},{9,11},{10,... | collective-permute-start | bytes 786440 | tf_op jit(solution)/shard_map/ppermute | solution.py:152
  11.3 3.3 %score_part.1 = (bf16[128,1024]{1,0:T(8,128)(2,1)S(1)}, bf16[128,1024]{1,0:T(8,128)(2,1)S(1)}, bf16[128,1024]{1,0:T(8,128)(2,1)S(1)}, bf16[128,1024]{1,0:T(8,128)(2,1)S(1)}) custom-call(bf16[128,2048]{1,0:T(8,128)(2,1)S(1)} %bitcast.10, bf16[128,2048]{1,0:T(8,128)(2,1)S(1)} %collective-permute-done.q1.refs_1_, bf16[128,2048]{1,0:T(8,128)(2,1)S(1)} %bitcast.13, ...), custom_call_target="tpu_custom_call" | custom-call | tf_op jit(solution)/shard_map/score_part/pallas_call | solution.py:163
  14.7 0.6 %collective-permute-start.5 = (bf16[128,1024]{1,0:T(8,128)(2,1)S(1)}, bf16[128,1024]{1,0:T(8,128)(2,1)S(1)}, u32[]{:S(2)}, u32[]{:S(2)}) collective-permute-start(bf16[128,1024]{1,0:T(8,128)(2,1)S(1)} %get-tuple-element.37), channel_id=1, source_target_pairs={{0,1},{1,0},{2,3},{3,2},{4,5},{5,4},{6,7},{7,6},{8,9},{9,8},{10,11... | collective-permute-start | bytes 786440 | tf_op jit(solution)/shard_map/ppermute | solution.py:152
  15.3 0.1 collective-permute-start.6
  15.3 0.4 collective-permute-start.7
  15.8 1.3 %collective-permute-done.11 = bf16[256,512]{1,0:T(8,128)(2,1)S(1)} collective-permute-done((bf16[256,512]{1,0:T(8,128)(2,1)S(1)}, bf16[256,512]{1,0:T(8,128)(2,1)S(1)}, u32[]{:S(2)}, u32[]{:S(2)}) %collective-permute-start.11) | collective-permute-done | bytes 262176 | tf_op jit(solution)/shard_map/ppermute | solution.py:152
  17.1 0.2 turned.1.refs_0_
  17.3 1.6 %collective-permute-start.13 = (bf16[512,512]{1,0:T(8,128)(2,1)S(1)}, bf16[512,512]{1,0:T(8,128)(2,1)S(1)}, u32[]{:S(2)}, u32[]{:S(2)}) collective-permute-start(bf16[512,512]{1,0:T(8,128)(2,1)S(1)} %turned.1.refs_0_), channel_id=1, source_target_pairs={{0,2},{1,3},{2,0},{3,1},{4,6},{5,7},{6,4},{7,5},{8,10},{9,11},{10,... | collective-permute-start | bytes 1572872 | tf_op jit(solution)/shard_map/ppermute | solution.py:152
  19.0 1.5 %collective-permute-start.19 = (bf16[512,256]{1,0:T(8,128)(2,1)S(1)}, bf16[512,256]{1,0:T(8,128)(2,1)S(1)}, u32[]{:S(2)}, u32[]{:S(2)}) collective-permute-start(bf16[512,256]{1,0:T(8,128)(2,1)S(1)} %pad_maximum_fusion.2), channel_id=1, source_target_pairs={{0,8},{8,0},{16,24},{24,16},{1,9},{9,1},{17,25},{25,17},{2,10},{10... | collective-permute-start | bytes 786440 | tf_op jit(solution)/shard_map/ppermute | solution.py:152
  20.5 1.5 %collective-permute-start.20 = (bf16[512,256]{1,0:T(8,128)(2,1)S(1)}, bf16[512,256]{1,0:T(8,128)(2,1)S(1)}, u32[]{:S(2)}, u32[]{:S(2)}) collective-permute-start(bf16[512,256]{1,0:T(8,128)(2,1)S(1)} %pad_maximum_fusion.2), channel_id=1, source_target_pairs={{0,16},{8,24},{16,0},{24,8},{1,17},{9,25},{17,1},{25,9},{2,18},{10... | collective-permute-start | bytes 786440 | tf_op jit(solution)/shard_map/ppermute | solution.py:152
  22.1 0.6 %collective-permute-start.15 = (bf16[512,256]{1,0:T(8,128)(2,1)S(1)}, bf16[512,256]{1,0:T(8,128)(2,1)S(1)}, u32[]{:S(2)}, u32[]{:S(2)}) collective-permute-start(bf16[512,256]{1,0:T(8,128)(2,1)S(1)} %pad_maximum_fusion.1), channel_id=1, source_target_pairs={{0,8},{8,0},{16,24},{24,16},{1,9},{9,1},{17,25},{25,17},{2,10},{10... | collective-permute-start | bytes 786440 | tf_op jit(solution)/shard_map/ppermute | solution.py:152
  22.7 0.5 collective-permute-start.16
  23.2 1.5 %joined.1 = (bf16[128,2048]{1,0:T(8,128)(2,1)}, bf16[128,2048]{1,0:T(8,128)(2,1)}, bf16[128,2048]{1,0:T(8,128)(2,1)}) custom-call(bf16[128,1024]{1,0:T(8,128)(2,1)S(1)} %get-tuple-element.32.refs_0_, bf16[128,1024]{1,0:T(8,128)(2,1)S(1)} %get-tuple-element.33.refs_1_, bf16[128,512]{1,0:T(8,128)(2,1)S(1)} %get-tuple-element.77.refs_2_, ...), custom_call_target="tpu_custom_call" | custom-call | tf_op jit(solution)/shard_map/joined/pallas_call | solution.py:163
  24.7 3.4 %collective-permute-done.19 = bf16[512,256]{1,0:T(8,128)(2,1)S(1)} collective-permute-done((bf16[512,256]{1,0:T(8,128)(2,1)S(1)}, bf16[512,256]{1,0:T(8,128)(2,1)S(1)}, u32[]{:S(2)}, u32[]{:S(2)}) %collective-permute-start.19) | collective-permute-done | bytes 262176 | tf_op jit(solution)/shard_map/ppermute | solution.py:152
  28.1 1.2 %collective-permute-done.20 = bf16[512,256]{1,0:T(8,128)(2,1)S(1)} collective-permute-done((bf16[512,256]{1,0:T(8,128)(2,1)S(1)}, bf16[512,256]{1,0:T(8,128)(2,1)S(1)}, u32[]{:S(2)}, u32[]{:S(2)}) %collective-permute-start.20) | collective-permute-done | bytes 262176 | tf_op jit(solution)/shard_map/ppermute | solution.py:152
  29.3 1.5 %collective-permute-start.21 = (bf16[512,256]{1,0:T(8,128)(2,1)S(1)}, bf16[512,256]{1,0:T(8,128)(2,1)S(1)}, u32[]{:S(2)}, u32[]{:S(2)}) collective-permute-start(bf16[512,256]{1,0:T(8,128)(2,1)S(1)} %collective-permute-done.19), channel_id=1, source_target_pairs={{0,16},{8,24},{16,0},{24,8},{1,17},{9,25},{17,1},{25,9},{2,18},{10... | collective-permute-start | bytes 786440 | tf_op jit(solution)/shard_map/ppermute | solution.py:152
  30.9 0.1 collective-permute-done.15
  30.9 1.9 %collective-permute-done.16 = bf16[512,256]{1,0:T(8,128)(2,1)S(1)} collective-permute-done((bf16[512,256]{1,0:T(8,128)(2,1)S(1)}, bf16[512,256]{1,0:T(8,128)(2,1)S(1)}, u32[]{:S(2)}, u32[]{:S(2)}) %collective-permute-start.16) | collective-permute-done | bytes 262176 | tf_op jit(solution)/shard_map/ppermute | solution.py:152
  32.9 4.8 %collective-permute-done.21 = bf16[512,256]{1,0:T(8,128)(2,1)S(1)} collective-permute-done((bf16[512,256]{1,0:T(8,128)(2,1)S(1)}, bf16[512,256]{1,0:T(8,128)(2,1)S(1)}, u32[]{:S(2)}, u32[]{:S(2)}) %collective-permute-start.21) | collective-permute-done | bytes 262176 | tf_op jit(solution)/shard_map/ppermute | solution.py:152
  37.8 0.7 %term_part.3 = (f32[512,128]{1,0:T(8,128)S(1)}, bf16[512,128]{1,0:T(8,128)(2,1)S(1)}) custom-call(bf16[512,512]{1,0:T(8,128)(2,1)S(1)} %turned.1.refs_0_, bf16[512,512]{1,0:T(8,128)(2,1)S(1)} %collective-permute-done.12.refs_1_, bf16[512,512]{1,0:T(8,128)(2,1)S(1)} %collective-permute-done.13.refs_2_, bf16[512,512]{1,0:T(8,128)(2,1)S(1)} %collective-permute-done.14.refs_3_, ...), custom_call_target="tpu_custom_call" | custom-call | tf_op jit(solution)/shard_map/term_part/pallas_call | solution.py:163
  38.5 2.7 %collective-permute-start.22 = (bf16[512,128]{1,0:T(8,128)(2,1)S(1)}, bf16[512,128]{1,0:T(8,128)(2,1)S(1)}, u32[]{:S(2)}, u32[]{:S(2)}) collective-permute-start(bf16[512,128]{1,0:T(8,128)(2,1)S(1)} %get-tuple-element.57), channel_id=1, source_target_pairs={{0,4},{1,5},{2,6},{3,7},{4,0},{5,1},{6,2},{7,3},{8,12},{9,13},{10,... | collective-permute-start | bytes 393224 | tf_op jit(solution)/shard_map/ppermute | solution.py:152
  41.2 0.7 %term_part.2 = (f32[512,128]{1,0:T(8,128)S(1)}, bf16[512,128]{1,0:T(8,128)(2,1)S(1)}) custom-call(bf16[512,512]{1,0:T(8,128)(2,1)S(1)} %turned.1.refs_0_, bf16[512,512]{1,0:T(8,128)(2,1)S(1)} %collective-permute-done.12.refs_1_, bf16[512,512]{1,0:T(8,128)(2,1)S(1)} %collective-permute-done.13.refs_2_, bf16[512,512]{1,0:T(8,128)(2,1)S(1)} %collective-permute-done.14.refs_3_, ...), custom_call_target="tpu_custom_call" | custom-call | tf_op jit(solution)/shard_map/term_part/pallas_call | solution.py:163
  41.9 1.2 %collective-permute-start.18 = (bf16[512,128]{1,0:T(8,128)(2,1)S(1)}, bf16[512,128]{1,0:T(8,128)(2,1)S(1)}, u32[]{:S(2)}, u32[]{:S(2)}) collective-permute-start(bf16[512,128]{1,0:T(8,128)(2,1)S(1)} %get-tuple-element.53), channel_id=1, source_target_pairs={{0,4},{1,5},{2,6},{3,7},{4,0},{5,1},{6,2},{7,3},{8,12},{9,13},{10,... | collective-permute-start | bytes 393224 | tf_op jit(solution)/shard_map/ppermute | solution.py:152
  43.1 7.0 %collective-permute-done.22 = bf16[512,128]{1,0:T(8,128)(2,1)S(1)} collective-permute-done((bf16[512,128]{1,0:T(8,128)(2,1)S(1)}, bf16[512,128]{1,0:T(8,128)(2,1)S(1)}, u32[]{:S(2)}, u32[]{:S(2)}) %collective-permute-start.22) | collective-permute-done | bytes 131104 | tf_op jit(solution)/shard_map/ppermute | solution.py:152
  50.1 2.5 %collective-permute-done.18 = bf16[512,128]{1,0:T(8,128)(2,1)S(1)} collective-permute-done((bf16[512,128]{1,0:T(8,128)(2,1)S(1)}, bf16[512,128]{1,0:T(8,128)(2,1)S(1)}, u32[]{:S(2)}, u32[]{:S(2)}) %collective-permute-start.18) | collective-permute-done | bytes 131104 | tf_op jit(solution)/shard_map/ppermute | solution.py:152
  52.6 0.8 %pad_maximum_fusion = f32[512,256]{1,0:T(8,128)} fusion(f32[512,128]{1,0:T(8,128)S(1)} %convert_add_fusion, f32[512,128]{1,0:T(8,128)S(1)} %convert_add_fusion.1), kind=kLoop, calls=%fused_computation | loop fusion | flops 131072 | bytes 1048576 | tf_op jit(solution)/shard_map/concatenate | solution.py:390
  (40 shorter events, 0.6 us)
Async XLA Ops:
  0.6 5.4 %collective-permute-start = (bf16[128,2048]{1,0:T(8,128)(2,1)}, bf16[128,2048]{1,0:T(8,128)(2,1)S(1)}, u32[]{:S(2)}, u32[]{:S(2)}) collective-permute-start(bf16[128,2048]{1,0:T(8,128)(2,1)} %bitcast.8), channel_id=1, source_target_pairs={{0,1},{1,0},{2,3},{3,2},{4,5},{5,4},{6,7},{7,6},{8,9},{9,8},{10,11... | collective-permute-start | bytes 1572872 | tf_op jit(solution)/shard_map/ppermute | solution.py:152
  1.1 6.4 %collective-permute-start.1 = (bf16[128,2048]{1,0:T(8,128)(2,1)}, bf16[128,2048]{1,0:T(8,128)(2,1)S(1)}, u32[]{:S(2)}, u32[]{:S(2)}) collective-permute-start(bf16[128,2048]{1,0:T(8,128)(2,1)} %bitcast.11), channel_id=1, source_target_pairs={{0,1},{1,0},{2,3},{3,2},{4,5},{5,4},{6,7},{7,6},{8,9},{9,8},{10,11... | collective-permute-start | bytes 1572872 | tf_op jit(solution)/shard_map/ppermute | solution.py:152
  1.2 6.4 %collective-permute-start.3 = (bf16[128,2048]{1,0:T(8,128)(2,1)}, bf16[128,2048]{1,0:T(8,128)(2,1)S(1)}, u32[]{:S(2)}, u32[]{:S(2)}) collective-permute-start(bf16[128,2048]{1,0:T(8,128)(2,1)} %bitcast.17), channel_id=1, source_target_pairs={{0,1},{1,0},{2,3},{3,2},{4,5},{5,4},{6,7},{7,6},{8,9},{9,8},{10,11... | collective-permute-start | bytes 1572872 | tf_op jit(solution)/shard_map/ppermute | solution.py:152
  1.7 9.6 %collective-permute-start.2 = (bf16[128,2048]{1,0:T(8,128)(2,1)}, bf16[128,2048]{1,0:T(8,128)(2,1)S(1)}, u32[]{:S(2)}, u32[]{:S(2)}) collective-permute-start(bf16[128,2048]{1,0:T(8,128)(2,1)} %bitcast.14), channel_id=1, source_target_pairs={{0,1},{1,0},{2,3},{3,2},{4,5},{5,4},{6,7},{7,6},{8,9},{9,8},{10,11... | collective-permute-start | bytes 1572872 | tf_op jit(solution)/shard_map/ppermute | solution.py:152
  1.7 5.9 %copy-start = (bf16[1,128,2048]{2,1,0:T(8,128)(2,1)S(1)}, bf16[1,128,2048]{2,1,0:T(8,128)(2,1)}, u32[]{:S(2)}) copy-start(bf16[1,128,2048]{2,1,0:T(8,128)(2,1)} %param.5) | copy-start | bytes 1572868
  1.7 5.9 %copy-start.1 = (bf16[1,128,2048]{2,1,0:T(8,128)(2,1)S(1)}, bf16[1,128,2048]{2,1,0:T(8,128)(2,1)}, u32[]{:S(2)}) copy-start(bf16[1,128,2048]{2,1,0:T(8,128)(2,1)} %param.6) | copy-start | bytes 1572868
  3.1 11.6 %collective-permute-start.8 = (bf16[128,512]{1,0:T(8,128)(2,1)S(1)}, bf16[128,512]{1,0:T(8,128)(2,1)S(1)}, u32[]{:S(2)}, u32[]{:S(2)}) collective-permute-start(bf16[128,512]{1,0:T(8,128)(2,1)S(1)} %get-tuple-element.42), channel_id=1, source_target_pairs={{0,8},{8,0},{16,24},{24,16},{1,9},{9,1},{17,25},{25,17},{2,10},{10... | collective-permute-start | bytes 393224 | tf_op jit(solution)/shard_map/ppermute | solution.py:152
  6.1 9.2 %collective-permute-start.9 = (bf16[128,512]{1,0:T(8,128)(2,1)S(1)}, bf16[128,512]{1,0:T(8,128)(2,1)S(1)}, u32[]{:S(2)}, u32[]{:S(2)}) collective-permute-start(bf16[128,512]{1,0:T(8,128)(2,1)S(1)} %get-tuple-element.43), channel_id=1, source_target_pairs={{0,16},{8,24},{16,0},{24,8},{1,17},{9,25},{17,1},{25,9},{2,18},{10... | collective-permute-start | bytes 393224 | tf_op jit(solution)/shard_map/ppermute | solution.py:152
  7.6 7.8 %collective-permute-start.10 = (bf16[128,512]{1,0:T(8,128)(2,1)S(1)}, bf16[128,512]{1,0:T(8,128)(2,1)S(1)}, u32[]{:S(2)}, u32[]{:S(2)}) collective-permute-start(bf16[128,512]{1,0:T(8,128)(2,1)S(1)} %get-tuple-element.44), channel_id=1, source_target_pairs={{0,24},{8,16},{16,8},{24,0},{1,25},{9,17},{17,9},{25,1},{2,26},{10... | collective-permute-start | bytes 393224 | tf_op jit(solution)/shard_map/ppermute | solution.py:152
  9.1 2.2 %copy-start.2 = (bf16[1,128,2048]{2,1,0:T(8,128)(2,1)S(1)}, bf16[1,128,2048]{2,1,0:T(8,128)(2,1)}, u32[]{:S(2)}) copy-start(bf16[1,128,2048]{2,1,0:T(8,128)(2,1)} %param.7) | copy-start | bytes 1572868
  9.1 8.0 %collective-permute-start.11 = (bf16[256,512]{1,0:T(8,128)(2,1)S(1)}, bf16[256,512]{1,0:T(8,128)(2,1)S(1)}, u32[]{:S(2)}, u32[]{:S(2)}) collective-permute-start(bf16[256,512]{1,0:T(8,128)(2,1)S(1)} %get-tuple-element.35), channel_id=1, source_target_pairs={{0,2},{1,3},{2,0},{3,1},{4,6},{5,7},{6,4},{7,5},{8,10},{9,11},{10,... | collective-permute-start | bytes 786440 | tf_op jit(solution)/shard_map/ppermute | solution.py:152
  14.6 7.5 %collective-permute-start.4 = (bf16[128,1024]{1,0:T(8,128)(2,1)S(1)}, bf16[128,1024]{1,0:T(8,128)(2,1)S(1)}, u32[]{:S(2)}, u32[]{:S(2)}) collective-permute-start(bf16[128,1024]{1,0:T(8,128)(2,1)S(1)} %get-tuple-element.36), channel_id=1, source_target_pairs={{0,1},{1,0},{2,3},{3,2},{4,5},{5,4},{6,7},{7,6},{8,9},{9,8},{10,11... | collective-permute-start | bytes 786440 | tf_op jit(solution)/shard_map/ppermute | solution.py:152
  14.7 8.0 %collective-permute-start.5 = (bf16[128,1024]{1,0:T(8,128)(2,1)S(1)}, bf16[128,1024]{1,0:T(8,128)(2,1)S(1)}, u32[]{:S(2)}, u32[]{:S(2)}) collective-permute-start(bf16[128,1024]{1,0:T(8,128)(2,1)S(1)} %get-tuple-element.37), channel_id=1, source_target_pairs={{0,1},{1,0},{2,3},{3,2},{4,5},{5,4},{6,7},{7,6},{8,9},{9,8},{10,11... | collective-permute-start | bytes 786440 | tf_op jit(solution)/shard_map/ppermute | solution.py:152
  15.3 3.7 %collective-permute-start.6 = (bf16[128,512]{1,0:T(8,128)(2,1)S(1)}, bf16[128,512]{1,0:T(8,128)(2,1)S(1)}, u32[]{:S(2)}, u32[]{:S(2)}) collective-permute-start(bf16[128,512]{1,0:T(8,128)(2,1)S(1)} %get-tuple-element.76), channel_id=1, source_target_pairs={{0,1},{1,0},{2,3},{3,2},{4,5},{5,4},{6,7},{7,6},{8,9},{9,8},{10,11... | collective-permute-start | bytes 393224 | tf_op jit(solution)/shard_map/ppermute | solution.py:152
  15.3 5.2 %collective-permute-start.7 = (bf16[128,512]{1,0:T(8,128)(2,1)S(1)}, bf16[128,512]{1,0:T(8,128)(2,1)S(1)}, u32[]{:S(2)}, u32[]{:S(2)}) collective-permute-start(bf16[128,512]{1,0:T(8,128)(2,1)S(1)} %get-tuple-element.74), channel_id=1, source_target_pairs={{0,1},{1,0},{2,3},{3,2},{4,5},{5,4},{6,7},{7,6},{8,9},{9,8},{10,11... | collective-permute-start | bytes 393224 | tf_op jit(solution)/shard_map/ppermute | solution.py:152
  17.3 13.5 %collective-permute-start.13 = (bf16[512,512]{1,0:T(8,128)(2,1)S(1)}, bf16[512,512]{1,0:T(8,128)(2,1)S(1)}, u32[]{:S(2)}, u32[]{:S(2)}) collective-permute-start(bf16[512,512]{1,0:T(8,128)(2,1)S(1)} %turned.1.refs_0_), channel_id=1, source_target_pairs={{0,2},{1,3},{2,0},{3,1},{4,6},{5,7},{6,4},{7,5},{8,10},{9,11},{10,... | collective-permute-start | bytes 1572872 | tf_op jit(solution)/shard_map/ppermute | solution.py:152
  19.0 9.1 %collective-permute-start.19 = (bf16[512,256]{1,0:T(8,128)(2,1)S(1)}, bf16[512,256]{1,0:T(8,128)(2,1)S(1)}, u32[]{:S(2)}, u32[]{:S(2)}) collective-permute-start(bf16[512,256]{1,0:T(8,128)(2,1)S(1)} %pad_maximum_fusion.2), channel_id=1, source_target_pairs={{0,8},{8,0},{16,24},{24,16},{1,9},{9,1},{17,25},{25,17},{2,10},{10... | collective-permute-start | bytes 786440 | tf_op jit(solution)/shard_map/ppermute | solution.py:152
  20.5 8.8 %collective-permute-start.20 = (bf16[512,256]{1,0:T(8,128)(2,1)S(1)}, bf16[512,256]{1,0:T(8,128)(2,1)S(1)}, u32[]{:S(2)}, u32[]{:S(2)}) collective-permute-start(bf16[512,256]{1,0:T(8,128)(2,1)S(1)} %pad_maximum_fusion.2), channel_id=1, source_target_pairs={{0,16},{8,24},{16,0},{24,8},{1,17},{9,25},{17,1},{25,9},{2,18},{10... | collective-permute-start | bytes 786440 | tf_op jit(solution)/shard_map/ppermute | solution.py:152
  22.1 8.9 %collective-permute-start.15 = (bf16[512,256]{1,0:T(8,128)(2,1)S(1)}, bf16[512,256]{1,0:T(8,128)(2,1)S(1)}, u32[]{:S(2)}, u32[]{:S(2)}) collective-permute-start(bf16[512,256]{1,0:T(8,128)(2,1)S(1)} %pad_maximum_fusion.1), channel_id=1, source_target_pairs={{0,8},{8,0},{16,24},{24,16},{1,9},{9,1},{17,25},{25,17},{2,10},{10... | collective-permute-start | bytes 786440 | tf_op jit(solution)/shard_map/ppermute | solution.py:152
  22.7 10.2 %collective-permute-start.16 = (bf16[512,256]{1,0:T(8,128)(2,1)S(1)}, bf16[512,256]{1,0:T(8,128)(2,1)S(1)}, u32[]{:S(2)}, u32[]{:S(2)}) collective-permute-start(bf16[512,256]{1,0:T(8,128)(2,1)S(1)} %pad_maximum_fusion.1), channel_id=1, source_target_pairs={{0,16},{8,24},{16,0},{24,8},{1,17},{9,25},{17,1},{25,9},{2,18},{10... | collective-permute-start | bytes 786440 | tf_op jit(solution)/shard_map/ppermute | solution.py:152
  28.1 9.6 %collective-permute-start.12 = (bf16[512,512]{1,0:T(8,128)(2,1)S(1)}, bf16[512,512]{1,0:T(8,128)(2,1)S(1)}, u32[]{:S(2)}, u32[]{:S(2)}) collective-permute-start(bf16[512,512]{1,0:T(8,128)(2,1)S(1)} %turned.1.refs_0_), channel_id=1, source_target_pairs={{0,1},{1,0},{2,3},{3,2},{4,5},{5,4},{6,7},{7,6},{8,9},{9,8},{10,11... | collective-permute-start | bytes 1572872 | tf_op jit(solution)/shard_map/ppermute | solution.py:152
  29.3 8.4 %collective-permute-start.21 = (bf16[512,256]{1,0:T(8,128)(2,1)S(1)}, bf16[512,256]{1,0:T(8,128)(2,1)S(1)}, u32[]{:S(2)}, u32[]{:S(2)}) collective-permute-start(bf16[512,256]{1,0:T(8,128)(2,1)S(1)} %collective-permute-done.19), channel_id=1, source_target_pairs={{0,16},{8,24},{16,0},{24,8},{1,17},{9,25},{17,1},{25,9},{2,18},{10... | collective-permute-start | bytes 786440 | tf_op jit(solution)/shard_map/ppermute | solution.py:152
  30.8 6.9 %collective-permute-start.14 = (bf16[512,512]{1,0:T(8,128)(2,1)S(1)}, bf16[512,512]{1,0:T(8,128)(2,1)S(1)}, u32[]{:S(2)}, u32[]{:S(2)}) collective-permute-start(bf16[512,512]{1,0:T(8,128)(2,1)S(1)} %collective-permute-done.13.refs_2_), channel_id=1, source_target_pairs={{0,1},{1,0},{2,3},{3,2},{4,5},{5,4},{6,7},{7,6},{8,9},{9,8},{10,11... | collective-permute-start | bytes 1572872 | tf_op jit(solution)/shard_map/ppermute | solution.py:152
  32.9 8.2 %collective-permute-start.17 = (bf16[512,256]{1,0:T(8,128)(2,1)S(1)}, bf16[512,256]{1,0:T(8,128)(2,1)S(1)}, u32[]{:S(2)}, u32[]{:S(2)}) collective-permute-start(bf16[512,256]{1,0:T(8,128)(2,1)S(1)} %collective-permute-done.16), channel_id=1, source_target_pairs={{0,8},{8,0},{16,24},{24,16},{1,9},{9,1},{17,25},{25,17},{2,10},{10... | collective-permute-start | bytes 786440 | tf_op jit(solution)/shard_map/ppermute | solution.py:152
  38.5 11.5 %collective-permute-start.22 = (bf16[512,128]{1,0:T(8,128)(2,1)S(1)}, bf16[512,128]{1,0:T(8,128)(2,1)S(1)}, u32[]{:S(2)}, u32[]{:S(2)}) collective-permute-start(bf16[512,128]{1,0:T(8,128)(2,1)S(1)} %get-tuple-element.57), channel_id=1, source_target_pairs={{0,4},{1,5},{2,6},{3,7},{4,0},{5,1},{6,2},{7,3},{8,12},{9,13},{10,... | collective-permute-start | bytes 393224 | tf_op jit(solution)/shard_map/ppermute | solution.py:152
  41.9 10.7 %collective-permute-start.18 = (bf16[512,128]{1,0:T(8,128)(2,1)S(1)}, bf16[512,128]{1,0:T(8,128)(2,1)S(1)}, u32[]{:S(2)}, u32[]{:S(2)}) collective-permute-start(bf16[512,128]{1,0:T(8,128)(2,1)S(1)} %get-tuple-element.53), channel_id=1, source_target_pairs={{0,4},{1,5},{2,6},{3,7},{4,0},{5,1},{6,2},{7,3},{8,12},{9,13},{10,... | collective-permute-start | bytes 393224 | tf_op jit(solution)/shard_map/ppermute | solution.py:152

commit v5 on v4

--- a/solution.py
+++ b/solution.py
@@ -373,9 +373,9 @@
         here = slice(2 * head * HD, 2 * (head + 1) * HD)
         paired = jnp.concatenate([kept[:, here], got[:, here]], axis=0)
         by_x, by_y = after([swap(paired, "dp", 1), swap(paired, "dp", 2)])
-        cross = swap(by_x, "dp", 2) if head else swap(by_y, "dp", 1)
-        near = [paired[: 2 * half], by_x[: 2 * half], by_y[: 2 * half], cross[: 2 * half]]
-        far = [paired[2 * half :], by_x[2 * half :], by_y[2 * half :], cross[2 * half :]]
+        first, second = after([swap(by_y[: 2 * half], "dp", 1), swap(by_x[2 * half :], "dp", 2)])
+        near = [paired[: 2 * half], by_x[: 2 * half], by_y[: 2 * half], first]
+        far = [paired[2 * half :], by_x[2 * half :], by_y[2 * half :], second]
         sides.append((near, far))
 
     x_mine = after(x_mine, got, q_theirs)

time: 53.6 us -> 53.4 us (level)
  waiting for transfers between devices: 22.3 us -> 13.8 us
  starting transfers between devices: 20 us -> 28.4 us
    ppermute x23 -> x25, waiting for transfers between devices: 22.3 us -> 13.8 us  [swap(): lax.ppermute(value, axis, [(i, i ^ bit) for i in range(lax.axis_size(axis...]
    ppermute x23 -> x25, starting transfers between devices: 20 us -> 28.4 us  [swap(): lax.ppermute(value, axis, [(i, i ^ bit) for i in range(lax.axis_size(axis...]
  transfers between devices with their start and end apart: 23 -> 25, of which waited for: 8 -> 6; matrix products, arithmetic and copies ran while one was open for 0% -> 0% of each run, Pallas kernels for 17% -> 17%
where the time goes in v5:
time: 53.4 us; the launch traced here: 53.3 us
  starting transfers between devices  28.4 us (53%)
  waiting for transfers between devices  13.8 us (26%)
  Pallas kernels  9.2 us (17%)
  other arithmetic  0.91 us (2%)
  between operations  0.83 us (2%)
    ppermute x25, starting transfers between devices, swap(): lax.ppermute(value, axis, [(i, i ^ bit) for i in range(lax.axis_size(axis...  28.4 us
    ppermute x25, waiting for transfers between devices, swap(): lax.ppermute(value, axis, [(i, i ^ bit) for i in range(lax.axis_size(axis...  13.8 us
    pallas_call x6, Pallas kernels, call(): pl.pallas_call(kernel, in_specs=[in_vmem] * len(operands), out_specs=[in_...  7.88 us
    pallas_call x1, Pallas kernels, packed_inputs(): pl.pallas_call(kernel, in_specs=[pl.BlockSpec(memory_space=pl.ANY)] * (co...  1.31 us
  transfers between devices with their start and end apart: 25, of which 6 were waited for; matrix products, arithmetic and copies ran while one was open for 0% of the time, Pallas kernels for 17%

profile of v5, /device:TPU:0, one launch (start us, length us, event | category | flops | bytes accessed | tf_op | source)
XLA Modules:
  0.0 53.3 jit_solution(13711385831134965883)
XLA Ops:
  0.6 0.5 collective-permute-start
  1.2 0.4 collective-permute-start.3
  1.7 1.3 %packed_inputs.1 = (bf16[128,1024]{1,0:T(8,128)(2,1)S(1)}, bf16[128,512]{1,0:T(8,128)(2,1)S(1)}, bf16[128,512]{1,0:T(8,128)(2,1)S(1)}, bf16[128,512]{1,0:T(8,128)(2,1)S(1)}, bf16[128,512]{1,0:T(8,128)(2,1)S(1)}) custom-call(bf16[128,2048]{1,0:T(8,128)(2,1)} %bitcast.18, bf16[128,2048]{1,0:T(8,128)(2,1)} %bitcast.16), custom_call_target="tpu_custom_call" | custom-call | tf_op jit(solution)/shard_map/packed_inputs/pallas_call | solution.py:210
  3.1 3.0 %collective-permute-start.8 = (bf16[128,512]{1,0:T(8,128)(2,1)S(1)}, bf16[128,512]{1,0:T(8,128)(2,1)S(1)}, u32[]{:S(2)}, u32[]{:S(2)}) collective-permute-start(bf16[128,512]{1,0:T(8,128)(2,1)S(1)} %get-tuple-element.46), channel_id=1, source_target_pairs={{0,8},{8,0},{16,24},{24,16},{1,9},{9,1},{17,25},{25,17},{2,10},{10... | collective-permute-start | bytes 393224 | tf_op jit(solution)/shard_map/ppermute | solution.py:152
  6.1 1.5 %collective-permute-start.9 = (bf16[128,512]{1,0:T(8,128)(2,1)S(1)}, bf16[128,512]{1,0:T(8,128)(2,1)S(1)}, u32[]{:S(2)}, u32[]{:S(2)}) collective-permute-start(bf16[128,512]{1,0:T(8,128)(2,1)S(1)} %get-tuple-element.47), channel_id=1, source_target_pairs={{0,16},{8,24},{16,0},{24,8},{1,17},{9,25},{17,1},{25,9},{2,18},{10... | collective-permute-start | bytes 393224 | tf_op jit(solution)/shard_map/ppermute | solution.py:152
  7.6 1.5 %value_part.1 = (bf16[256,512]{1,0:T(8,128)(2,1)S(1)}, bf16[256,512]{1,0:T(8,128)(2,1)S(1)}) custom-call(bf16[128,2048]{1,0:T(8,128)(2,1)S(1)} %bitcast.9, bf16[128,2048]{1,0:T(8,128)(2,1)S(1)} %collective-permute-done.q1.refs_1_, bf16[128,2048]{1,0:T(8,128)(2,1)S(1)} %bitcast.12, bf16[128,2048]{1,0:T(8,128)(2,1)S(1)} %collective-permute-done.1.k1.refs_3_, ...), custom_call_target="tpu_custom_call" | custom-call | tf_op jit(solution)/shard_map/value_part/pallas_call | solution.py:163
  9.1 2.1 %collective-permute-start.11 = (bf16[256,512]{1,0:T(8,128)(2,1)S(1)}, bf16[256,512]{1,0:T(8,128)(2,1)S(1)}, u32[]{:S(2)}, u32[]{:S(2)}) collective-permute-start(bf16[256,512]{1,0:T(8,128)(2,1)S(1)} %get-tuple-element.39), channel_id=1, source_target_pairs={{0,2},{1,3},{2,0},{3,1},{4,6},{5,7},{6,4},{7,5},{8,10},{9,11},{10,... | collective-permute-start | bytes 786440 | tf_op jit(solution)/shard_map/ppermute | solution.py:152
  11.3 3.3 %score_part.1 = (bf16[128,1024]{1,0:T(8,128)(2,1)S(1)}, bf16[128,1024]{1,0:T(8,128)(2,1)S(1)}, bf16[128,1024]{1,0:T(8,128)(2,1)S(1)}, bf16[128,1024]{1,0:T(8,128)(2,1)S(1)}) custom-call(bf16[128,2048]{1,0:T(8,128)(2,1)S(1)} %bitcast.10, bf16[128,2048]{1,0:T(8,128)(2,1)S(1)} %collective-permute-done.q1.refs_1_, bf16[128,2048]{1,0:T(8,128)(2,1)S(1)} %bitcast.13, ...), custom_call_target="tpu_custom_call" | custom-call | tf_op jit(solution)/shard_map/score_part/pallas_call | solution.py:163
  14.7 0.6 %collective-permute-start.5 = (bf16[128,1024]{1,0:T(8,128)(2,1)S(1)}, bf16[128,1024]{1,0:T(8,128)(2,1)S(1)}, u32[]{:S(2)}, u32[]{:S(2)}) collective-permute-start(bf16[128,1024]{1,0:T(8,128)(2,1)S(1)} %get-tuple-element.41), channel_id=1, source_target_pairs={{0,1},{1,0},{2,3},{3,2},{4,5},{5,4},{6,7},{7,6},{8,9},{9,8},{10,11... | collective-permute-start | bytes 786440 | tf_op jit(solution)/shard_map/ppermute | solution.py:152
  15.3 0.4 collective-permute-start.7
  15.8 1.3 %collective-permute-done.11 = bf16[256,512]{1,0:T(8,128)(2,1)S(1)} collective-permute-done((bf16[256,512]{1,0:T(8,128)(2,1)S(1)}, bf16[256,512]{1,0:T(8,128)(2,1)S(1)}, u32[]{:S(2)}, u32[]{:S(2)}) %collective-permute-start.11) | collective-permute-done | bytes 262176 | tf_op jit(solution)/shard_map/ppermute | solution.py:152
  17.1 0.2 turned.1.refs_0_
  17.3 1.6 %collective-permute-start.13 = (bf16[512,512]{1,0:T(8,128)(2,1)S(1)}, bf16[512,512]{1,0:T(8,128)(2,1)S(1)}, u32[]{:S(2)}, u32[]{:S(2)}) collective-permute-start(bf16[512,512]{1,0:T(8,128)(2,1)S(1)} %turned.1.refs_0_), channel_id=1, source_target_pairs={{0,2},{1,3},{2,0},{3,1},{4,6},{5,7},{6,4},{7,5},{8,10},{9,11},{10,... | collective-permute-start | bytes 1572872 | tf_op jit(solution)/shard_map/ppermute | solution.py:152
  19.0 1.5 %collective-permute-start.20 = (bf16[512,256]{1,0:T(8,128)(2,1)S(1)}, bf16[512,256]{1,0:T(8,128)(2,1)S(1)}, u32[]{:S(2)}, u32[]{:S(2)}) collective-permute-start(bf16[512,256]{1,0:T(8,128)(2,1)S(1)} %pad_maximum_fusion.2), channel_id=1, source_target_pairs={{0,8},{8,0},{16,24},{24,16},{1,9},{9,1},{17,25},{25,17},{2,10},{10... | collective-permute-start | bytes 786440 | tf_op jit(solution)/shard_map/ppermute | solution.py:152
  20.5 1.5 %collective-permute-start.21 = (bf16[512,256]{1,0:T(8,128)(2,1)S(1)}, bf16[512,256]{1,0:T(8,128)(2,1)S(1)}, u32[]{:S(2)}, u32[]{:S(2)}) collective-permute-start(bf16[512,256]{1,0:T(8,128)(2,1)S(1)} %pad_maximum_fusion.2), channel_id=1, source_target_pairs={{0,16},{8,24},{16,0},{24,8},{1,17},{9,25},{17,1},{25,9},{2,18},{10... | collective-permute-start | bytes 786440 | tf_op jit(solution)/shard_map/ppermute | solution.py:152
  22.2 0.6 %collective-permute-start.15 = (bf16[512,256]{1,0:T(8,128)(2,1)S(1)}, bf16[512,256]{1,0:T(8,128)(2,1)S(1)}, u32[]{:S(2)}, u32[]{:S(2)}) collective-permute-start(bf16[512,256]{1,0:T(8,128)(2,1)S(1)} %pad_maximum_fusion.1), channel_id=1, source_target_pairs={{0,8},{8,0},{16,24},{24,16},{1,9},{9,1},{17,25},{25,17},{2,10},{10... | collective-permute-start | bytes 786440 | tf_op jit(solution)/shard_map/ppermute | solution.py:152
  22.8 1.5 %joined.1 = (bf16[128,2048]{1,0:T(8,128)(2,1)}, bf16[128,2048]{1,0:T(8,128)(2,1)}, bf16[128,2048]{1,0:T(8,128)(2,1)}) custom-call(bf16[128,1024]{1,0:T(8,128)(2,1)S(1)} %get-tuple-element.36.refs_0_, bf16[128,1024]{1,0:T(8,128)(2,1)S(1)} %get-tuple-element.37.refs_1_, bf16[128,512]{1,0:T(8,128)(2,1)S(1)} %get-tuple-element.81.refs_2_, ...), custom_call_target="tpu_custom_call" | custom-call | tf_op jit(solution)/shard_map/joined/pallas_call | solution.py:163
  24.3 1.3 %collective-permute-done.20 = bf16[512,256]{1,0:T(8,128)(2,1)S(1)} collective-permute-done((bf16[512,256]{1,0:T(8,128)(2,1)S(1)}, bf16[512,256]{1,0:T(8,128)(2,1)S(1)}, u32[]{:S(2)}, u32[]{:S(2)}) %collective-permute-start.20) | collective-permute-done | bytes 262176 | tf_op jit(solution)/shard_map/ppermute | solution.py:152
  25.5 2.5 %collective-permute-start.16 = (bf16[512,256]{1,0:T(8,128)(2,1)S(1)}, bf16[512,256]{1,0:T(8,128)(2,1)S(1)}, u32[]{:S(2)}, u32[]{:S(2)}) collective-permute-start(bf16[512,256]{1,0:T(8,128)(2,1)S(1)} %pad_maximum_fusion.1), channel_id=1, source_target_pairs={{0,16},{8,24},{16,0},{24,8},{1,17},{9,25},{17,1},{25,9},{2,18},{10... | collective-permute-start | bytes 786440 | tf_op jit(solution)/shard_map/ppermute | solution.py:152
  28.1 1.9 %collective-permute-done.13.refs_2_ = bf16[512,512]{1,0:T(8,128)(2,1)S(1)} collective-permute-done((bf16[512,512]{1,0:T(8,128)(2,1)S(1)}, bf16[512,512]{1,0:T(8,128)(2,1)S(1)}, u32[]{:S(2)}, u32[]{:S(2)}) %collective-permute-start.13) | collective-permute-done | bytes 524320 | tf_op jit(solution)/shard_map/ppermute | solution.py:152
  30.0 1.5 %collective-permute-start.22 = (bf16[256,256]{1,0:T(8,128)(2,1)S(1)}, bf16[256,256]{1,0:T(8,128)(2,1)S(1)}, u32[]{:S(2)}, u32[]{:S(2)}) collective-permute-start(bf16[256,256]{1,0:T(8,128)(2,1)S(1)} %get-tuple-element.75.refs_6_), channel_id=1, source_target_pairs={{0,8},{8,0},{16,24},{24,16},{1,9},{9,1},{17,25},{25,17},{2,10},{10... | collective-permute-start | bytes 393224 | tf_op jit(solution)/shard_map/ppermute | solution.py:152
  31.5 1.5 %collective-permute-start.23 = (bf16[256,256]{1,0:T(8,128)(2,1)S(1)}, bf16[256,256]{1,0:T(8,128)(2,1)S(1)}, u32[]{:S(2)}, u32[]{:S(2)}) collective-permute-start(bf16[256,256]{1,0:T(8,128)(2,1)S(1)} %get-tuple-element.76.refs_9_), channel_id=1, source_target_pairs={{0,16},{8,24},{16,0},{24,8},{1,17},{9,25},{17,1},{25,9},{2,18},{10... | collective-permute-start | bytes 393224 | tf_op jit(solution)/shard_map/ppermute | solution.py:152
  33.1 1.9 %collective-permute-start.17 = (bf16[256,256]{1,0:T(8,128)(2,1)S(1)}, bf16[256,256]{1,0:T(8,128)(2,1)S(1)}, u32[]{:S(2)}, u32[]{:S(2)}) collective-permute-start(bf16[256,256]{1,0:T(8,128)(2,1)S(1)} %get-tuple-element.67.refs_6_), channel_id=1, source_target_pairs={{0,8},{8,0},{16,24},{24,16},{1,9},{9,1},{17,25},{25,17},{2,10},{10... | collective-permute-start | bytes 393224 | tf_op jit(solution)/shard_map/ppermute | solution.py:152
  35.0 1.3 %collective-permute-done.22.refs_7_ = bf16[256,256]{1,0:T(8,128)(2,1)S(1)} collective-permute-done((bf16[256,256]{1,0:T(8,128)(2,1)S(1)}, bf16[256,256]{1,0:T(8,128)(2,1)S(1)}, u32[]{:S(2)}, u32[]{:S(2)}) %collective-permute-start.22) | collective-permute-done | bytes 131104 | tf_op jit(solution)/shard_map/ppermute | solution.py:152
  36.3 1.6 %collective-permute-start.18 = (bf16[256,256]{1,0:T(8,128)(2,1)S(1)}, bf16[256,256]{1,0:T(8,128)(2,1)S(1)}, u32[]{:S(2)}, u32[]{:S(2)}) collective-permute-start(bf16[256,256]{1,0:T(8,128)(2,1)S(1)} %get-tuple-element.68.refs_9_), channel_id=1, source_target_pairs={{0,16},{8,24},{16,0},{24,8},{1,17},{9,25},{17,1},{25,9},{2,18},{10... | collective-permute-start | bytes 393224 | tf_op jit(solution)/shard_map/ppermute | solution.py:152
  37.9 0.7 %term_part.3 = (f32[512,128]{1,0:T(8,128)S(1)}, bf16[512,128]{1,0:T(8,128)(2,1)S(1)}) custom-call(bf16[512,512]{1,0:T(8,128)(2,1)S(1)} %turned.1.refs_0_, bf16[512,512]{1,0:T(8,128)(2,1)S(1)} %collective-permute-done.12.refs_1_, bf16[512,512]{1,0:T(8,128)(2,1)S(1)} %collective-permute-done.13.refs_2_, bf16[512,512]{1,0:T(8,128)(2,1)S(1)} %collective-permute-done.14.refs_3_, ...), custom_call_target="tpu_custom_call" | custom-call | tf_op jit(solution)/shard_map/term_part/pallas_call | solution.py:163
  38.6 2.7 %collective-permute-start.24 = (bf16[512,128]{1,0:T(8,128)(2,1)S(1)}, bf16[512,128]{1,0:T(8,128)(2,1)S(1)}, u32[]{:S(2)}, u32[]{:S(2)}) collective-permute-start(bf16[512,128]{1,0:T(8,128)(2,1)S(1)} %get-tuple-element.65), channel_id=1, source_target_pairs={{0,4},{1,5},{2,6},{3,7},{4,0},{5,1},{6,2},{7,3},{8,12},{9,13},{10,... | collective-permute-start | bytes 393224 | tf_op jit(solution)/shard_map/ppermute | solution.py:152
  41.2 0.7 %term_part.2 = (f32[512,128]{1,0:T(8,128)S(1)}, bf16[512,128]{1,0:T(8,128)(2,1)S(1)}) custom-call(bf16[512,512]{1,0:T(8,128)(2,1)S(1)} %turned.1.refs_0_, bf16[512,512]{1,0:T(8,128)(2,1)S(1)} %collective-permute-done.12.refs_1_, bf16[512,512]{1,0:T(8,128)(2,1)S(1)} %collective-permute-done.13.refs_2_, bf16[512,512]{1,0:T(8,128)(2,1)S(1)} %collective-permute-done.14.refs_3_, ...), custom_call_target="tpu_custom_call" | custom-call | tf_op jit(solution)/shard_map/term_part/pallas_call | solution.py:163
  42.0 2.5 %collective-permute-start.19 = (bf16[512,128]{1,0:T(8,128)(2,1)S(1)}, bf16[512,128]{1,0:T(8,128)(2,1)S(1)}, u32[]{:S(2)}, u32[]{:S(2)}) collective-permute-start(bf16[512,128]{1,0:T(8,128)(2,1)S(1)} %get-tuple-element.59), channel_id=1, source_target_pairs={{0,4},{1,5},{2,6},{3,7},{4,0},{5,1},{6,2},{7,3},{8,12},{9,13},{10,... | collective-permute-start | bytes 393224 | tf_op jit(solution)/shard_map/ppermute | solution.py:152
  44.5 5.9 %collective-permute-done.24 = bf16[512,128]{1,0:T(8,128)(2,1)S(1)} collective-permute-done((bf16[512,128]{1,0:T(8,128)(2,1)S(1)}, bf16[512,128]{1,0:T(8,128)(2,1)S(1)}, u32[]{:S(2)}, u32[]{:S(2)}) %collective-permute-start.24) | collective-permute-done | bytes 131104 | tf_op jit(solution)/shard_map/ppermute | solution.py:152
  50.4 2.1 %collective-permute-done.19 = bf16[512,128]{1,0:T(8,128)(2,1)S(1)} collective-permute-done((bf16[512,128]{1,0:T(8,128)(2,1)S(1)}, bf16[512,128]{1,0:T(8,128)(2,1)S(1)}, u32[]{:S(2)}, u32[]{:S(2)}) %collective-permute-start.19) | collective-permute-done | bytes 131104 | tf_op jit(solution)/shard_map/ppermute | solution.py:152
  52.5 0.8 %pad_maximum_fusion = f32[512,256]{1,0:T(8,128)} fusion(f32[512,128]{1,0:T(8,128)S(1)} %convert_add_fusion, f32[512,128]{1,0:T(8,128)S(1)} %convert_add_fusion.1), kind=kLoop, calls=%fused_computation | loop fusion | flops 131072 | bytes 1048576 | tf_op jit(solution)/shard_map/concatenate | solution.py:390
  (44 shorter events, 0.7 us)
Async XLA Ops:
  0.6 5.4 %collective-permute-start = (bf16[128,2048]{1,0:T(8,128)(2,1)}, bf16[128,2048]{1,0:T(8,128)(2,1)S(1)}, u32[]{:S(2)}, u32[]{:S(2)}) collective-permute-start(bf16[128,2048]{1,0:T(8,128)(2,1)} %bitcast.8), channel_id=1, source_target_pairs={{0,1},{1,0},{2,3},{3,2},{4,5},{5,4},{6,7},{7,6},{8,9},{9,8},{10,11... | collective-permute-start | bytes 1572872 | tf_op jit(solution)/shard_map/ppermute | solution.py:152
  1.1 6.4 %collective-permute-start.1 = (bf16[128,2048]{1,0:T(8,128)(2,1)}, bf16[128,2048]{1,0:T(8,128)(2,1)S(1)}, u32[]{:S(2)}, u32[]{:S(2)}) collective-permute-start(bf16[128,2048]{1,0:T(8,128)(2,1)} %bitcast.11), channel_id=1, source_target_pairs={{0,1},{1,0},{2,3},{3,2},{4,5},{5,4},{6,7},{7,6},{8,9},{9,8},{10,11... | collective-permute-start | bytes 1572872 | tf_op jit(solution)/shard_map/ppermute | solution.py:152
  1.2 6.4 %collective-permute-start.3 = (bf16[128,2048]{1,0:T(8,128)(2,1)}, bf16[128,2048]{1,0:T(8,128)(2,1)S(1)}, u32[]{:S(2)}, u32[]{:S(2)}) collective-permute-start(bf16[128,2048]{1,0:T(8,128)(2,1)} %bitcast.17), channel_id=1, source_target_pairs={{0,1},{1,0},{2,3},{3,2},{4,5},{5,4},{6,7},{7,6},{8,9},{9,8},{10,11... | collective-permute-start | bytes 1572872 | tf_op jit(solution)/shard_map/ppermute | solution.py:152
  1.7 9.6 %collective-permute-start.2 = (bf16[128,2048]{1,0:T(8,128)(2,1)}, bf16[128,2048]{1,0:T(8,128)(2,1)S(1)}, u32[]{:S(2)}, u32[]{:S(2)}) collective-permute-start(bf16[128,2048]{1,0:T(8,128)(2,1)} %bitcast.14), channel_id=1, source_target_pairs={{0,1},{1,0},{2,3},{3,2},{4,5},{5,4},{6,7},{7,6},{8,9},{9,8},{10,11... | collective-permute-start | bytes 1572872 | tf_op jit(solution)/shard_map/ppermute | solution.py:152
  1.7 5.9 %copy-start = (bf16[1,128,2048]{2,1,0:T(8,128)(2,1)S(1)}, bf16[1,128,2048]{2,1,0:T(8,128)(2,1)}, u32[]{:S(2)}) copy-start(bf16[1,128,2048]{2,1,0:T(8,128)(2,1)} %param.5) | copy-start | bytes 1572868
  1.7 5.9 %copy-start.1 = (bf16[1,128,2048]{2,1,0:T(8,128)(2,1)S(1)}, bf16[1,128,2048]{2,1,0:T(8,128)(2,1)}, u32[]{:S(2)}) copy-start(bf16[1,128,2048]{2,1,0:T(8,128)(2,1)} %param.6) | copy-start | bytes 1572868
  3.1 11.6 %collective-permute-start.8 = (bf16[128,512]{1,0:T(8,128)(2,1)S(1)}, bf16[128,512]{1,0:T(8,128)(2,1)S(1)}, u32[]{:S(2)}, u32[]{:S(2)}) collective-permute-start(bf16[128,512]{1,0:T(8,128)(2,1)S(1)} %get-tuple-element.46), channel_id=1, source_target_pairs={{0,8},{8,0},{16,24},{24,16},{1,9},{9,1},{17,25},{25,17},{2,10},{10... | collective-permute-start | bytes 393224 | tf_op jit(solution)/shard_map/ppermute | solution.py:152
  6.1 9.2 %collective-permute-start.9 = (bf16[128,512]{1,0:T(8,128)(2,1)S(1)}, bf16[128,512]{1,0:T(8,128)(2,1)S(1)}, u32[]{:S(2)}, u32[]{:S(2)}) collective-permute-start(bf16[128,512]{1,0:T(8,128)(2,1)S(1)} %get-tuple-element.47), channel_id=1, source_target_pairs={{0,16},{8,24},{16,0},{24,8},{1,17},{9,25},{17,1},{25,9},{2,18},{10... | collective-permute-start | bytes 393224 | tf_op jit(solution)/shard_map/ppermute | solution.py:152
  7.6 7.8 %collective-permute-start.10 = (bf16[128,512]{1,0:T(8,128)(2,1)S(1)}, bf16[128,512]{1,0:T(8,128)(2,1)S(1)}, u32[]{:S(2)}, u32[]{:S(2)}) collective-permute-start(bf16[128,512]{1,0:T(8,128)(2,1)S(1)} %get-tuple-element.48), channel_id=1, source_target_pairs={{0,24},{8,16},{16,8},{24,0},{1,25},{9,17},{17,9},{25,1},{2,26},{10... | collective-permute-start | bytes 393224 | tf_op jit(solution)/shard_map/ppermute | solution.py:152
  9.1 2.2 %copy-start.2 = (bf16[1,128,2048]{2,1,0:T(8,128)(2,1)S(1)}, bf16[1,128,2048]{2,1,0:T(8,128)(2,1)}, u32[]{:S(2)}) copy-start(bf16[1,128,2048]{2,1,0:T(8,128)(2,1)} %param.7) | copy-start | bytes 1572868
  9.1 8.0 %collective-permute-start.11 = (bf16[256,512]{1,0:T(8,128)(2,1)S(1)}, bf16[256,512]{1,0:T(8,128)(2,1)S(1)}, u32[]{:S(2)}, u32[]{:S(2)}) collective-permute-start(bf16[256,512]{1,0:T(8,128)(2,1)S(1)} %get-tuple-element.39), channel_id=1, source_target_pairs={{0,2},{1,3},{2,0},{3,1},{4,6},{5,7},{6,4},{7,5},{8,10},{9,11},{10,... | collective-permute-start | bytes 786440 | tf_op jit(solution)/shard_map/ppermute | solution.py:152
  14.6 7.5 %collective-permute-start.4 = (bf16[128,1024]{1,0:T(8,128)(2,1)S(1)}, bf16[128,1024]{1,0:T(8,128)(2,1)S(1)}, u32[]{:S(2)}, u32[]{:S(2)}) collective-permute-start(bf16[128,1024]{1,0:T(8,128)(2,1)S(1)} %get-tuple-element.40), channel_id=1, source_target_pairs={{0,1},{1,0},{2,3},{3,2},{4,5},{5,4},{6,7},{7,6},{8,9},{9,8},{10,11... | collective-permute-start | bytes 786440 | tf_op jit(solution)/shard_map/ppermute | solution.py:152
  14.7 7.5 %collective-permute-start.5 = (bf16[128,1024]{1,0:T(8,128)(2,1)S(1)}, bf16[128,1024]{1,0:T(8,128)(2,1)S(1)}, u32[]{:S(2)}, u32[]{:S(2)}) collective-permute-start(bf16[128,1024]{1,0:T(8,128)(2,1)S(1)} %get-tuple-element.41), channel_id=1, source_target_pairs={{0,1},{1,0},{2,3},{3,2},{4,5},{5,4},{6,7},{7,6},{8,9},{9,8},{10,11... | collective-permute-start | bytes 786440 | tf_op jit(solution)/shard_map/ppermute | solution.py:152
  15.3 3.7 %collective-permute-start.6 = (bf16[128,512]{1,0:T(8,128)(2,1)S(1)}, bf16[128,512]{1,0:T(8,128)(2,1)S(1)}, u32[]{:S(2)}, u32[]{:S(2)}) collective-permute-start(bf16[128,512]{1,0:T(8,128)(2,1)S(1)} %get-tuple-element.80), channel_id=1, source_target_pairs={{0,1},{1,0},{2,3},{3,2},{4,5},{5,4},{6,7},{7,6},{8,9},{9,8},{10,11... | collective-permute-start | bytes 393224 | tf_op jit(solution)/shard_map/ppermute | solution.py:152
  15.3 5.2 %collective-permute-start.7 = (bf16[128,512]{1,0:T(8,128)(2,1)S(1)}, bf16[128,512]{1,0:T(8,128)(2,1)S(1)}, u32[]{:S(2)}, u32[]{:S(2)}) collective-permute-start(bf16[128,512]{1,0:T(8,128)(2,1)S(1)} %get-tuple-element.78), channel_id=1, source_target_pairs={{0,1},{1,0},{2,3},{3,2},{4,5},{5,4},{6,7},{7,6},{8,9},{9,8},{10,11... | collective-permute-start | bytes 393224 | tf_op jit(solution)/shard_map/ppermute | solution.py:152
  17.3 12.7 %collective-permute-start.13 = (bf16[512,512]{1,0:T(8,128)(2,1)S(1)}, bf16[512,512]{1,0:T(8,128)(2,1)S(1)}, u32[]{:S(2)}, u32[]{:S(2)}) collective-permute-start(bf16[512,512]{1,0:T(8,128)(2,1)S(1)} %turned.1.refs_0_), channel_id=1, source_target_pairs={{0,2},{1,3},{2,0},{3,1},{4,6},{5,7},{6,4},{7,5},{8,10},{9,11},{10,... | collective-permute-start | bytes 1572872 | tf_op jit(solution)/shard_map/ppermute | solution.py:152
  19.0 6.5 %collective-permute-start.20 = (bf16[512,256]{1,0:T(8,128)(2,1)S(1)}, bf16[512,256]{1,0:T(8,128)(2,1)S(1)}, u32[]{:S(2)}, u32[]{:S(2)}) collective-permute-start(bf16[512,256]{1,0:T(8,128)(2,1)S(1)} %pad_maximum_fusion.2), channel_id=1, source_target_pairs={{0,8},{8,0},{16,24},{24,16},{1,9},{9,1},{17,25},{25,17},{2,10},{10... | collective-permute-start | bytes 786440 | tf_op jit(solution)/shard_map/ppermute | solution.py:152
  20.5 7.5 %collective-permute-start.21 = (bf16[512,256]{1,0:T(8,128)(2,1)S(1)}, bf16[512,256]{1,0:T(8,128)(2,1)S(1)}, u32[]{:S(2)}, u32[]{:S(2)}) collective-permute-start(bf16[512,256]{1,0:T(8,128)(2,1)S(1)} %pad_maximum_fusion.2), channel_id=1, source_target_pairs={{0,16},{8,24},{16,0},{24,8},{1,17},{9,25},{17,1},{25,9},{2,18},{10... | collective-permute-start | bytes 786440 | tf_op jit(solution)/shard_map/ppermute | solution.py:152
  22.1 15.8 %collective-permute-start.12 = (bf16[512,512]{1,0:T(8,128)(2,1)S(1)}, bf16[512,512]{1,0:T(8,128)(2,1)S(1)}, u32[]{:S(2)}, u32[]{:S(2)}) collective-permute-start(bf16[512,512]{1,0:T(8,128)(2,1)S(1)} %turned.1.refs_0_), channel_id=1, source_target_pairs={{0,1},{1,0},{2,3},{3,2},{4,5},{5,4},{6,7},{7,6},{8,9},{9,8},{10,11... | collective-permute-start | bytes 1572872 | tf_op jit(solution)/shard_map/ppermute | solution.py:152
  22.2 9.4 %collective-permute-start.15 = (bf16[512,256]{1,0:T(8,128)(2,1)S(1)}, bf16[512,256]{1,0:T(8,128)(2,1)S(1)}, u32[]{:S(2)}, u32[]{:S(2)}) collective-permute-start(bf16[512,256]{1,0:T(8,128)(2,1)S(1)} %pad_maximum_fusion.1), channel_id=1, source_target_pairs={{0,8},{8,0},{16,24},{24,16},{1,9},{9,1},{17,25},{25,17},{2,10},{10... | collective-permute-start | bytes 786440 | tf_op jit(solution)/shard_map/ppermute | solution.py:152
  25.5 7.5 %collective-permute-start.16 = (bf16[512,256]{1,0:T(8,128)(2,1)S(1)}, bf16[512,256]{1,0:T(8,128)(2,1)S(1)}, u32[]{:S(2)}, u32[]{:S(2)}) collective-permute-start(bf16[512,256]{1,0:T(8,128)(2,1)S(1)} %pad_maximum_fusion.1), channel_id=1, source_target_pairs={{0,16},{8,24},{16,0},{24,8},{1,17},{9,25},{17,1},{25,9},{2,18},{10... | collective-permute-start | bytes 786440 | tf_op jit(solution)/shard_map/ppermute | solution.py:152
  30.0 7.9 %collective-permute-start.14 = (bf16[512,512]{1,0:T(8,128)(2,1)S(1)}, bf16[512,512]{1,0:T(8,128)(2,1)S(1)}, u32[]{:S(2)}, u32[]{:S(2)}) collective-permute-start(bf16[512,512]{1,0:T(8,128)(2,1)S(1)} %collective-permute-done.13.refs_2_), channel_id=1, source_target_pairs={{0,1},{1,0},{2,3},{3,2},{4,5},{5,4},{6,7},{7,6},{8,9},{9,8},{10,11... | collective-permute-start | bytes 1572872 | tf_op jit(solution)/shard_map/ppermute | solution.py:152
  30.0 6.2 %collective-permute-start.22 = (bf16[256,256]{1,0:T(8,128)(2,1)S(1)}, bf16[256,256]{1,0:T(8,128)(2,1)S(1)}, u32[]{:S(2)}, u32[]{:S(2)}) collective-permute-start(bf16[256,256]{1,0:T(8,128)(2,1)S(1)} %get-tuple-element.75.refs_6_), channel_id=1, source_target_pairs={{0,8},{8,0},{16,24},{24,16},{1,9},{9,1},{17,25},{25,17},{2,10},{10... | collective-permute-start | bytes 393224 | tf_op jit(solution)/shard_map/ppermute | solution.py:152
  31.5 6.3 %collective-permute-start.23 = (bf16[256,256]{1,0:T(8,128)(2,1)S(1)}, bf16[256,256]{1,0:T(8,128)(2,1)S(1)}, u32[]{:S(2)}, u32[]{:S(2)}) collective-permute-start(bf16[256,256]{1,0:T(8,128)(2,1)S(1)} %get-tuple-element.76.refs_9_), channel_id=1, source_target_pairs={{0,16},{8,24},{16,0},{24,8},{1,17},{9,25},{17,1},{25,9},{2,18},{10... | collective-permute-start | bytes 393224 | tf_op jit(solution)/shard_map/ppermute | solution.py:152
  33.1 8.2 %collective-permute-start.17 = (bf16[256,256]{1,0:T(8,128)(2,1)S(1)}, bf16[256,256]{1,0:T(8,128)(2,1)S(1)}, u32[]{:S(2)}, u32[]{:S(2)}) collective-permute-start(bf16[256,256]{1,0:T(8,128)(2,1)S(1)} %get-tuple-element.67.refs_6_), channel_id=1, source_target_pairs={{0,8},{8,0},{16,24},{24,16},{1,9},{9,1},{17,25},{25,17},{2,10},{10... | collective-permute-start | bytes 393224 | tf_op jit(solution)/shard_map/ppermute | solution.py:152
  36.3 5.0 %collective-permute-start.18 = (bf16[256,256]{1,0:T(8,128)(2,1)S(1)}, bf16[256,256]{1,0:T(8,128)(2,1)S(1)}, u32[]{:S(2)}, u32[]{:S(2)}) collective-permute-start(bf16[256,256]{1,0:T(8,128)(2,1)S(1)} %get-tuple-element.68.refs_9_), channel_id=1, source_target_pairs={{0,16},{8,24},{16,0},{24,8},{1,17},{9,25},{17,1},{25,9},{2,18},{10... | collective-permute-start | bytes 393224 | tf_op jit(solution)/shard_map/ppermute | solution.py:152
  38.6 11.8 %collective-permute-start.24 = (bf16[512,128]{1,0:T(8,128)(2,1)S(1)}, bf16[512,128]{1,0:T(8,128)(2,1)S(1)}, u32[]{:S(2)}, u32[]{:S(2)}) collective-permute-start(bf16[512,128]{1,0:T(8,128)(2,1)S(1)} %get-tuple-element.65), channel_id=1, source_target_pairs={{0,4},{1,5},{2,6},{3,7},{4,0},{5,1},{6,2},{7,3},{8,12},{9,13},{10,... | collective-permute-start | bytes 393224 | tf_op jit(solution)/shard_map/ppermute | solution.py:152
  42.0 10.5 %collective-permute-start.19 = (bf16[512,128]{1,0:T(8,128)(2,1)S(1)}, bf16[512,128]{1,0:T(8,128)(2,1)S(1)}, u32[]{:S(2)}, u32[]{:S(2)}) collective-permute-start(bf16[512,128]{1,0:T(8,128)(2,1)S(1)} %get-tuple-element.59), channel_id=1, source_target_pairs={{0,4},{1,5},{2,6},{3,7},{4,0},{5,1},{6,2},{7,3},{8,12},{9,13},{10,... | collective-permute-start | bytes 393224 | tf_op jit(solution)/shard_map/ppermute | solution.py:152

commit v6 on v5

--- a/solution.py
+++ b/solution.py
@@ -179,12 +179,11 @@
 
 def both(mine, theirs, group, core, head):
     packed, spread = columns(2 * group + head), columns(4 * group + 2 * core + head)
-    own = packed if mine.shape[1] < theirs.shape[1] else spread
-    return jnp.concatenate([mine[:, own], theirs[:, spread]], axis=0)
+    return jnp.concatenate([mine[:, packed], theirs[:, spread]], axis=0)
 
 
 def packed_inputs(arrays, inputs):
-    half, width = inputs.shape
+    half, width = arrays[0].shape
     block = inputs.shape[1] // 4
     count = len(arrays)
     groups = width // (4 * HD)
@@ -248,7 +247,7 @@
             for head in range(2):
                 group = chip ^ apart
                 packed, spread = columns(2 * group + head), columns(4 * group + 2 * core + head)
-                mine = [ref[:, packed if ref.shape[1] < width else spread] for ref in (q0, k0, g0)]
+                mine = [ref[:, packed] for ref in (q0, k0, g0)]
                 theirs = [ref[:, spread] for ref in (q1, k1, g1)]
                 low, high = (theirs, mine) if core else (mine, theirs)
                 late = causal_probs(high[0], jnp.concatenate([low[1], high[1]], axis=0), half)
@@ -280,8 +279,10 @@
         for head in range(heads):
             where = head // 2, core, head % 2
             queries, keys = both(q0, q1, *where), both(k0, k1, *where)
+            spread = columns(4 * (head // 2) + 2 * core + head % 2)
+            values = jnp.concatenate([v0[:, spread], v1[:, spread]], axis=0)
             probs = probs_by_key(core, queries, keys)
-            dprob = dot(both(v0, v1, *where), both(g0, g1, *where), ((1,), (1,)))
+            dprob = dot(values, both(g0, g1, *where), ((1,), (1,)))
             delta = jnp.sum(probs * dprob, axis=0, keepdims=True)
             dscore = (probs * (dprob - delta) * HD ** (-0.5)).astype(jnp.bfloat16)
             key_grad = dot(dscore, queries, ((1,), (0,))).astype(jnp.bfloat16)
@@ -358,9 +359,8 @@
 def chip_body(queries, key_vectors, values, out_grad, inputs):
     half = queries.shape[1]
     arrays = [a[0] for a in (queries, key_vectors, out_grad, values)]
-    *packed, x_here, x_1, x_2, x_3 = packed_inputs([arrays[i] for i in (2,)], inputs[0])
-    own = dict(zip((2,), packed))
-    q, k, g, v = ((own.get(i, a), swap(a, "seq", 1)) for i, a in enumerate(arrays))
+    *own, x_here, x_1, x_2, x_3 = packed_inputs(arrays[:3], inputs[0])
+    q, k, g, v = ((mine, swap(a, "seq", 1)) for mine, a in zip((*own, arrays[3]), arrays))
     x_mine = [x_here, swap(x_1, "dp", 1), swap(x_2, "dp", 2), swap(x_3, "dp", 3)]
 
     kept, given = value_part(q, k, g)

time: 53.4 us -> 53.6 us (level)
  no operation moved by 1% of the time
where the time goes in v6:
time: 53.6 us; the launch traced here: 53.4 us
  starting transfers between devices  28.9 us (54%)
  waiting for transfers between devices  13.3 us (25%)
  Pallas kernels  9.32 us (17%)
  other arithmetic  0.91 us (2%)
  between operations  0.83 us (2%)
    ppermute x25, starting transfers between devices, swap(): lax.ppermute(value, axis, [(i, i ^ bit) for i in range(lax.axis_size(axis...  28.9 us
    ppermute x25, waiting for transfers between devices, swap(): lax.ppermute(value, axis, [(i, i ^ bit) for i in range(lax.axis_size(axis...  13.3 us
    pallas_call x6, Pallas kernels, call(): pl.pallas_call(kernel, in_specs=[in_vmem] * len(operands), out_specs=[in_...  7.86 us
    pallas_call x1, Pallas kernels, packed_inputs(): pl.pallas_call(kernel, in_specs=[pl.BlockSpec(memory_space=pl.ANY)] * (co...  1.46 us
  transfers between devices with their start and end apart: 25, of which 6 were waited for; matrix products, arithmetic and copies ran while one was open for 0% of the time, Pallas kernels for 17%

profile of v6, /device:TPU:0, one launch (start us, length us, event | category | flops | bytes accessed | tf_op | source)
XLA Modules:
  0.0 53.4 jit_solution(14473197834643908938)
XLA Ops:
  0.6 0.5 collective-permute-start
  1.2 0.4 collective-permute-start.3
  1.7 1.5 %packed_inputs.1 = (bf16[128,1024]{1,0:T(8,128)(2,1)S(1)}, bf16[128,1024]{1,0:T(8,128)(2,1)S(1)}, bf16[128,1024]{1,0:T(8,128)(2,1)S(1)}, bf16[128,512]{1,0:T(8,1...) custom-call(bf16[128,2048]{1,0:T(8,128)(2,1)} %bitcast.12, ...), custom_call_target="tpu_custom_call" | custom-call | tf_op jit(solution)/shard_map/packed_inputs/pallas_call | solution.py:209
  3.2 3.0 %collective-permute-start.8 = (bf16[128,512]{1,0:T(8,128)(2,1)S(1)}, bf16[128,512]{1,0:T(8,128)(2,1)S(1)}, u32[]{:S(2)}, u32[]{:S(2)}) collective-permute-start(bf16[128,512]{1,0:T(8,128)(2,1)S(1)} %get-tuple-element.50), channel_id=1, source_target_pairs={{0,8},{8,0},{16,24},{24,16},{1,9},{9,1},{17,25},{25,17},{2,10},{10... | collective-permute-start | bytes 393224 | tf_op jit(solution)/shard_map/ppermute | solution.py:152
  6.2 1.5 %collective-permute-start.9 = (bf16[128,512]{1,0:T(8,128)(2,1)S(1)}, bf16[128,512]{1,0:T(8,128)(2,1)S(1)}, u32[]{:S(2)}, u32[]{:S(2)}) collective-permute-start(bf16[128,512]{1,0:T(8,128)(2,1)S(1)} %get-tuple-element.51), channel_id=1, source_target_pairs={{0,16},{8,24},{16,0},{24,8},{1,17},{9,25},{17,1},{25,9},{2,18},{10... | collective-permute-start | bytes 393224 | tf_op jit(solution)/shard_map/ppermute | solution.py:152
  7.8 1.4 %value_part.1 = (bf16[256,512]{1,0:T(8,128)(2,1)S(1)}, bf16[256,512]{1,0:T(8,128)(2,1)S(1)}) custom-call(bf16[128,1024]{1,0:T(8,128)(2,1)S(1)} %get-tuple-element.37.q0.refs_0_, bf16[128,2048]{1,0:T(8,128)(2,1)S(1)} %collective-permute-done.q1.refs_1_, bf16[128,1024]{1,0:T(8,128)(2,1)S(1)} %get-tuple-element.38.k0.refs_2_, ...), custom_call_target="tpu_custom_call" | custom-call | tf_op jit(solution)/shard_map/value_part/pallas_call | solution.py:163
  9.2 2.1 %collective-permute-start.11 = (bf16[256,512]{1,0:T(8,128)(2,1)S(1)}, bf16[256,512]{1,0:T(8,128)(2,1)S(1)}, u32[]{:S(2)}, u32[]{:S(2)}) collective-permute-start(bf16[256,512]{1,0:T(8,128)(2,1)S(1)} %get-tuple-element.43), channel_id=1, source_target_pairs={{0,2},{1,3},{2,0},{3,1},{4,6},{5,7},{6,4},{7,5},{8,10},{9,11},{10,... | collective-permute-start | bytes 786440 | tf_op jit(solution)/shard_map/ppermute | solution.py:152
  11.4 3.3 %score_part.1 = (bf16[128,1024]{1,0:T(8,128)(2,1)S(1)}, bf16[128,1024]{1,0:T(8,128)(2,1)S(1)}, bf16[128,1024]{1,0:T(8,128)(2,1)S(1)}, bf16[128,1024]{1,0:T(8,128)(2,1)S(1)}) custom-call(bf16[128,1024]{1,0:T(8,128)(2,1)S(1)} %get-tuple-element.37.q0.refs_0_, bf16[128,2048]{1,0:T(8,128)(2,1)S(1)} %collective-permute-done.q1.refs_1_, ...), custom_call_target="tpu_custom_call" | custom-call | tf_op jit(solution)/shard_map/score_part/pallas_call | solution.py:163
  14.8 0.6 %collective-permute-start.5 = (bf16[128,1024]{1,0:T(8,128)(2,1)S(1)}, bf16[128,1024]{1,0:T(8,128)(2,1)S(1)}, u32[]{:S(2)}, u32[]{:S(2)}) collective-permute-start(bf16[128,1024]{1,0:T(8,128)(2,1)S(1)} %get-tuple-element.45), channel_id=1, source_target_pairs={{0,1},{1,0},{2,3},{3,2},{4,5},{5,4},{6,7},{7,6},{8,9},{9,8},{10,11... | collective-permute-start | bytes 786440 | tf_op jit(solution)/shard_map/ppermute | solution.py:152
  15.5 0.4 collective-permute-start.7
  15.9 1.2 %collective-permute-done.11 = bf16[256,512]{1,0:T(8,128)(2,1)S(1)} collective-permute-done((bf16[256,512]{1,0:T(8,128)(2,1)S(1)}, bf16[256,512]{1,0:T(8,128)(2,1)S(1)}, u32[]{:S(2)}, u32[]{:S(2)}) %collective-permute-start.11) | collective-permute-done | bytes 262176 | tf_op jit(solution)/shard_map/ppermute | solution.py:152
  17.1 0.2 turned.1.refs_0_
  17.3 1.8 %collective-permute-start.13 = (bf16[512,512]{1,0:T(8,128)(2,1)S(1)}, bf16[512,512]{1,0:T(8,128)(2,1)S(1)}, u32[]{:S(2)}, u32[]{:S(2)}) collective-permute-start(bf16[512,512]{1,0:T(8,128)(2,1)S(1)} %turned.1.refs_0_), channel_id=1, source_target_pairs={{0,2},{1,3},{2,0},{3,1},{4,6},{5,7},{6,4},{7,5},{8,10},{9,11},{10,... | collective-permute-start | bytes 1572872 | tf_op jit(solution)/shard_map/ppermute | solution.py:152
  19.1 1.6 %collective-permute-start.20 = (bf16[512,256]{1,0:T(8,128)(2,1)S(1)}, bf16[512,256]{1,0:T(8,128)(2,1)S(1)}, u32[]{:S(2)}, u32[]{:S(2)}) collective-permute-start(bf16[512,256]{1,0:T(8,128)(2,1)S(1)} %pad_maximum_fusion.2), channel_id=1, source_target_pairs={{0,8},{8,0},{16,24},{24,16},{1,9},{9,1},{17,25},{25,17},{2,10},{10... | collective-permute-start | bytes 786440 | tf_op jit(solution)/shard_map/ppermute | solution.py:152
  20.6 1.5 %collective-permute-start.21 = (bf16[512,256]{1,0:T(8,128)(2,1)S(1)}, bf16[512,256]{1,0:T(8,128)(2,1)S(1)}, u32[]{:S(2)}, u32[]{:S(2)}) collective-permute-start(bf16[512,256]{1,0:T(8,128)(2,1)S(1)} %pad_maximum_fusion.2), channel_id=1, source_target_pairs={{0,16},{8,24},{16,0},{24,8},{1,17},{9,25},{17,1},{25,9},{2,18},{10... | collective-permute-start | bytes 786440 | tf_op jit(solution)/shard_map/ppermute | solution.py:152
  22.3 0.6 %collective-permute-start.15 = (bf16[512,256]{1,0:T(8,128)(2,1)S(1)}, bf16[512,256]{1,0:T(8,128)(2,1)S(1)}, u32[]{:S(2)}, u32[]{:S(2)}) collective-permute-start(bf16[512,256]{1,0:T(8,128)(2,1)S(1)} %pad_maximum_fusion.1), channel_id=1, source_target_pairs={{0,8},{8,0},{16,24},{24,16},{1,9},{9,1},{17,25},{25,17},{2,10},{10... | collective-permute-start | bytes 786440 | tf_op jit(solution)/shard_map/ppermute | solution.py:152
  22.9 1.5 %joined.1 = (bf16[128,2048]{1,0:T(8,128)(2,1)}, bf16[128,2048]{1,0:T(8,128)(2,1)}, bf16[128,2048]{1,0:T(8,128)(2,1)}) custom-call(bf16[128,1024]{1,0:T(8,128)(2,1)S(1)} %get-tuple-element.40.refs_0_, bf16[128,1024]{1,0:T(8,128)(2,1)S(1)} %get-tuple-element.41.refs_1_, bf16[128,512]{1,0:T(8,128)(2,1)S(1)} %get-tuple-element.85.refs_2_, ...), custom_call_target="tpu_custom_call" | custom-call | tf_op jit(solution)/shard_map/joined/pallas_call | solution.py:163
  24.4 1.2 %collective-permute-done.20 = bf16[512,256]{1,0:T(8,128)(2,1)S(1)} collective-permute-done((bf16[512,256]{1,0:T(8,128)(2,1)S(1)}, bf16[512,256]{1,0:T(8,128)(2,1)S(1)}, u32[]{:S(2)}, u32[]{:S(2)}) %collective-permute-start.20) | collective-permute-done | bytes 262176 | tf_op jit(solution)/shard_map/ppermute | solution.py:152
  25.6 2.6 %collective-permute-start.16 = (bf16[512,256]{1,0:T(8,128)(2,1)S(1)}, bf16[512,256]{1,0:T(8,128)(2,1)S(1)}, u32[]{:S(2)}, u32[]{:S(2)}) collective-permute-start(bf16[512,256]{1,0:T(8,128)(2,1)S(1)} %pad_maximum_fusion.1), channel_id=1, source_target_pairs={{0,16},{8,24},{16,0},{24,8},{1,17},{9,25},{17,1},{25,9},{2,18},{10... | collective-permute-start | bytes 786440 | tf_op jit(solution)/shard_map/ppermute | solution.py:152
  28.2 1.8 %collective-permute-done.13.refs_2_ = bf16[512,512]{1,0:T(8,128)(2,1)S(1)} collective-permute-done((bf16[512,512]{1,0:T(8,128)(2,1)S(1)}, bf16[512,512]{1,0:T(8,128)(2,1)S(1)}, u32[]{:S(2)}, u32[]{:S(2)}) %collective-permute-start.13) | collective-permute-done | bytes 524320 | tf_op jit(solution)/shard_map/ppermute | solution.py:152
  30.1 1.6 %collective-permute-start.22 = (bf16[256,256]{1,0:T(8,128)(2,1)S(1)}, bf16[256,256]{1,0:T(8,128)(2,1)S(1)}, u32[]{:S(2)}, u32[]{:S(2)}) collective-permute-start(bf16[256,256]{1,0:T(8,128)(2,1)S(1)} %get-tuple-element.79.refs_6_), channel_id=1, source_target_pairs={{0,8},{8,0},{16,24},{24,16},{1,9},{9,1},{17,25},{25,17},{2,10},{10... | collective-permute-start | bytes 393224 | tf_op jit(solution)/shard_map/ppermute | solution.py:152
  31.6 1.5 %collective-permute-start.23 = (bf16[256,256]{1,0:T(8,128)(2,1)S(1)}, bf16[256,256]{1,0:T(8,128)(2,1)S(1)}, u32[]{:S(2)}, u32[]{:S(2)}) collective-permute-start(bf16[256,256]{1,0:T(8,128)(2,1)S(1)} %get-tuple-element.80.refs_9_), channel_id=1, source_target_pairs={{0,16},{8,24},{16,0},{24,8},{1,17},{9,25},{17,1},{25,9},{2,18},{10... | collective-permute-start | bytes 393224 | tf_op jit(solution)/shard_map/ppermute | solution.py:152
  33.2 1.9 %collective-permute-start.17 = (bf16[256,256]{1,0:T(8,128)(2,1)S(1)}, bf16[256,256]{1,0:T(8,128)(2,1)S(1)}, u32[]{:S(2)}, u32[]{:S(2)}) collective-permute-start(bf16[256,256]{1,0:T(8,128)(2,1)S(1)} %get-tuple-element.71.refs_6_), channel_id=1, source_target_pairs={{0,8},{8,0},{16,24},{24,16},{1,9},{9,1},{17,25},{25,17},{2,10},{10... | collective-permute-start | bytes 393224 | tf_op jit(solution)/shard_map/ppermute | solution.py:152
  35.1 1.1 %collective-permute-done.22.refs_7_ = bf16[256,256]{1,0:T(8,128)(2,1)S(1)} collective-permute-done((bf16[256,256]{1,0:T(8,128)(2,1)S(1)}, bf16[256,256]{1,0:T(8,128)(2,1)S(1)}, u32[]{:S(2)}, u32[]{:S(2)}) %collective-permute-start.22) | collective-permute-done | bytes 131104 | tf_op jit(solution)/shard_map/ppermute | solution.py:152
  36.3 1.7 %collective-permute-start.18 = (bf16[256,256]{1,0:T(8,128)(2,1)S(1)}, bf16[256,256]{1,0:T(8,128)(2,1)S(1)}, u32[]{:S(2)}, u32[]{:S(2)}) collective-permute-start(bf16[256,256]{1,0:T(8,128)(2,1)S(1)} %get-tuple-element.72.refs_9_), channel_id=1, source_target_pairs={{0,16},{8,24},{16,0},{24,8},{1,17},{9,25},{17,1},{25,9},{2,18},{10... | collective-permute-start | bytes 393224 | tf_op jit(solution)/shard_map/ppermute | solution.py:152
  38.0 0.7 %term_part.3 = (f32[512,128]{1,0:T(8,128)S(1)}, bf16[512,128]{1,0:T(8,128)(2,1)S(1)}) custom-call(bf16[512,512]{1,0:T(8,128)(2,1)S(1)} %turned.1.refs_0_, bf16[512,512]{1,0:T(8,128)(2,1)S(1)} %collective-permute-done.12.refs_1_, bf16[512,512]{1,0:T(8,128)(2,1)S(1)} %collective-permute-done.13.refs_2_, bf16[512,512]{1,0:T(8,128)(2,1)S(1)} %collective-permute-done.14.refs_3_, ...), custom_call_target="tpu_custom_call" | custom-call | tf_op jit(solution)/shard_map/term_part/pallas_call | solution.py:163
  38.7 2.7 %collective-permute-start.24 = (bf16[512,128]{1,0:T(8,128)(2,1)S(1)}, bf16[512,128]{1,0:T(8,128)(2,1)S(1)}, u32[]{:S(2)}, u32[]{:S(2)}) collective-permute-start(bf16[512,128]{1,0:T(8,128)(2,1)S(1)} %get-tuple-element.69), channel_id=1, source_target_pairs={{0,4},{1,5},{2,6},{3,7},{4,0},{5,1},{6,2},{7,3},{8,12},{9,13},{10,... | collective-permute-start | bytes 393224 | tf_op jit(solution)/shard_map/ppermute | solution.py:152
  41.4 0.7 %term_part.2 = (f32[512,128]{1,0:T(8,128)S(1)}, bf16[512,128]{1,0:T(8,128)(2,1)S(1)}) custom-call(bf16[512,512]{1,0:T(8,128)(2,1)S(1)} %turned.1.refs_0_, bf16[512,512]{1,0:T(8,128)(2,1)S(1)} %collective-permute-done.12.refs_1_, bf16[512,512]{1,0:T(8,128)(2,1)S(1)} %collective-permute-done.13.refs_2_, bf16[512,512]{1,0:T(8,128)(2,1)S(1)} %collective-permute-done.14.refs_3_, ...), custom_call_target="tpu_custom_call" | custom-call | tf_op jit(solution)/shard_map/term_part/pallas_call | solution.py:163
  42.1 2.5 %collective-permute-start.19 = (bf16[512,128]{1,0:T(8,128)(2,1)S(1)}, bf16[512,128]{1,0:T(8,128)(2,1)S(1)}, u32[]{:S(2)}, u32[]{:S(2)}) collective-permute-start(bf16[512,128]{1,0:T(8,128)(2,1)S(1)} %get-tuple-element.63), channel_id=1, source_target_pairs={{0,4},{1,5},{2,6},{3,7},{4,0},{5,1},{6,2},{7,3},{8,12},{9,13},{10,... | collective-permute-start | bytes 393224 | tf_op jit(solution)/shard_map/ppermute | solution.py:152
  44.6 5.9 %collective-permute-done.24 = bf16[512,128]{1,0:T(8,128)(2,1)S(1)} collective-permute-done((bf16[512,128]{1,0:T(8,128)(2,1)S(1)}, bf16[512,128]{1,0:T(8,128)(2,1)S(1)}, u32[]{:S(2)}, u32[]{:S(2)}) %collective-permute-start.24) | collective-permute-done | bytes 131104 | tf_op jit(solution)/shard_map/ppermute | solution.py:152
  50.5 2.1 %collective-permute-done.19 = bf16[512,128]{1,0:T(8,128)(2,1)S(1)} collective-permute-done((bf16[512,128]{1,0:T(8,128)(2,1)S(1)}, bf16[512,128]{1,0:T(8,128)(2,1)S(1)}, u32[]{:S(2)}, u32[]{:S(2)}) %collective-permute-start.19) | collective-permute-done | bytes 131104 | tf_op jit(solution)/shard_map/ppermute | solution.py:152
  52.6 0.8 %pad_maximum_fusion = f32[512,256]{1,0:T(8,128)} fusion(f32[512,128]{1,0:T(8,128)S(1)} %convert_add_fusion, f32[512,128]{1,0:T(8,128)S(1)} %convert_add_fusion.1), kind=kLoop, calls=%fused_computation | loop fusion | flops 131072 | bytes 1048576 | tf_op jit(solution)/shard_map/concatenate | solution.py:390
  (40 shorter events, 0.7 us)
Async XLA Ops:
  0.6 5.6 %collective-permute-start = (bf16[128,2048]{1,0:T(8,128)(2,1)}, bf16[128,2048]{1,0:T(8,128)(2,1)S(1)}, u32[]{:S(2)}, u32[]{:S(2)}) collective-permute-start(bf16[128,2048]{1,0:T(8,128)(2,1)} %bitcast.11), channel_id=1, source_target_pairs={{0,1},{1,0},{2,3},{3,2},{4,5},{5,4},{6,7},{7,6},{8,9},{9,8},{10,11... | collective-permute-start | bytes 1572872 | tf_op jit(solution)/shard_map/ppermute | solution.py:152
  1.1 6.6 %collective-permute-start.1 = (bf16[128,2048]{1,0:T(8,128)(2,1)}, bf16[128,2048]{1,0:T(8,128)(2,1)S(1)}, u32[]{:S(2)}, u32[]{:S(2)}) collective-permute-start(bf16[128,2048]{1,0:T(8,128)(2,1)} %bitcast.13), channel_id=1, source_target_pairs={{0,1},{1,0},{2,3},{3,2},{4,5},{5,4},{6,7},{7,6},{8,9},{9,8},{10,11... | collective-permute-start | bytes 1572872 | tf_op jit(solution)/shard_map/ppermute | solution.py:152
  1.2 6.5 %collective-permute-start.3 = (bf16[128,2048]{1,0:T(8,128)(2,1)}, bf16[128,2048]{1,0:T(8,128)(2,1)S(1)}, u32[]{:S(2)}, u32[]{:S(2)}) collective-permute-start(bf16[128,2048]{1,0:T(8,128)(2,1)} %bitcast.15), channel_id=1, source_target_pairs={{0,1},{1,0},{2,3},{3,2},{4,5},{5,4},{6,7},{7,6},{8,9},{9,8},{10,11... | collective-permute-start | bytes 1572872 | tf_op jit(solution)/shard_map/ppermute | solution.py:152
  1.7 9.7 %collective-permute-start.2 = (bf16[128,2048]{1,0:T(8,128)(2,1)}, bf16[128,2048]{1,0:T(8,128)(2,1)S(1)}, u32[]{:S(2)}, u32[]{:S(2)}) collective-permute-start(bf16[128,2048]{1,0:T(8,128)(2,1)} %bitcast.8), channel_id=1, source_target_pairs={{0,1},{1,0},{2,3},{3,2},{4,5},{5,4},{6,7},{7,6},{8,9},{9,8},{10,11... | collective-permute-start | bytes 1572872 | tf_op jit(solution)/shard_map/ppermute | solution.py:152
  3.2 11.6 %collective-permute-start.8 = (bf16[128,512]{1,0:T(8,128)(2,1)S(1)}, bf16[128,512]{1,0:T(8,128)(2,1)S(1)}, u32[]{:S(2)}, u32[]{:S(2)}) collective-permute-start(bf16[128,512]{1,0:T(8,128)(2,1)S(1)} %get-tuple-element.50), channel_id=1, source_target_pairs={{0,8},{8,0},{16,24},{24,16},{1,9},{9,1},{17,25},{25,17},{2,10},{10... | collective-permute-start | bytes 393224 | tf_op jit(solution)/shard_map/ppermute | solution.py:152
  6.2 9.2 %collective-permute-start.9 = (bf16[128,512]{1,0:T(8,128)(2,1)S(1)}, bf16[128,512]{1,0:T(8,128)(2,1)S(1)}, u32[]{:S(2)}, u32[]{:S(2)}) collective-permute-start(bf16[128,512]{1,0:T(8,128)(2,1)S(1)} %get-tuple-element.51), channel_id=1, source_target_pairs={{0,16},{8,24},{16,0},{24,8},{1,17},{9,25},{17,1},{25,9},{2,18},{10... | collective-permute-start | bytes 393224 | tf_op jit(solution)/shard_map/ppermute | solution.py:152
  7.7 7.7 %collective-permute-start.10 = (bf16[128,512]{1,0:T(8,128)(2,1)S(1)}, bf16[128,512]{1,0:T(8,128)(2,1)S(1)}, u32[]{:S(2)}, u32[]{:S(2)}) collective-permute-start(bf16[128,512]{1,0:T(8,128)(2,1)S(1)} %get-tuple-element.52), channel_id=1, source_target_pairs={{0,24},{8,16},{16,8},{24,0},{1,25},{9,17},{17,9},{25,1},{2,26},{10... | collective-permute-start | bytes 393224 | tf_op jit(solution)/shard_map/ppermute | solution.py:152
  9.2 2.2 %copy-start = (bf16[1,128,2048]{2,1,0:T(8,128)(2,1)S(1)}, bf16[1,128,2048]{2,1,0:T(8,128)(2,1)}, u32[]{:S(2)}) copy-start(bf16[1,128,2048]{2,1,0:T(8,128)(2,1)} %param.7) | copy-start | bytes 1572868
  9.2 7.8 %collective-permute-start.11 = (bf16[256,512]{1,0:T(8,128)(2,1)S(1)}, bf16[256,512]{1,0:T(8,128)(2,1)S(1)}, u32[]{:S(2)}, u32[]{:S(2)}) collective-permute-start(bf16[256,512]{1,0:T(8,128)(2,1)S(1)} %get-tuple-element.43), channel_id=1, source_target_pairs={{0,2},{1,3},{2,0},{3,1},{4,6},{5,7},{6,4},{7,5},{8,10},{9,11},{10,... | collective-permute-start | bytes 786440 | tf_op jit(solution)/shard_map/ppermute | solution.py:152
  14.7 7.5 %collective-permute-start.4 = (bf16[128,1024]{1,0:T(8,128)(2,1)S(1)}, bf16[128,1024]{1,0:T(8,128)(2,1)S(1)}, u32[]{:S(2)}, u32[]{:S(2)}) collective-permute-start(bf16[128,1024]{1,0:T(8,128)(2,1)S(1)} %get-tuple-element.44), channel_id=1, source_target_pairs={{0,1},{1,0},{2,3},{3,2},{4,5},{5,4},{6,7},{7,6},{8,9},{9,8},{10,11... | collective-permute-start | bytes 786440 | tf_op jit(solution)/shard_map/ppermute | solution.py:152
  14.8 7.5 %collective-permute-start.5 = (bf16[128,1024]{1,0:T(8,128)(2,1)S(1)}, bf16[128,1024]{1,0:T(8,128)(2,1)S(1)}, u32[]{:S(2)}, u32[]{:S(2)}) collective-permute-start(bf16[128,1024]{1,0:T(8,128)(2,1)S(1)} %get-tuple-element.45), channel_id=1, source_target_pairs={{0,1},{1,0},{2,3},{3,2},{4,5},{5,4},{6,7},{7,6},{8,9},{9,8},{10,11... | collective-permute-start | bytes 786440 | tf_op jit(solution)/shard_map/ppermute | solution.py:152
  15.4 3.7 %collective-permute-start.6 = (bf16[128,512]{1,0:T(8,128)(2,1)S(1)}, bf16[128,512]{1,0:T(8,128)(2,1)S(1)}, u32[]{:S(2)}, u32[]{:S(2)}) collective-permute-start(bf16[128,512]{1,0:T(8,128)(2,1)S(1)} %get-tuple-element.84), channel_id=1, source_target_pairs={{0,1},{1,0},{2,3},{3,2},{4,5},{5,4},{6,7},{7,6},{8,9},{9,8},{10,11... | collective-permute-start | bytes 393224 | tf_op jit(solution)/shard_map/ppermute | solution.py:152
  15.5 5.2 %collective-permute-start.7 = (bf16[128,512]{1,0:T(8,128)(2,1)S(1)}, bf16[128,512]{1,0:T(8,128)(2,1)S(1)}, u32[]{:S(2)}, u32[]{:S(2)}) collective-permute-start(bf16[128,512]{1,0:T(8,128)(2,1)S(1)} %get-tuple-element.82), channel_id=1, source_target_pairs={{0,1},{1,0},{2,3},{3,2},{4,5},{5,4},{6,7},{7,6},{8,9},{9,8},{10,11... | collective-permute-start | bytes 393224 | tf_op jit(solution)/shard_map/ppermute | solution.py:152
  17.3 12.8 %collective-permute-start.13 = (bf16[512,512]{1,0:T(8,128)(2,1)S(1)}, bf16[512,512]{1,0:T(8,128)(2,1)S(1)}, u32[]{:S(2)}, u32[]{:S(2)}) collective-permute-start(bf16[512,512]{1,0:T(8,128)(2,1)S(1)} %turned.1.refs_0_), channel_id=1, source_target_pairs={{0,2},{1,3},{2,0},{3,1},{4,6},{5,7},{6,4},{7,5},{8,10},{9,11},{10,... | collective-permute-start | bytes 1572872 | tf_op jit(solution)/shard_map/ppermute | solution.py:152
  19.1 6.5 %collective-permute-start.20 = (bf16[512,256]{1,0:T(8,128)(2,1)S(1)}, bf16[512,256]{1,0:T(8,128)(2,1)S(1)}, u32[]{:S(2)}, u32[]{:S(2)}) collective-permute-start(bf16[512,256]{1,0:T(8,128)(2,1)S(1)} %pad_maximum_fusion.2), channel_id=1, source_target_pairs={{0,8},{8,0},{16,24},{24,16},{1,9},{9,1},{17,25},{25,17},{2,10},{10... | collective-permute-start | bytes 786440 | tf_op jit(solution)/shard_map/ppermute | solution.py:152
  20.6 7.6 %collective-permute-start.21 = (bf16[512,256]{1,0:T(8,128)(2,1)S(1)}, bf16[512,256]{1,0:T(8,128)(2,1)S(1)}, u32[]{:S(2)}, u32[]{:S(2)}) collective-permute-start(bf16[512,256]{1,0:T(8,128)(2,1)S(1)} %pad_maximum_fusion.2), channel_id=1, source_target_pairs={{0,16},{8,24},{16,0},{24,8},{1,17},{9,25},{17,1},{25,9},{2,18},{10... | collective-permute-start | bytes 786440 | tf_op jit(solution)/shard_map/ppermute | solution.py:152
  22.2 15.8 %collective-permute-start.12 = (bf16[512,512]{1,0:T(8,128)(2,1)S(1)}, bf16[512,512]{1,0:T(8,128)(2,1)S(1)}, u32[]{:S(2)}, u32[]{:S(2)}) collective-permute-start(bf16[512,512]{1,0:T(8,128)(2,1)S(1)} %turned.1.refs_0_), channel_id=1, source_target_pairs={{0,1},{1,0},{2,3},{3,2},{4,5},{5,4},{6,7},{7,6},{8,9},{9,8},{10,11... | collective-permute-start | bytes 1572872 | tf_op jit(solution)/shard_map/ppermute | solution.py:152
  22.3 9.4 %collective-permute-start.15 = (bf16[512,256]{1,0:T(8,128)(2,1)S(1)}, bf16[512,256]{1,0:T(8,128)(2,1)S(1)}, u32[]{:S(2)}, u32[]{:S(2)}) collective-permute-start(bf16[512,256]{1,0:T(8,128)(2,1)S(1)} %pad_maximum_fusion.1), channel_id=1, source_target_pairs={{0,8},{8,0},{16,24},{24,16},{1,9},{9,1},{17,25},{25,17},{2,10},{10... | collective-permute-start | bytes 786440 | tf_op jit(solution)/shard_map/ppermute | solution.py:152
  25.6 7.6 %collective-permute-start.16 = (bf16[512,256]{1,0:T(8,128)(2,1)S(1)}, bf16[512,256]{1,0:T(8,128)(2,1)S(1)}, u32[]{:S(2)}, u32[]{:S(2)}) collective-permute-start(bf16[512,256]{1,0:T(8,128)(2,1)S(1)} %pad_maximum_fusion.1), channel_id=1, source_target_pairs={{0,16},{8,24},{16,0},{24,8},{1,17},{9,25},{17,1},{25,9},{2,18},{10... | collective-permute-start | bytes 786440 | tf_op jit(solution)/shard_map/ppermute | solution.py:152
  30.1 7.9 %collective-permute-start.14 = (bf16[512,512]{1,0:T(8,128)(2,1)S(1)}, bf16[512,512]{1,0:T(8,128)(2,1)S(1)}, u32[]{:S(2)}, u32[]{:S(2)}) collective-permute-start(bf16[512,512]{1,0:T(8,128)(2,1)S(1)} %collective-permute-done.13.refs_2_), channel_id=1, source_target_pairs={{0,1},{1,0},{2,3},{3,2},{4,5},{5,4},{6,7},{7,6},{8,9},{9,8},{10,11... | collective-permute-start | bytes 1572872 | tf_op jit(solution)/shard_map/ppermute | solution.py:152
  30.1 6.2 %collective-permute-start.22 = (bf16[256,256]{1,0:T(8,128)(2,1)S(1)}, bf16[256,256]{1,0:T(8,128)(2,1)S(1)}, u32[]{:S(2)}, u32[]{:S(2)}) collective-permute-start(bf16[256,256]{1,0:T(8,128)(2,1)S(1)} %get-tuple-element.79.refs_6_), channel_id=1, source_target_pairs={{0,8},{8,0},{16,24},{24,16},{1,9},{9,1},{17,25},{25,17},{2,10},{10... | collective-permute-start | bytes 393224 | tf_op jit(solution)/shard_map/ppermute | solution.py:152
  31.6 6.3 %collective-permute-start.23 = (bf16[256,256]{1,0:T(8,128)(2,1)S(1)}, bf16[256,256]{1,0:T(8,128)(2,1)S(1)}, u32[]{:S(2)}, u32[]{:S(2)}) collective-permute-start(bf16[256,256]{1,0:T(8,128)(2,1)S(1)} %get-tuple-element.80.refs_9_), channel_id=1, source_target_pairs={{0,16},{8,24},{16,0},{24,8},{1,17},{9,25},{17,1},{25,9},{2,18},{10... | collective-permute-start | bytes 393224 | tf_op jit(solution)/shard_map/ppermute | solution.py:152
  33.2 8.2 %collective-permute-start.17 = (bf16[256,256]{1,0:T(8,128)(2,1)S(1)}, bf16[256,256]{1,0:T(8,128)(2,1)S(1)}, u32[]{:S(2)}, u32[]{:S(2)}) collective-permute-start(bf16[256,256]{1,0:T(8,128)(2,1)S(1)} %get-tuple-element.71.refs_6_), channel_id=1, source_target_pairs={{0,8},{8,0},{16,24},{24,16},{1,9},{9,1},{17,25},{25,17},{2,10},{10... | collective-permute-start | bytes 393224 | tf_op jit(solution)/shard_map/ppermute | solution.py:152
  36.3 5.1 %collective-permute-start.18 = (bf16[256,256]{1,0:T(8,128)(2,1)S(1)}, bf16[256,256]{1,0:T(8,128)(2,1)S(1)}, u32[]{:S(2)}, u32[]{:S(2)}) collective-permute-start(bf16[256,256]{1,0:T(8,128)(2,1)S(1)} %get-tuple-element.72.refs_9_), channel_id=1, source_target_pairs={{0,16},{8,24},{16,0},{24,8},{1,17},{9,25},{17,1},{25,9},{2,18},{10... | collective-permute-start | bytes 393224 | tf_op jit(solution)/shard_map/ppermute | solution.py:152
  38.7 11.8 %collective-permute-start.24 = (bf16[512,128]{1,0:T(8,128)(2,1)S(1)}, bf16[512,128]{1,0:T(8,128)(2,1)S(1)}, u32[]{:S(2)}, u32[]{:S(2)}) collective-permute-start(bf16[512,128]{1,0:T(8,128)(2,1)S(1)} %get-tuple-element.69), channel_id=1, source_target_pairs={{0,4},{1,5},{2,6},{3,7},{4,0},{5,1},{6,2},{7,3},{8,12},{9,13},{10,... | collective-permute-start | bytes 393224 | tf_op jit(solution)/shard_map/ppermute | solution.py:152
  42.1 10.5 %collective-permute-start.19 = (bf16[512,128]{1,0:T(8,128)(2,1)S(1)}, bf16[512,128]{1,0:T(8,128)(2,1)S(1)}, u32[]{:S(2)}, u32[]{:S(2)}) collective-permute-start(bf16[512,128]{1,0:T(8,128)(2,1)S(1)} %get-tuple-element.63), channel_id=1, source_target_pairs={{0,4},{1,5},{2,6},{3,7},{4,0},{5,1},{6,2},{7,3},{8,12},{9,13},{10,... | collective-permute-start | bytes 393224 | tf_op jit(solution)/shard_map/ppermute | solution.py:152
